TPU v7x, 32 devices: a whole 2x2x4 slice. The times are simulated.
32 devices in a mesh: seq: 4 (over y, x), wshard: 8 (over z, core).
Axes of the slice: x: 2, y: 2, z: 4, core: 2. Of those that a mesh axis runs over, the one named last changes fastest.
Arguments:
- layer_input: bfloat16 [8, 1024, 1536], P('wshard', 'seq'), may hold values from -6 to 6
- lengths: int32 [8], P('wshard'), may hold values from 256 to 1024, as said below
- norm_attn: float32 [1536], replicated, may hold values from 0.1 to 1.9
- w_query: bfloat16 [1536, 1536], P('wshard'), may hold values from -0.15625 to 0.15625
- w_key: bfloat16 [1536, 1536], P('wshard'), may hold values from -0.15625 to 0.15625
- w_value: bfloat16 [1536, 1536], P('wshard'), may hold values from -0.15625 to 0.15625
- w_ogate: bfloat16 [1536, 1536], P('wshard'), may hold values from -0.15625 to 0.15625
- w_forget: bfloat16 [1536, 24], P('wshard'), may hold values from -0.15625 to 0.15625
- forget_bias: float32 [24], replicated, may hold values from 3.5 to 8
- w_out: bfloat16 [1536, 1536], P('wshard'), may hold values from -1 to 1
- norm_ffn: float32 [1536], replicated, may hold values from 0.1 to 1.9
- w_gate: bfloat16 [1536, 4096], P('wshard'), may hold values from -0.15625 to 0.15625
- w_up: bfloat16 [1536, 4096], P('wshard'), may hold values from -0.15625 to 0.15625
- w_down: bfloat16 [4096, 1536], P('wshard'), may hold values from -0.09375 to 0.09375
- output_grad: bfloat16 [8, 1024, 1536], P('wshard', 'seq'), may hold values from -6 to 6
Outputs:
- layer_output: bfloat16 [8, 1024, 1536], P('wshard', 'seq')
- grad_input: float32 [8, 1024, 1536], P('wshard', 'seq')
- grad_norm_attn: float32 [1536], replicated
- grad_w_query: float32 [1536, 1536], P('wshard')
- grad_w_key: float32 [1536, 1536], P('wshard')
- grad_w_value: float32 [1536, 1536], P('wshard')
- grad_w_ogate: float32 [1536, 1536], P('wshard')
- grad_w_forget: float32 [1536, 24], P('wshard')
- grad_forget_bias: float32 [24], replicated
- grad_w_out: float32 [1536, 1536], P('wshard')
- grad_norm_ffn: float32 [1536], replicated
- grad_w_gate: float32 [1536, 4096], P('wshard')
- grad_w_up: float32 [1536, 4096], P('wshard')
- grad_w_down: float32 [4096, 1536], P('wshard')
Inputs may be any that keep to these rules, and one draw needn't show every extreme that they name: Each sequence has 1024 slots of which the first lengths[s] are valid; in every draw one sequence is full and one has exactly 256 valid slots.
All inputs are finite; a program needn't handle non-finite values.
Results may differ from a plain program's by a relative error of at most 0.014.
Values may be sent and summed in bfloat16 or wider, within the bound.
A program may use at most 320 MiB of HBM per device.

v0:
```python
import jax
import jax.numpy as jnp
from jax import lax
from jax.sharding import PartitionSpec as P

EPS = 1e-06
NEG_FILL = -1e30


def product(left, right):
    return jnp.dot(left, right, preferred_element_type=jnp.float32)


def product_tn(left, right):
    return lax.dot_general(
        left, right, (((0,), (0,)), ((), ())), preferred_element_type=jnp.float32
    )


def product_nt(left, right):
    return lax.dot_general(
        left, right, (((1,), (1,)), ((), ())), preferred_element_type=jnp.float32
    )


def rms_norm(values, gain):
    return values * lax.rsqrt(jnp.mean(values * values, axis=-1, keepdims=True) + EPS) * gain


def gate_product(attended, gate_pre):
    return attended * jax.nn.sigmoid(gate_pre)


def swiglu(gate, upward):
    return jax.nn.silu(gate) * upward


def block_scores(query_block, key_block, cum_rows, cum_keys, first_row, length, scale):
    plain = (
        jnp.einsum("qhd,khd->hqk", query_block, key_block, preferred_element_type=jnp.float32)
        * scale
    )
    plain = plain + cum_rows.T[:, :, None] - cum_keys.T[:, None, :]
    rows = first_row + jnp.arange(query_block.shape[0], dtype=jnp.int32)
    columns = jnp.arange(key_block.shape[0], dtype=jnp.int32)
    allowed = (columns[None, :] <= rows[:, None]) & (columns[None, :] < length)
    return jnp.where(allowed[None], plain, NEG_FILL)


def on_device(
    layer_input,
    lengths,
    norm_attn,
    w_query,
    w_key,
    w_value,
    w_ogate,
    w_forget,
    forget_bias,
    w_out,
    norm_ffn,
    w_gate,
    w_up,
    w_down,
    output_grad,
):
    tokens = layer_input.shape[1]
    heads = forget_bias.shape[0]
    groups = lax.axis_size("seq")
    local_heads = heads // groups
    head_size = layer_input.shape[2] // heads
    slots = tokens * groups
    block = min(512, slots)
    scale = head_size ** (-0.5)
    length = lengths[0]
    seq_rank = lax.axis_index("seq")
    positions = seq_rank * tokens + jnp.arange(tokens, dtype=jnp.int32)
    valid_slots = (positions < length).astype(jnp.float32)[:, None]
    inputs = layer_input[0].astype(jnp.float32)
    cotangent = output_grad[0].astype(jnp.float32) * valid_slots
    full_query, full_key, full_value, full_ogate, full_forget, full_out = (
        lax.all_gather(w_query, "wshard", axis=0, tiled=True),
        lax.all_gather(w_key, "wshard", axis=0, tiled=True),
        lax.all_gather(w_value, "wshard", axis=0, tiled=True),
        lax.all_gather(w_ogate, "wshard", axis=0, tiled=True),
        lax.all_gather(w_forget, "wshard", axis=0, tiled=True),
        lax.all_gather(w_out, "wshard", axis=0, tiled=True),
    )
    normed_attn = rms_norm(inputs, norm_attn).astype(jnp.bfloat16)
    queries = product(normed_attn, full_query).astype(jnp.bfloat16)
    keys_proj = product(normed_attn, full_key).astype(jnp.bfloat16)
    values_proj = product(normed_attn, full_value).astype(jnp.bfloat16)
    gate_pre = product(normed_attn, full_ogate)
    forget_pre = product(normed_attn, full_forget).astype(jnp.bfloat16)
    head_query, head_key, head_value, head_forget = (
        lax.all_to_all(queries, "seq", split_axis=1, concat_axis=0, tiled=True),
        lax.all_to_all(keys_proj, "seq", split_axis=1, concat_axis=0, tiled=True),
        lax.all_to_all(values_proj, "seq", split_axis=1, concat_axis=0, tiled=True),
        lax.all_to_all(forget_pre, "seq", split_axis=1, concat_axis=0, tiled=True),
    )
    head_query = head_query.reshape(slots, local_heads, head_size)
    head_key = head_key.reshape(slots, local_heads, head_size)
    head_value = head_value.reshape(slots, local_heads, head_size)
    bias_local = lax.dynamic_slice_in_dim(forget_bias, seq_rank * local_heads, local_heads)
    forget_total = head_forget.astype(jnp.float32) + bias_local
    log_forget, pull_forget = jax.vjp(jax.nn.log_sigmoid, forget_total)
    cumulative = jnp.cumsum(log_forget, axis=0)
    attn_blocks = []
    log_totals = []
    for number in range(slots // block):
        first = number * block
        last = first + block
        masked = block_scores(
            head_query[first:last],
            head_key[:last],
            cumulative[first:last],
            cumulative[:last],
            first,
            length,
            scale,
        )
        log_total = jax.nn.logsumexp(masked, axis=-1, keepdims=True)
        probability = jnp.exp(masked - log_total).astype(jnp.bfloat16)
        attn_blocks.append(
            jnp.einsum(
                "hqk,khd->qhd", probability, head_value[:last], preferred_element_type=jnp.float32
            )
        )
        log_totals.append(log_total)
    head_output = (
        jnp.concatenate(attn_blocks, axis=0)
        .reshape(slots, local_heads * head_size)
        .astype(jnp.bfloat16)
    )
    attended = lax.all_to_all(head_output, "seq", split_axis=0, concat_axis=1, tiled=True).astype(
        jnp.float32
    )
    gated_full, pull_gate = jax.vjp(gate_product, attended, gate_pre)
    gated = gated_full.astype(jnp.bfloat16)
    middle = inputs + product(gated, full_out)
    full_gate, full_up, full_down = (
        lax.all_gather(w_gate, "wshard", axis=0, tiled=True),
        lax.all_gather(w_up, "wshard", axis=0, tiled=True),
        lax.all_gather(w_down, "wshard", axis=0, tiled=True),
    )
    normed_ffn_full, pull_ffn_norm = jax.vjp(rms_norm, middle, norm_ffn)
    normed_ffn = normed_ffn_full.astype(jnp.bfloat16)
    gate_value = product(normed_ffn, full_gate)
    up_value = product(normed_ffn, full_up)
    hidden_full, pull_swiglu = jax.vjp(swiglu, gate_value, up_value)
    hidden = hidden_full.astype(jnp.bfloat16)
    result = middle + product(hidden, full_down)
    layer_output = result.astype(jnp.bfloat16)[None]
    full_gate, full_up, full_down = (
        lax.all_gather(w_gate, "wshard", axis=0, tiled=True),
        lax.all_gather(w_up, "wshard", axis=0, tiled=True),
        lax.all_gather(w_down, "wshard", axis=0, tiled=True),
    )
    cotangent_low = cotangent.astype(jnp.bfloat16)
    grad_w_down = product_tn(hidden, cotangent_low)
    grad_hidden = product_nt(cotangent_low, full_down)
    grad_gate_full, grad_up_full = pull_swiglu(grad_hidden)
    grad_gate = grad_gate_full.astype(jnp.bfloat16)
    grad_up = grad_up_full.astype(jnp.bfloat16)
    grad_w_gate = product_tn(normed_ffn, grad_gate)
    grad_w_up = product_tn(normed_ffn, grad_up)
    share_gate, share_up, share_down = (
        lax.psum_scatter(grad_w_gate, "wshard", scatter_dimension=0, tiled=True),
        lax.psum_scatter(grad_w_up, "wshard", scatter_dimension=0, tiled=True),
        lax.psum_scatter(grad_w_down, "wshard", scatter_dimension=0, tiled=True),
    )
    grad_normed_ffn = product_nt(grad_gate, full_gate) + product_nt(grad_up, full_up)
    grad_middle_part, grad_norm_ffn = pull_ffn_norm(grad_normed_ffn)
    grad_middle = cotangent + grad_middle_part
    full_query, full_key, full_value, full_ogate, full_forget, full_out = (
        lax.all_gather(w_query, "wshard", axis=0, tiled=True),
        lax.all_gather(w_key, "wshard", axis=0, tiled=True),
        lax.all_gather(w_value, "wshard", axis=0, tiled=True),
        lax.all_gather(w_ogate, "wshard", axis=0, tiled=True),
        lax.all_gather(w_forget, "wshard", axis=0, tiled=True),
        lax.all_gather(w_out, "wshard", axis=0, tiled=True),
    )
    grad_branch = grad_middle.astype(jnp.bfloat16)
    grad_w_out = product_tn(gated, grad_branch)
    grad_gated = product_nt(grad_branch, full_out)
    grad_attended_full, grad_gate_pre_full = pull_gate(grad_gated)
    grad_attended = grad_attended_full.astype(jnp.bfloat16)
    grad_gate_pre = grad_gate_pre_full.astype(jnp.bfloat16)
    head_grad = lax.all_to_all(
        grad_attended, "seq", split_axis=1, concat_axis=0, tiled=True
    ).reshape(slots, local_heads, head_size)
    grad_query_blocks = []
    grad_keys = jnp.zeros((slots, local_heads, head_size), jnp.float32)
    grad_values = jnp.zeros((slots, local_heads, head_size), jnp.float32)
    grad_cum = jnp.zeros((slots, local_heads), jnp.float32)
    for number in range(slots // block):
        first = number * block
        last = first + block
        masked = block_scores(
            head_query[first:last],
            head_key[:last],
            cumulative[first:last],
            cumulative[:last],
            first,
            length,
            scale,
        )
        probability = jnp.exp(masked - log_totals[number])
        probability_low = probability.astype(jnp.bfloat16)
        grad_block = head_grad[first:last]
        grad_probability = jnp.einsum(
            "qhd,khd->hqk", grad_block, head_value[:last], preferred_element_type=jnp.float32
        )
        row_dot = jnp.sum(grad_probability * probability, axis=-1, keepdims=True)
        score_terms = probability * (grad_probability - row_dot)
        grad_scores = score_terms.astype(jnp.bfloat16)
        grad_cum = grad_cum.at[first:last].add(jnp.sum(score_terms, axis=2).T)
        grad_cum = grad_cum.at[:last].add(-jnp.sum(score_terms, axis=1).T)
        grad_query_blocks.append(
            jnp.einsum(
                "hqk,khd->qhd", grad_scores, head_key[:last], preferred_element_type=jnp.float32
            )
            * scale
        )
        grad_keys = grad_keys.at[:last].add(
            jnp.einsum(
                "hqk,qhd->khd",
                grad_scores,
                head_query[first:last],
                preferred_element_type=jnp.float32,
            )
            * scale
        )
        grad_values = grad_values.at[:last].add(
            jnp.einsum(
                "hqk,qhd->khd", probability_low, grad_block, preferred_element_type=jnp.float32
            )
        )
    grad_head_query = (
        jnp.concatenate(grad_query_blocks, axis=0)
        .reshape(slots, local_heads * head_size)
        .astype(jnp.bfloat16)
    )
    grad_head_key = grad_keys.reshape(slots, local_heads * head_size).astype(jnp.bfloat16)
    grad_head_value = grad_values.reshape(slots, local_heads * head_size).astype(jnp.bfloat16)
    grad_log_forget = jnp.flip(jnp.cumsum(jnp.flip(grad_cum, 0), axis=0), 0)
    grad_forget_total = pull_forget(grad_log_forget)[0]
    grad_bias_local = jnp.sum(grad_forget_total, axis=0)
    grad_head_forget = grad_forget_total.astype(jnp.bfloat16)
    grad_bias = lax.dynamic_update_slice_in_dim(
        jnp.zeros((heads,), jnp.float32), grad_bias_local, seq_rank * local_heads, 0
    )
    grad_query_tok, grad_key_tok, grad_value_tok, grad_forget_tok = (
        lax.all_to_all(grad_head_query, "seq", split_axis=0, concat_axis=1, tiled=True),
        lax.all_to_all(grad_head_key, "seq", split_axis=0, concat_axis=1, tiled=True),
        lax.all_to_all(grad_head_value, "seq", split_axis=0, concat_axis=1, tiled=True),
        lax.all_to_all(grad_head_forget, "seq", split_axis=0, concat_axis=1, tiled=True),
    )
    grad_w_query = product_tn(normed_attn, grad_query_tok)
    grad_w_key = product_tn(normed_attn, grad_key_tok)
    grad_w_value = product_tn(normed_attn, grad_value_tok)
    grad_w_ogate = product_tn(normed_attn, grad_gate_pre)
    grad_w_forget = product_tn(normed_attn, grad_forget_tok)
    grad_normed_attn = (
        product_nt(grad_query_tok, full_query)
        + product_nt(grad_key_tok, full_key)
        + product_nt(grad_value_tok, full_value)
        + product_nt(grad_gate_pre, full_ogate)
        + product_nt(grad_forget_tok, full_forget)
    )
    unused_normed, pull_attn_norm = jax.vjp(rms_norm, inputs, norm_attn)
    grad_input_part, grad_norm_attn = pull_attn_norm(grad_normed_attn)
    grad_input = (grad_middle + grad_input_part)[None]
    share_query, share_key, share_value, share_ogate, share_forget, share_out = (
        lax.psum_scatter(grad_w_query, "wshard", scatter_dimension=0, tiled=True),
        lax.psum_scatter(grad_w_key, "wshard", scatter_dimension=0, tiled=True),
        lax.psum_scatter(grad_w_value, "wshard", scatter_dimension=0, tiled=True),
        lax.psum_scatter(grad_w_ogate, "wshard", scatter_dimension=0, tiled=True),
        lax.psum_scatter(grad_w_forget, "wshard", scatter_dimension=0, tiled=True),
        lax.psum_scatter(grad_w_out, "wshard", scatter_dimension=0, tiled=True),
    )
    summed = lax.psum(
        (
            share_query,
            share_key,
            share_value,
            share_ogate,
            share_forget,
            share_out,
            share_gate,
            share_up,
            share_down,
        ),
        "seq",
    )
    small = lax.psum((grad_norm_attn, grad_norm_ffn, grad_bias), ("seq", "wshard"))
    return (
        layer_output,
        grad_input,
        small[0],
        summed[0],
        summed[1],
        summed[2],
        summed[3],
        summed[4],
        small[2],
        summed[5],
        small[1],
        summed[6],
        summed[7],
        summed[8],
    )


def solution(mesh):
    return jax.shard_map(
        on_device,
        mesh=mesh,
        in_specs=(
            P("wshard", "seq", None),
            P("wshard"),
            P(),
            P("wshard", None),
            P("wshard", None),
            P("wshard", None),
            P("wshard", None),
            P("wshard", None),
            P(),
            P("wshard", None),
            P(),
            P("wshard", None),
            P("wshard", None),
            P("wshard", None),
            P("wshard", "seq", None),
        ),
        out_specs=(
            P("wshard", "seq", None),
            P("wshard", "seq", None),
            P(),
            P("wshard", None),
            P("wshard", None),
            P("wshard", None),
            P("wshard", None),
            P("wshard", None),
            P(),
            P("wshard", None),
            P(),
            P("wshard", None),
            P("wshard", None),
            P("wshard", None),
        ),
        check_vma=False,
    )
```

profile of v0, /device:TPU:0, one launch (start us, length us, event | category | flops | bytes accessed | tf_op | source)
XLA Modules:
  0.0 2258.0 jit_solution(14034626148076068896)
XLA Ops:
  12.7 15.9 all-gather
  30.0 3.7 all-to-all-start.3
  34.4 30.0 %all-gather.10.cloned.1.call-done = bf16[1536,1536]{1,0:T(8,128)(2,1)} async-done(((bf16[192,1536]{1,0:T(8,128)(2,1)}), bf16[1536,1536]{1,0:T(8,128)(2,1)}) %all-gather.10.cloned.1.call-update) | async-done | bytes 4718608 | tf_op jit(solution)/shard_map/all_gather | solution.py:84
  64.4 3.8 convolution_convert_fusion.2
  69.2 3.6 all-to-all-start
  74.1 42.5 %all-gather.14.cloned.1.call-done = bf16[1536,1536]{1,0:T(8,128)(2,1)} async-done(((bf16[192,1536]{1,0:T(8,128)(2,1)}), bf16[1536,1536]{1,0:T(8,128)(2,1)}) %all-gather.14.cloned.1.call-update) | async-done | bytes 4718608 | tf_op jit(solution)/shard_map/all_gather | solution.py:83
  116.6 3.8 convolution_convert_fusion
  121.3 3.7 all-to-all-start.2
  125.8 43.0 %all-gather.12.cloned.1.call-done = bf16[1536,1536]{1,0:T(8,128)(2,1)} async-done(((bf16[192,1536]{1,0:T(8,128)(2,1)}), bf16[1536,1536]{1,0:T(8,128)(2,1)}) %all-gather.12.cloned.1.call-update) | async-done | bytes 4718608 | tf_op jit(solution)/shard_map/all_gather | solution.py:82
  168.8 3.8 convolution_convert_fusion.1
  173.5 3.8 all-to-all-start.1
  185.5 3.2 all-to-all-done.1
  202.2 4.6 fusion.120
  208.8 2.8 exponential_reduce_fusion
  217.9 3.5 all-to-all-start.4
  221.5 10.5 all-to-all-done.4
  233.7 5.5 multiply_convert_fusion.4
  239.3 33.6 %all-gather.18.cloned.1.call-done = bf16[1536,1536]{1,0:T(8,128)(2,1)} async-done(((bf16[192,1536]{1,0:T(8,128)(2,1)}), bf16[1536,1536]{1,0:T(8,128)(2,1)}) %all-gather.18.cloned.1.call-update) | async-done | bytes 4718608 | tf_op jit(solution)/shard_map/all_gather | solution.py:87
  272.9 3.8 multiply_reduce_fusion.4
  276.9 113.0 %all-gather.20.cloned.1.call-done = bf16[1536,4096]{1,0:T(8,128)(2,1)} async-done(((bf16[192,4096]{1,0:T(8,128)(2,1)}), bf16[1536,4096]{1,0:T(8,128)(2,1)}) %all-gather.20.cloned.1.call-update) | async-done | bytes 12582928 | tf_op jit(solution)/shard_map/all_gather | solution.py:142
  390.0 9.5 fusion.122
  399.4 107.2 %all-gather.22.cloned.1.call-done = bf16[1536,4096]{1,0:T(8,128)(2,1)} async-done(((bf16[192,4096]{1,0:T(8,128)(2,1)}), bf16[1536,4096]{1,0:T(8,128)(2,1)}) %all-gather.22.cloned.1.call-update) | async-done | bytes 12582928 | tf_op jit(solution)/shard_map/all_gather | solution.py:143
  506.6 9.5 fusion.123
  516.1 107.1 %all-gather.24.cloned.1.call-done = bf16[4096,1536]{1,0:T(8,128)(2,1)} async-done(((bf16[512,1536]{1,0:T(8,128)(2,1)}), bf16[4096,1536]{1,0:T(8,128)(2,1)}) %all-gather.24.cloned.1.call-update) | async-done | bytes 12582928 | tf_op jit(solution)/shard_map/all_gather | solution.py:144
  623.2 11.4 multiply_convert_fusion
  634.6 10.6 fusion.124
  645.2 10.6 multiply_reduce_fusion.2
  662.1 5.2 fusion.107
  667.4 6.6 fusion.83
  675.3 15.4 all_to_all.154
  697.3 4.5 multiply_reduce_fusion.1
  701.8 4.6 fusion.115
  708.8 6.3 multiply_reduce_fusion
  715.1 7.9 fusion.114
  730.6 13.1 all_to_all.155
  744.5 5.0 fusion.105
  749.8 3.1 fusion.54
  753.0 4.9 fusion.39
  757.9 2.7 convert_element_type.169
  761.8 12.0 all_to_all.156
  774.7 5.1 fusion.103
  779.9 3.9 convolution_bitcast_fusion
  783.9 6.9 fusion.38
  794.7 10.9 all_to_all.157
  806.5 5.1 fusion.101
  811.7 12.0 fusion.126
  824.1 12.0 fusion.127
  837.2 12.2 fusion.87
  853.7 7.1 all_to_all.158
  862.3 3.0 reduce-scatter.20.cloned.1.call-done
  865.3 100.2 %reduce-scatter.12.cloned.1.call-done = f32[192,1536]{1,0:T(8,128)} async-done(((f32[1536,1536]{1,0:T(8,128)}), f32[192,1536]{1,0:T(8,128)}) %reduce-scatter.12.cloned.1.call-update) | async-done | bytes 1179664 | tf_op jit(solution)/shard_map/reduce_scatter | solution.py:275
  965.5 100.1 %reduce-scatter.14.cloned.1.call-done = f32[192,1536]{1,0:T(8,128)} async-done(((f32[1536,1536]{1,0:T(8,128)}), f32[192,1536]{1,0:T(8,128)}) %reduce-scatter.14.cloned.1.call-update) | async-done | bytes 1179664 | tf_op jit(solution)/shard_map/reduce_scatter | solution.py:276
  1065.5 100.2 %reduce-scatter.16.cloned.1.call-done = f32[192,1536]{1,0:T(8,128)} async-done(((f32[1536,1536]{1,0:T(8,128)}), f32[192,1536]{1,0:T(8,128)}) %reduce-scatter.16.cloned.1.call-update) | async-done | bytes 1179664 | tf_op jit(solution)/shard_map/reduce_scatter | solution.py:277
  1165.7 247.8 %reduce-scatter.22.cloned.1.call-done = f32[192,4096]{1,0:T(8,128)} async-done(((f32[1536,4096]{1,0:T(8,128)}), f32[192,4096]{1,0:T(8,128)}) %reduce-scatter.22.cloned.1.call-update) | async-done | bytes 3145744 | tf_op jit(solution)/shard_map/reduce_scatter | solution.py:168
  1413.5 247.8 %reduce-scatter.24.cloned.1.call-done = f32[192,4096]{1,0:T(8,128)} async-done(((f32[1536,4096]{1,0:T(8,128)}), f32[192,4096]{1,0:T(8,128)}) %reduce-scatter.24.cloned.1.call-update) | async-done | bytes 3145744 | tf_op jit(solution)/shard_map/reduce_scatter | solution.py:169
  1661.3 247.8 %reduce-scatter.26.cloned.1.call-done = f32[512,1536]{1,0:T(8,128)} async-done(((f32[4096,1536]{1,0:T(8,128)}), f32[512,1536]{1,0:T(8,128)}) %reduce-scatter.26.cloned.1.call-update) | async-done | bytes 3145744 | tf_op jit(solution)/shard_map/reduce_scatter | solution.py:170
  1909.1 9.9 fusion.14
  1919.1 22.5 reduce-scatter.28.cloned.1.call-done
  1942.6 17.7 psum.89
  1960.2 4.0 fusion.125
  1964.2 4.4 convolution_add_fusion.3
  1973.4 37.7 %all-reduce.3 = (f32[1536]{0:T(1024)}, f32[24]{0:T(128)}, f32[1536]{0:T(1024)}) all-reduce(f32[1536]{0:T(1024)S(1)} %get-tuple-element.140, f32[24]{0:T(128)S(1)} %negate_dynamic-update-slice_fusion, f32[1536]{0:T(1024)S(1)} %copy-done.60), channel_id=1, replica_groups=mesh['seq'=4,'wshard'=8] {'seq','wshard'}, use_global_device_ids=true, to_apply=%region_19.20 | all-reduce | flops 3096 | bytes 24768 | tf_op jit(solution)/shard_map/psum | solution.py:296
  2011.1 3.0 fusion.36
  2014.1 221.7 %all-reduce.7.cloned.1.call-done = (f32[192,1536]{1,0:T(8,128)}, f32[192,1536]{1,0:T(8,128)}, f32[192,1536]{1,0:T(8,128)}, f32[192,1536]{1,0:T(8,128)}, f32[192,...) async-done(((f32[192,1536]{1,0:T(8,128)}, f32[192,1536]{1,0:T(8,128)}, f32[192,1536]{1,0:T(8,128)}, f32[192,1536]{1,0:T(8,128)}, ...) | async-done | bytes 15335440 | tf_op jit(solution)/shard_map/psum | solution.py:282
  (294 shorter events, 103.7 us)
Async XLA Ops:
  7.2 57.2 %all-gather.10.cloned.1.call-start = ((), (), s32[]{:S(2)}) async-start(), calls=%async_computation.19 | async-start | bytes 5308416 | tf_op jit(solution)/shard_map/all_gather | solution.py:84
  7.9 108.7 %all-gather.14.cloned.1.call-start = ((), (), s32[]{:S(2)}) async-start(), calls=%async_computation.21 | async-start | bytes 5308416 | tf_op jit(solution)/shard_map/all_gather | solution.py:83
  8.7 160.1 %all-gather.12.cloned.1.call-start = ((), (), s32[]{:S(2)}) async-start(), calls=%async_computation.20 | async-start | bytes 5308416 | tf_op jit(solution)/shard_map/all_gather | solution.py:82
  9.4 224.3 %all-gather.16.cloned.1.call-start = ((), (), s32[]{:S(2)}) async-start(), calls=%async_computation.22 | async-start | bytes 5308416 | tf_op jit(solution)/shard_map/all_gather | solution.py:85
  10.0 262.9 %all-gather.18.cloned.1.call-start = ((), (), s32[]{:S(2)}) async-start(), calls=%async_computation.23 | async-start | bytes 5308416 | tf_op jit(solution)/shard_map/all_gather | solution.py:87
  10.6 379.4 %all-gather.20.cloned.1.call-start = ((), (), s32[]{:S(2)}) async-start(), calls=%async_computation.24 | async-start | bytes 14155776 | tf_op jit(solution)/shard_map/all_gather | solution.py:142
  11.1 17.6 copy-start.3
  11.2 17.8 copy-start.39
  11.2 495.4 %all-gather.22.cloned.1.call-start = ((), (), s32[]{:S(2)}) async-start(), calls=%async_computation.25 | async-start | bytes 14155776 | tf_op jit(solution)/shard_map/all_gather | solution.py:143
  11.9 611.3 %all-gather.24.cloned.1.call-start = ((), (), s32[]{:S(2)}) async-start(), calls=%async_computation.26 | async-start | bytes 14155776 | tf_op jit(solution)/shard_map/all_gather | solution.py:144
  28.7 39.4 %copy-start.47 = (bf16[1536,24]{0,1:T(8,128)(2,1)}, bf16[1536,24]{0,1:T(8,128)(2,1)S(1)}, u32[]{:S(2)}) copy-start(bf16[1536,24]{0,1:T(8,128)(2,1)S(1)} %reshape.558) | copy-start | bytes 221188
  29.0 39.2 %copy-start.58 = (f32[256]{0:T(256)}, f32[256]{0:T(256)S(1)}, u32[]{:S(2)}) copy-start(f32[256]{0:T(256)S(1)} %fusion.28) | copy-start | bytes 3076
  30.0 39.1 %all-to-all-start.3 = ((bf16[256,4,6]{0,2,1:T(8,128)(2,1)}), bf16[256,4,6]{0,2,1:T(8,128)(2,1)S(1)}, u32[]{:S(2)}, u32[]{:S(2)}) async-start(bf16[256,4,6]{0,2,1:T(8,128)(2,1)} %all_to_all.125), calls=%async_computation.3 | async-start | bytes 32768 | tf_op jit(solution)/shard_map/all_to_all | solution.py:99
  68.2 5.8 copy-start.63
  69.2 52.2 %all-to-all-start = ((bf16[256,4,384]{2,0,1:T(8,128)(2,1)}), bf16[256,4,384]{2,0,1:T(8,128)(2,1)S(1)}, u32[]{:S(2)}, u32[]{:S(2)}) async-start(bf16[256,4,384]{2,0,1:T(8,128)(2,1)} %bitcast.242), calls=%async_computation | async-start | bytes 1572864 | tf_op jit(solution)/shard_map/all_to_all | solution.py:98
  74.1 103.3 %copy-start.61 = (f32[6]{0:T(128)}, f32[6]{0:T(128)S(1)}, u32[]{:S(2)}) copy-start(f32[6]{0:T(128)S(1)} %dynamic_slice.3) | copy-start | bytes 76
  121.3 52.2 %all-to-all-start.2 = ((bf16[256,4,384]{2,0,1:T(8,128)(2,1)}), bf16[256,4,384]{2,0,1:T(8,128)(2,1)S(1)}, u32[]{:S(2)}, u32[]{:S(2)}) async-start(bf16[256,4,384]{2,0,1:T(8,128)(2,1)} %bitcast.240), calls=%async_computation.2 | async-start | bytes 1572864 | tf_op jit(solution)/shard_map/all_to_all | solution.py:97
  125.8 51.5 %copy-start.45 = (f32[256,4,6]{0,2,1:T(8,128)}, f32[256,4,6]{0,2,1:T(8,128)S(1)}, u32[]{:S(2)}) copy-start(f32[256,4,6]{0,2,1:T(8,128)S(1)} %convert_element_type.181) | copy-start | bytes 73732
  173.5 15.1 all-to-all-start.1
  185.5 28.4 %copy-start.5 = (bf16[1024,6,64]{0,2,1:T(8,128)(2,1)}, bf16[1024,6,64]{0,2,1:T(8,128)(2,1)S(1)}, u32[]{:S(2)}) copy-start(bf16[1024,6,64]{0,2,1:T(8,128)(2,1)S(1)} %reshape.549) | copy-start | bytes 2359300
  190.4 11.8 copy-start.27
  192.4 9.9 copy-start.16
  194.7 17.8 copy-start.9
  198.1 8.8 copy-start.30
  202.2 4.7 copy-start.32
  202.2 4.7 copy-start.49
  202.2 4.7 copy-start.56
  206.9 7.0 copy-start
  208.7 4.0 copy-start.1
  217.9 14.1 all-to-all-start.4
  221.4 640.9 %reduce-scatter.18.cloned.1.call-start = ((), (), s32[]{:S(2)}) async-start(), calls=%async_computation.30 | async-start | bytes 10616832 | tf_op jit(solution)/shard_map/reduce_scatter | solution.py:278
  239.3 37.4 %copy-start.34 = (bf16[256,1536]{1,0:T(8,128)(2,1)}, bf16[256,1536]{1,0:T(8,128)(2,1)S(1)}, u32[]{:S(2)}) copy-start(bf16[256,1536]{1,0:T(8,128)(2,1)S(1)} %get-tuple-element.174) | copy-start | bytes 2359300
  272.9 3.9 copy-start.55
  276.7 368.5 %copy-start.7 = (f32[256,1536]{1,0:T(8,128)}, f32[256,1536]{1,0:T(8,128)S(1)}, u32[]{:S(2)}) copy-start(f32[256,1536]{1,0:T(8,128)S(1)} %get-tuple-element.177) | copy-start | bytes 4718596
  634.6 10.6 copy-start.29
  634.6 23.8 %slice-start.3 = ((s8[4718592]{0:T(1024)(128)(4,1)}), s8[4194304]{0:T(1024)(128)(4,1)S(1)}, s32[]{:S(2)}) async-start(s8[4718592]{0:T(1024)(128)(4,1)} %bitcast.261), calls=%async_computation.40 | async-start | bytes 8388608
  645.2 10.6 copy-start.23
  645.2 13.2 slice-start.4
  667.3 197.9 %reduce-scatter.20.cloned.1.call-start = ((), (), s32[]{:S(2)}) async-start(), calls=%async_computation.31 | async-start | bytes 10616832 | tf_op jit(solution)/shard_map/reduce_scatter | solution.py:280
  674.0 291.5 %reduce-scatter.12.cloned.1.call-start = ((), (), s32[]{:S(2)}) async-start(), calls=%async_computation.27 | async-start | bytes 10616832 | tf_op jit(solution)/shard_map/reduce_scatter | solution.py:275
  697.3 4.5 copy-start.44
  697.3 11.5 slice-start
  697.3 11.5 slice-start.1
  701.8 6.3 copy-start.33
  701.8 7.0 slice-start.2
  715.1 7.9 copy-start.17
  749.6 316.0 %reduce-scatter.14.cloned.1.call-start = ((), (), s32[]{:S(2)}) async-start(), calls=%async_computation.28 | async-start | bytes 10616832 | tf_op jit(solution)/shard_map/reduce_scatter | solution.py:276
  779.8 385.9 %reduce-scatter.16.cloned.1.call-start = ((), (), s32[]{:S(2)}) async-start(), calls=%async_computation.29 | async-start | bytes 10616832 | tf_op jit(solution)/shard_map/reduce_scatter | solution.py:277
  779.9 4.0 copy-start.11
  779.9 4.0 copy-start.42
  811.6 601.9 %reduce-scatter.22.cloned.1.call-start = ((), (), s32[]{:S(2)}) async-start(), calls=%async_computation.32 | async-start | bytes 28311552 | tf_op jit(solution)/shard_map/reduce_scatter | solution.py:168
  823.7 837.6 %reduce-scatter.24.cloned.1.call-start = ((), (), s32[]{:S(2)}) async-start(), calls=%async_computation.33 | async-start | bytes 28311552 | tf_op jit(solution)/shard_map/reduce_scatter | solution.py:169
  836.1 1072.9 %reduce-scatter.26.cloned.1.call-start = ((), (), s32[]{:S(2)}) async-start(), calls=%async_computation.34 | async-start | bytes 28311552 | tf_op jit(solution)/shard_map/reduce_scatter | solution.py:170
  849.4 4.1 copy-start.46
  849.4 4.1 copy-start.62
  849.5 1092.2 %reduce-scatter.28.cloned.1.call-start = ((), (), s32[]{:S(2)}) async-start(), calls=%async_computation.35 | async-start | bytes 884736
  862.2 1373.6 %all-reduce.7.cloned.1.call-start = ((), (), s32[]{:S(2)}) async-start(), calls=%async_computation.36 | async-start | bytes 30670848 | tf_op jit(solution)/shard_map/psum | solution.py:282
  1909.0 51.2 %copy-start.13 = (bf16[4,256,384]{1,2,0:T(8,128)(2,1)S(1)}, bf16[4,256,384]{1,2,0:T(8,128)(2,1)}, u32[]{:S(2)}) copy-start(bf16[4,256,384]{1,2,0:T(8,128)(2,1)} %copy-done.12) | copy-start | bytes 2359300
  1960.2 4.0 copy-start.15
  1960.2 8.4 slice-start.5
  1964.2 4.5 copy-start.19
  1964.2 4.5 slice-start.6
  1964.2 5.9 slice-start.7
  1971.6 39.5 %copy-start.59 = (f32[256]{0:T(256)S(1)}, f32[256]{0:T(256)}, u32[]{:S(2)}) copy-start(f32[256]{0:T(256)} %copy-done.58) | copy-start | bytes 3076
  (32 other events, 58.8 us)
Sparse Core Ops, SparseCore 0:
  9.7 54.6 all-gather.9
  66.0 50.5 all-gather.13
  118.2 50.5 all-gather.11
  170.3 50.5 all-gather.15
  222.3 50.5 all-gather.17
  274.4 115.5 all-gather.19
  391.6 114.9 all-gather.21
  508.2 114.9 all-gather.23
  667.5 97.7 reduce-scatter.17
  767.4 97.8 reduce-scatter.19
  867.6 97.8 reduce-scatter.11
  967.6 97.8 reduce-scatter.13
  1067.8 97.8 reduce-scatter.15
  1168.0 245.5 reduce-scatter.21
  1415.7 245.5 reduce-scatter.23
  1663.5 245.5 reduce-scatter.25
  1911.7 29.8 reduce-scatter.27
  1946.8 288.9 all-reduce.6
where the time goes:
time: 2260 us
  waiting for transfers between devices  1790 us (79%)
  matrix products  205 us (9%)
  blocking collectives  130 us (6%)
  local copies, waits for them, and re-layouts  71.5 us (3%)
  other arithmetic  29.9 us (1%)
    reduce_scatter x1, waiting for transfers between devices, on_device(): lax.psum_scatter(grad_w_gate, 'wshard', scatter_dimension=0, tiled=True)  248 us
    reduce_scatter x1, waiting for transfers between devices, on_device(): lax.psum_scatter(grad_w_down, 'wshard', scatter_dimension=0, tiled=True)  248 us
    reduce_scatter x1, waiting for transfers between devices, on_device(): lax.psum_scatter(grad_w_up, 'wshard', scatter_dimension=0, tiled=True)  248 us
    psum x1, waiting for transfers between devices, on_device(): lax.psum((share_query, share_key, share_value, share_ogate, share_forget,...  222 us
    all_gather x1, waiting for transfers between devices, on_device(): lax.all_gather(w_gate, 'wshard', axis=0, tiled=True)  113 us
    all_gather x1, waiting for transfers between devices, on_device(): lax.all_gather(w_up, 'wshard', axis=0, tiled=True)  107 us
    all_gather x1, waiting for transfers between devices, on_device(): lax.all_gather(w_down, 'wshard', axis=0, tiled=True)  107 us
    reduce_scatter x1, waiting for transfers between devices, on_device(): lax.psum_scatter(grad_w_query, 'wshard', scatter_dimension=0, tiled=True)  100 us
  transfers between devices with their start and end apart: 23, of which 18 were waited for; matrix products, arithmetic and copies ran while one was open for 11% of the time, Pallas kernels for 0%

commit v1 on v0

v1 whole, which is shorter than its diff:
```python
import jax
import jax.numpy as jnp
from jax import lax
from jax.experimental import pallas as pl
from jax.experimental.pallas import tpu as pltpu
from jax.sharding import PartitionSpec as P

EPS = 1e-06
NEG_FILL = -1e30
PAIR = 128


def product(left, right):
    return jnp.dot(left, right, preferred_element_type=jnp.float32)


def product_tn(left, right):
    return lax.dot_general(
        left, right, (((0,), (0,)), ((), ())), preferred_element_type=jnp.float32
    )


def product_nt(left, right):
    return lax.dot_general(
        left, right, (((1,), (1,)), ((), ())), preferred_element_type=jnp.float32
    )


def rms_norm(values, gain):
    return values * lax.rsqrt(jnp.mean(values * values, axis=-1, keepdims=True) + EPS) * gain


def gate_product(attended, gate_pre):
    return attended * jax.nn.sigmoid(gate_pre)


def swiglu(gate, upward):
    return jax.nn.silu(gate) * upward


def attention_fwd(q, k, v, cum_row, key_col, heads_half):
    slots, width = q.shape
    pairs = width // PAIR
    tile = min(256, slots)
    half = heads_half

    def body(q_ref, k_ref, v_ref, row_ref, col_ref, o_ref, lse_ref):
        key_all = k_ref[...]
        value_t = v_ref[...].T
        query_t = q_ref[...].T
        sub = lax.broadcasted_iota(jnp.int32, (PAIR, tile), 0)
        diag = lax.broadcasted_iota(jnp.int32, (tile, tile), 0) <= lax.broadcasted_iota(
            jnp.int32, (tile, tile), 1
        )
        for number in range(slots // tile):
            first, last = number * tile, (number + 1) * tile
            outs = []
            for a in range(2):
                mine = (sub >= a * half) & (sub < (a + 1) * half)
                query = jnp.where(mine, query_t[:, first:last], jnp.zeros((), query_t.dtype))
                scores = product(key_all[:last], query)
                scores = scores + (row_ref[0, a : a + 1, first:last] - col_ref[0, :last, a : a + 1])
                tail = jnp.where(diag, scores[first:], NEG_FILL)
                scores = tail if number == 0 else jnp.concatenate([scores[:first], tail], axis=0)
                top = jnp.max(scores, axis=0, keepdims=True)
                weights = jnp.exp(scores - top)
                total = jnp.sum(weights, axis=0, keepdims=True)
                mixed = product(value_t[a * half : (a + 1) * half, :last], weights.astype(jnp.bfloat16))
                outs.append(mixed / total)
                lse_ref[0, a : a + 1, first:last] = top + jnp.log(total)
            o_ref[first:last, :] = jnp.concatenate(outs, axis=0).T.astype(o_ref.dtype)

    lane = pl.BlockSpec((slots, PAIR), lambda p: (0, p))
    row = pl.BlockSpec((1, 2, slots), lambda p: (p, 0, 0))
    col = pl.BlockSpec((1, slots, 2), lambda p: (p, 0, 0))
    return pl.pallas_call(
        body,
        grid=(pairs,),
        in_specs=[lane, lane, lane, row, col],
        out_specs=[lane, row],
        out_shape=[
            jax.ShapeDtypeStruct((slots, width), jnp.bfloat16),
            jax.ShapeDtypeStruct((pairs, 2, slots), jnp.float32),
        ],
        compiler_params=pltpu.CompilerParams(vmem_limit_bytes=56 << 20),
        cost_estimate=pl.CostEstimate(
            flops=4 * slots * slots * width, bytes_accessed=8 * slots * width, transcendentals=0
        ),
        name="attention_fwd",
    )(q, k, v, cum_row, key_col)


def attention_bwd(q, k, v, d_out, cum_row, key_col, lse, heads_half, scale):
    slots, width = q.shape
    pairs = width // PAIR
    tile = min(256, slots)
    half = heads_half

    def body(q_ref, k_ref, v_ref, do_ref, row_ref, col_ref, lse_ref,
             dq_ref, dk_ref, dv_ref, drow_ref, dcol_ref, dk_acc, dv_acc, dcol_acc):
        key_all = k_ref[...]
        value_all = v_ref[...]
        query_t = q_ref[...].T
        key_t = k_ref[...].T
        dout_t = do_ref[...].T
        sub = lax.broadcasted_iota(jnp.int32, (PAIR, tile), 0)
        lanes = lax.broadcasted_iota(jnp.int32, (tile, PAIR), 1)
        diag = lax.broadcasted_iota(jnp.int32, (tile, tile), 0) <= lax.broadcasted_iota(
            jnp.int32, (tile, tile), 1
        )
        zero = jnp.zeros((), jnp.bfloat16)
        dk_acc[...] = jnp.zeros_like(dk_acc)
        dv_acc[...] = jnp.zeros_like(dv_acc)
        dcol_acc[...] = jnp.zeros_like(dcol_acc)
        for number in range(slots // tile):
            first, last = number * tile, (number + 1) * tile
            outs = []
            for a in range(2):
                mine = (sub >= a * half) & (sub < (a + 1) * half)
                own = (lanes >= a * half) & (lanes < (a + 1) * half)
                scores = product(key_all[:last], jnp.where(mine, query_t[:, first:last], zero))
                offset = row_ref[0, a : a + 1, first:last] - lse_ref[0, a : a + 1, first:last]
                scores = scores + (offset - col_ref[0, :last, a : a + 1])
                tail = jnp.where(diag, scores[first:], NEG_FILL)
                scores = tail if number == 0 else jnp.concatenate([scores[:first], tail], axis=0)
                probs = jnp.exp(scores)
                d_probs = product(value_all[:last], jnp.where(mine, dout_t[:, first:last], zero))
                dot = jnp.sum(d_probs * probs, axis=0, keepdims=True)
                d_full = probs * (d_probs - dot)
                d_scores = d_full.astype(jnp.bfloat16)
                drow_ref[0, a : a + 1, first:last] = jnp.sum(d_full, axis=0, keepdims=True)
                dcol_acc[:last, a : a + 1] += jnp.sum(d_full, axis=1, keepdims=True)
                outs.append(product(key_t[a * half : (a + 1) * half, :last], d_scores) * scale)
                dk_acc[:last, :] += product(d_scores, jnp.where(own, q_ref[first:last, :], zero))
                dv_acc[:last, :] += product(
                    probs.astype(jnp.bfloat16), jnp.where(own, do_ref[first:last, :], zero)
                )
            dq_ref[first:last, :] = jnp.concatenate(outs, axis=0).T.astype(dq_ref.dtype)
        dk_ref[...] = dk_acc[...].astype(dk_ref.dtype)
        dv_ref[...] = dv_acc[...].astype(dv_ref.dtype)
        dcol_ref[0] = dcol_acc[...]

    lane = pl.BlockSpec((slots, PAIR), lambda p: (0, p))
    row = pl.BlockSpec((1, 2, slots), lambda p: (p, 0, 0))
    col = pl.BlockSpec((1, slots, 2), lambda p: (p, 0, 0))
    return pl.pallas_call(
        body,
        grid=(pairs,),
        in_specs=[lane, lane, lane, lane, row, col, row],
        out_specs=[lane, lane, lane, row, col],
        out_shape=[jax.ShapeDtypeStruct((slots, width), jnp.bfloat16)] * 3
        + [
            jax.ShapeDtypeStruct((pairs, 2, slots), jnp.float32),
            jax.ShapeDtypeStruct((pairs, slots, 2), jnp.float32),
        ],
        scratch_shapes=[
            pltpu.VMEM((slots, PAIR), jnp.float32),
            pltpu.VMEM((slots, PAIR), jnp.float32),
            pltpu.VMEM((slots, 2), jnp.float32),
        ],
        compiler_params=pltpu.CompilerParams(vmem_limit_bytes=56 << 20),
        cost_estimate=pl.CostEstimate(
            flops=10 * slots * slots * width, bytes_accessed=14 * slots * width, transcendentals=0
        ),
        name="attention_bwd",
    )(q, k, v, d_out, cum_row, key_col, lse)


def gather(value, axis_name):
    return lax.all_gather(value, axis_name, axis=0, tiled=True)


def scatter(value, axis_name):
    return lax.psum_scatter(value, axis_name, scatter_dimension=0, tiled=True)


def on_device(
    layer_input,
    lengths,
    norm_attn,
    w_query,
    w_key,
    w_value,
    w_ogate,
    w_forget,
    forget_bias,
    w_out,
    norm_ffn,
    w_gate,
    w_up,
    w_down,
    output_grad,
):
    low = jnp.bfloat16
    tokens, width = layer_input.shape[1:]
    heads = forget_bias.shape[0]
    groups = lax.axis_size("seq")
    shards = lax.axis_size("wshard")
    local_heads = heads // groups
    head_size = width // heads
    columns = width // groups
    slots = tokens * groups
    hidden_size = w_gate.shape[1]
    part = hidden_size // (groups * shards)
    scale = head_size ** (-0.5)
    length = lengths[0]
    seq_rank = lax.axis_index("seq")
    shard_rank = lax.axis_index("wshard")
    per_block = shards // groups
    positions = seq_rank * tokens + jnp.arange(tokens, dtype=jnp.int32)
    valid_slots = (positions < length)[:, None]
    inputs = layer_input[0].astype(jnp.float32)
    cotangent_low = jnp.where(valid_slots, output_grad[0], jnp.zeros((), low))
    cotangent = cotangent_low.astype(jnp.float32)
    pad_heads = PAIR

    def own_columns(weight):
        return lax.dynamic_slice_in_dim(weight, seq_rank * columns, columns, 1)

    def own_units(weight):
        split = weight.reshape(weight.shape[0], shards, groups, part)
        mine = lax.dynamic_index_in_dim(split, seq_rank, 2, keepdims=False)
        return mine.reshape(weight.shape[0], shards * part)

    own_forget = lax.dynamic_slice_in_dim(w_forget, seq_rank * local_heads, local_heads, 1)
    own_forget = jnp.pad(own_forget, ((0, 0), (0, pad_heads - local_heads)))
    mine_attn = jnp.concatenate(
        [own_columns(w_query), own_columns(w_key), own_columns(w_value), own_columns(w_ogate), own_forget],
        axis=1,
    )
    mine_ffn = jnp.concatenate([own_units(w_gate), own_units(w_up)], axis=1)
    mine_down = lax.dynamic_slice_in_dim(w_down, seq_rank * part, part, 0)
    full_attn = gather(mine_attn, "wshard")
    full_out = lax.dynamic_slice_in_dim(gather(w_out, "wshard"), seq_rank * columns, columns, 0)
    full_ffn = gather(mine_ffn, "wshard")
    full_down = gather(mine_down, "wshard")

    normed_attn = gather(rms_norm(inputs, norm_attn).astype(low), "seq")
    projected = product(normed_attn, full_attn)
    queries = projected[:, :columns].astype(low)
    keys = projected[:, columns : 2 * columns].astype(low)
    values = projected[:, 2 * columns : 3 * columns].astype(low)
    gate_pre = projected[:, 3 * columns : 4 * columns]
    forget_pre = projected[:, 4 * columns : 4 * columns + local_heads].astype(low)
    bias_local = lax.dynamic_slice_in_dim(forget_bias, seq_rank * local_heads, local_heads)
    forget_total = forget_pre.astype(jnp.float32) + bias_local
    log_forget, pull_forget = jax.vjp(jax.nn.log_sigmoid, forget_total)
    cumulative = jnp.cumsum(log_forget, axis=0)
    even = -local_heads % 2

    def pad_lanes(value):
        return jnp.pad(value, ((0, 0), (0, even * head_size))) if even else value

    pairs = (local_heads + even) // 2
    cum = jnp.pad(cumulative, ((0, 0), (0, even))) if even else cumulative
    usable = (jnp.arange(slots, dtype=jnp.int32) < length)[:, None]
    cum_row = cum.T.reshape(pairs, 2, slots)
    key_col = jnp.where(usable, cum, -NEG_FILL).reshape(slots, pairs, 2).transpose(1, 0, 2)
    q_in = pad_lanes((queries.astype(jnp.float32) * scale).astype(low))
    k_in = pad_lanes(keys)
    v_in = pad_lanes(values)
    attended_low, log_total = attention_fwd(q_in, k_in, v_in, cum_row, key_col, head_size)
    attended = attended_low[:, :columns].astype(jnp.float32)
    gated_full, pull_gate = jax.vjp(gate_product, attended, gate_pre)
    gated = gated_full.astype(low)
    branch = scatter(product(gated, full_out).astype(low), "seq")
    middle = inputs + branch.astype(jnp.float32)
    normed_ffn_own, pull_ffn_norm = jax.vjp(rms_norm, middle, norm_ffn)
    normed_ffn = gather(normed_ffn_own.astype(low), "seq")
    gate_up = product(normed_ffn, full_ffn)
    units = shards * part
    hidden_full, pull_swiglu = jax.vjp(swiglu, gate_up[:, :units], gate_up[:, units:])
    hidden = hidden_full.astype(low)
    lowered = scatter(product(hidden, full_down).astype(low), "seq")
    layer_output = (middle + lowered.astype(jnp.float32)).astype(low)[None]

    cotangent_all = gather(cotangent_low, "seq")
    grad_w_down = product_tn(hidden, cotangent_all).astype(low)
    grad_hidden = product_nt(cotangent_all, full_down)
    grad_gate_full, grad_up_full = pull_swiglu(grad_hidden)
    grad_gate_up = jnp.concatenate([grad_gate_full.astype(low), grad_up_full.astype(low)], axis=1)
    grad_w_ffn = product_tn(normed_ffn, grad_gate_up).astype(low)
    grad_normed_ffn = scatter(product_nt(grad_gate_up, full_ffn).astype(low), "seq")
    share_down = scatter(grad_w_down, "wshard")
    share_ffn = scatter(grad_w_ffn, "wshard")
    grad_middle_part, grad_norm_ffn = pull_ffn_norm(grad_normed_ffn.astype(jnp.float32))
    grad_middle = cotangent + grad_middle_part
    grad_branch = gather(grad_middle.astype(low), "seq")
    grad_w_out = product_tn(gated, grad_branch).astype(low)
    grad_gated = product_nt(grad_branch, full_out)
    grad_attended_full, grad_gate_pre_full = pull_gate(grad_gated)
    grad_attended = pad_lanes(grad_attended_full.astype(low))
    grad_gate_pre = grad_gate_pre_full.astype(low)
    dq, dk, dv, drow, dcol = attention_bwd(
        q_in, k_in, v_in, grad_attended, cum_row, key_col, log_total, head_size, scale
    )
    grad_cum = drow.reshape(2 * pairs, slots).T - dcol.transpose(1, 0, 2).reshape(slots, 2 * pairs)
    grad_cum = grad_cum[:, :local_heads]
    grad_log_forget = jnp.flip(jnp.cumsum(jnp.flip(grad_cum, 0), axis=0), 0)
    grad_forget_total = pull_forget(grad_log_forget)[0]
    grad_bias_local = jnp.sum(grad_forget_total, axis=0)
    grad_forget = jnp.pad(grad_forget_total.astype(low), ((0, 0), (0, pad_heads - local_heads)))
    grad_bias = lax.dynamic_update_slice_in_dim(
        jnp.zeros((heads,), jnp.float32), grad_bias_local, seq_rank * local_heads, 0
    )
    grad_projected = jnp.concatenate(
        [dq[:, :columns], dk[:, :columns], dv[:, :columns], grad_gate_pre, grad_forget], axis=1
    )
    grad_w_attn = product_tn(normed_attn, grad_projected).astype(low)
    share_attn = scatter(grad_w_attn, "wshard")
    grad_normed_attn = scatter(product_nt(grad_projected, full_attn).astype(low), "seq")
    unused_normed, pull_attn_norm = jax.vjp(rms_norm, inputs, norm_attn)
    grad_input_part, grad_norm_attn = pull_attn_norm(grad_normed_attn.astype(jnp.float32))
    grad_input = (grad_middle + grad_input_part)[None]

    share_out = scatter(grad_w_out, "wshard")
    rows_out = columns // shards
    pieces_out = lax.all_gather(share_out, "seq", axis=0, tiled=False)
    lane_of = shard_rank // (shards // per_block)
    slots_out = jnp.where(
        (jnp.arange(per_block) == lane_of)[None, :, None, None], pieces_out[:, None], jnp.zeros((), low)
    ).reshape(shards, rows_out, width)
    moved = lax.all_to_all(slots_out, "wshard", split_axis=0, concat_axis=0, tiled=True)
    moved = moved.reshape(per_block, shards // per_block, rows_out, width)
    mine_out = lax.dynamic_index_in_dim(moved, shard_rank % per_block, 0, keepdims=False)
    grad_out = mine_out.reshape(columns // per_block, width).astype(jnp.float32)

    every_attn = lax.all_gather(share_attn, "seq", axis=0, tiled=False)
    every_ffn = lax.all_gather(share_ffn, "seq", axis=0, tiled=False)
    grad_down = gather(share_down, "seq").astype(jnp.float32)
    rows = share_attn.shape[0]

    def join(first):
        taken = every_attn[:, :, first * columns : (first + 1) * columns]
        return taken.transpose(1, 0, 2).reshape(rows, width).astype(jnp.float32)

    def join_units(first):
        taken = every_ffn[:, :, first * units : (first + 1) * units]
        taken = taken.reshape(groups, rows, shards, part).transpose(1, 2, 0, 3)
        return taken.reshape(rows, hidden_size).astype(jnp.float32)

    grad_forget_w = every_attn[:, :, 4 * columns : 4 * columns + local_heads]
    grad_forget_w = grad_forget_w.transpose(1, 0, 2).reshape(rows, heads).astype(jnp.float32)
    small = lax.psum((grad_norm_attn, grad_norm_ffn, grad_bias), ("seq", "wshard"))
    return (
        layer_output,
        grad_input,
        small[0],
        join(0),
        join(1),
        join(2),
        join(3),
        grad_forget_w,
        small[2],
        grad_out,
        small[1],
        join_units(0),
        join_units(1),
        grad_down,
    )


def solution(mesh):
    return jax.shard_map(
        on_device,
        mesh=mesh,
        in_specs=(
            P("wshard", "seq", None),
            P("wshard"),
            P(),
            P("wshard", None),
            P("wshard", None),
            P("wshard", None),
            P("wshard", None),
            P("wshard", None),
            P(),
            P("wshard", None),
            P(),
            P("wshard", None),
            P("wshard", None),
            P("wshard", None),
            P("wshard", "seq", None),
        ),
        out_specs=(
            P("wshard", "seq", None),
            P("wshard", "seq", None),
            P(),
            P("wshard", None),
            P("wshard", None),
            P("wshard", None),
            P("wshard", None),
            P("wshard", None),
            P(),
            P("wshard", None),
            P(),
            P("wshard", None),
            P("wshard", None),
            P("wshard", None),
        ),
        check_vma=False,
    )
```

time: 2260 us -> 997 us (0.44)
  waiting for transfers between devices: 1790 us -> 664 us
  matrix products: 205 us -> 107 us
  blocking collectives: 130 us -> 50.5 us
  Pallas kernels: 0 us -> 33.1 us
    reduce_scatter x8, waiting for transfers between devices: 1050 us -> 230 us  [scatter(): return lax.psum_scatter(value, axis_name, scatter_dimension=0, tiled=True)]
    psum x1 -> x0, waiting for transfers between devices: 222 us -> none  [on_device(): lax.psum((share_query, share_key, share_value, share_ogate, share_forget,...]
    all_to_all x5 -> x0, blocking collectives: 58.4 us -> none  [the longest x1 15.4 us: on_device(): lax.all_to_all(grad_attended, 'seq', split_axis=1, concat_axis=0, tiled=T...]
    all_gather x8 -> x11, waiting for transfers between devices: 476 us -> 433 us  [the longest x9 356 us: gather(): return lax.all_gather(value, axis_name, axis=0, tiled=True)]
    dot_general x12 -> x0, matrix products: 42.2 us -> none  [the longest x2 10.9 us: on_device(): jnp.einsum('hqk,qhd->khd', probability_low, grad_block, preferred_element...]
    pallas_call x0 -> x2, Pallas kernels: none -> 33.1 us  [the longest x1 19.5 us: attention_bwd(): pl.pallas_call(body, grid=(pairs,), in_specs=[lane, lane, lane, lane, row...]
    dot_general x8 -> x4, matrix products: 63.2 us -> 34.2 us  [product_tn(): lax.dot_general(left, right, (((0,), (0,)), ((), ())), preferred_element_...]
    unnamed x19, waiting for transfers between devices: 27.7 us -> 1.47 us
  transfers between devices with their start and end apart: 23 -> 20, of which waited for: 18 -> 18; matrix products, arithmetic and copies ran while one was open for 11% -> 17% of each run, Pallas kernels for 0% -> 3%
where the time goes in v1:
time: 997 us; the launch traced here: 989 us
  waiting for transfers between devices  664 us (67%)
  matrix products  107 us (11%)
  local copies, waits for them, and re-layouts  69.9 us (7%)
  blocking collectives  50.5 us (5%)
  other arithmetic  42.5 us (4%)
  Pallas kernels  33.1 us (3%)
  between operations  15.5 us (2%)
    all_gather x9, waiting for transfers between devices, gather(): return lax.all_gather(value, axis_name, axis=0, tiled=True)  356 us
    reduce_scatter x8, waiting for transfers between devices, scatter(): return lax.psum_scatter(value, axis_name, scatter_dimension=0, tiled=True)  230 us
    psum x1, blocking collectives, on_device(): lax.psum((grad_norm_attn, grad_norm_ffn, grad_bias), ('seq', 'wshard'))  40 us
    all_gather x1, waiting for transfers between devices, on_device(): every_ffn = lax.all_gather(share_ffn, 'seq', axis=0, tiled=False)  39.7 us
    dot_general x4, matrix products, product_nt(): lax.dot_general(left, right, (((1,), (1,)), ((), ())), preferred_element_...  37.3 us
    all_gather x1, waiting for transfers between devices, on_device(): every_attn = lax.all_gather(share_attn, 'seq', axis=0, tiled=False)  37.1 us
    dot_general x4, matrix products, product(): return jnp.dot(left, right, preferred_element_type=jnp.float32)  35.5 us
    dot_general x4, matrix products, product_tn(): lax.dot_general(left, right, (((0,), (0,)), ((), ())), preferred_element_...  34.2 us
  transfers between devices with their start and end apart: 20, of which 18 were waited for; matrix products, arithmetic and copies ran while one was open for 17% of the time, Pallas kernels for 3%

profile of v1, /device:TPU:0, one launch (start us, length us, event | category | flops | bytes accessed | tf_op | source)
XLA Modules:
  0.0 989.1 jit_solution(12996496477161388946)
XLA Ops:
  8.7 2.3 fusion.8
  18.1 39.7 %all-gather.15.cloned.1.call-done = bf16[1024,1536]{1,0:T(8,128)(2,1)} async-done(((bf16[256,1536]{1,0:T(8,128)(2,1)}), bf16[1024,1536]{1,0:T(8,128)(2,1)}) %all-gather.15.cloned.1.call-update) | async-done | bytes 3145744 | tf_op jit(solution)/shard_map/all_gather | solution.py:170
  57.9 57.2 %all-gather.17.cloned.1.call-done = bf16[1536,1664]{1,0:T(8,128)(2,1)} async-done(((bf16[192,1664]{1,0:T(8,128)(2,1)}), bf16[1536,1664]{1,0:T(8,128)(2,1)}) %all-gather.17.cloned.1.call-update) | async-done | bytes 5111824 | tf_op jit(solution)/shard_map/all_gather | solution.py:170
  115.1 10.7 %fusion.47 = (bf16[1024,1664]{1,0:T(8,128)(2,1)S(1)}, f32[1024,1664]{1,0:T(8,128)}) fusion(bf16[1024,1536]{1,0:T(8,128)(2,1)} %all-gather.15.cloned.1.call-done, bf16[1536,1664]{1,0:T(8,128)(2,1)} %all-gather.17.cloned.1.call-done), kind=kOutput, calls=%fused_computation.125 | convolution fusion | flops 5236195328 | bytes 18481152 | tf_op jit(solution)/shard_map/dot_general | solution.py:14
  125.8 1.7 copy-done.6
  128.1 1.7 reduce-window.14
  130.2 1.7 copy.63
  132.6 2.2 multiply_convert_fusion.4.q_ref
  134.7 2.7 fusion.46
  137.4 13.6 %attention_fwd.1 = (bf16[1024,384]{1,0:T(8,128)(2,1)}, f32[3,2,1024]{2,1,0:T(2,128)}) custom-call(bf16[1024,384]{1,0:T(8,128)(2,1)} %multiply_convert_fusion.4.q_ref, bf16[1024,384]{1,0:T(8,128)(2,1)} %get-tuple-element.41.k_ref, bf16[1024,384]{1,0:T(8,128)(2,1)} %get-tuple-element.40.v_ref, f32[3,2,1024]{2,1,0:T(2,128)} %reduce_window_sum.30.row_ref, ...), custom_call_target="tpu_custom_call" | custom-call | flops 1610612736 | bytes 3145728 | tf_op jit(solution)/shard_map/attention_fwd/pallas_call | solution.py:76
  151.0 16.3 %all-gather.19.cloned.1.call-done = bf16[1536,1536]{1,0:T(8,128)(2,1)} async-done(((bf16[192,1536]{1,0:T(8,128)(2,1)}), bf16[1536,1536]{1,0:T(8,128)(2,1)}) %all-gather.19.cloned.1.call-update) | async-done | bytes 4718608 | tf_op jit(solution)/shard_map/all_gather | solution.py:170
  167.2 5.5 convolution_convert_fusion.4
  173.0 2.8 reshape.172
  175.8 3.9 reshape.174
  179.8 6.1 dynamic-slice_reduce_fusion
  187.1 28.6 %reduce-scatter.9.cloned.1.call-done = bf16[256,1536]{1,0:T(8,128)(2,1)} async-done(((bf16[1024,1536]{1,0:T(8,128)(2,1)}), bf16[256,1536]{1,0:T(8,128)(2,1)}) %reduce-scatter.9.cloned.1.call-update) | async-done | bytes 786448 | tf_op jit(solution)/shard_map/reduce_scatter | solution.py:174
  218.5 2.1 bitcast_select_fusion.1
  221.8 60.6 %all-gather.23.cloned.1.call-done = bf16[1536,2048]{1,0:T(8,128)(2,1)} async-done(((bf16[192,2048]{1,0:T(8,128)(2,1)}), bf16[1536,2048]{1,0:T(8,128)(2,1)}) %all-gather.23.cloned.1.call-update) | async-done | bytes 6291472 | tf_op jit(solution)/shard_map/all_gather | solution.py:170
  282.5 44.9 %all-gather.21.cloned.1.call-done = bf16[1024,1536]{1,0:T(8,128)(2,1)} async-done(((bf16[256,1536]{1,0:T(8,128)(2,1)}), bf16[1024,1536]{1,0:T(8,128)(2,1)}) %all-gather.21.cloned.1.call-update) | async-done | bytes 3145744 | tf_op jit(solution)/shard_map/all_gather | solution.py:170
  327.4 11.7 %fusion.48 = f32[1024,2048]{1,0:T(8,128)} fusion(bf16[1024,1536]{1,0:T(8,128)(2,1)} %all-gather.21.cloned.1.call-done, bf16[1536,2048]{1,0:T(8,128)(2,1)} %all-gather.23.cloned.1.call-done), kind=kOutput, calls=%fused_computation.126 | convolution fusion | flops 6442450944 | bytes 17825792 | tf_op jit(solution)/shard_map/dot_general | solution.py:14
  339.1 34.8 %all-gather.27.cloned.1.call-done = bf16[1024,1536]{1,0:T(8,128)(2,1)} async-done(((bf16[256,1536]{1,0:T(8,128)(2,1)}), bf16[1024,1536]{1,0:T(8,128)(2,1)}) %all-gather.27.cloned.1.call-update) | async-done | bytes 3145744 | tf_op jit(solution)/shard_map/all_gather | solution.py:170
  373.8 40.5 %all-gather.25.cloned.1.call-done = bf16[1024,1536]{1,0:T(8,128)(2,1)} async-done(((bf16[128,1536]{1,0:T(8,128)(2,1)}), bf16[1024,1536]{1,0:T(8,128)(2,1)}) %all-gather.25.cloned.1.call-update) | async-done | bytes 3145744 | tf_op jit(solution)/shard_map/all_gather | solution.py:170
  414.4 11.4 %fusion.2 = (bf16[1024,1024]{1,0:T(8,128)(2,1)S(1)}, bf16[1024,1024]{1,0:T(8,128)(2,1)S(1)}, bf16[1024,1024]{1,0:T(8,128)(2,1)}) fusion(f32[1024,2048]{1,0:T(8,128)} %fusion.48, bf16[1024,1536]{1,0:T(8,128)(2,1)} %all-gather.27.cloned.1.call-done, bf16[1024,1536]{1,0:T(8,128)(2,1)} %all-gather.25.cloned.1.call-done), kind=kOutput, calls=%fused_computation.5 | convolution fusion | flops 3238002688 | bytes 20971520 | tf_op jit(solution)/shard_map/dot_general | solution.py:24
  427.8 9.9 %convolution_convert_fusion.2 = bf16[1024,1536]{1,0:T(8,128)(2,1)} fusion(bf16[1536,2048]{1,0:T(8,128)(2,1)} %all-gather.23.cloned.1.call-done, bf16[1024,1024]{1,0:T(8,128)(2,1)S(1)} %get-tuple-element.38, bf16[1024,1024]{1,0:T(8,128)(2,1)S(1)} %get-tuple-element.37), kind=kOutput, calls=%fused_computation.11 | convolution fusion | flops 6452412416 | bytes 13631488 | tf_op jit(solution)/shard_map/dot_general | solution.py:24
  437.8 42.9 %reduce-scatter.13.cloned.1.call-done = bf16[256,1536]{1,0:T(8,128)(2,1)} async-done(((bf16[1024,1536]{1,0:T(8,128)(2,1)}), bf16[256,1536]{1,0:T(8,128)(2,1)}) %reduce-scatter.13.cloned.1.call-update) | async-done | bytes 786448 | tf_op jit(solution)/shard_map/reduce_scatter | solution.py:174
  480.8 1.9 fusion.13
  482.7 1.6 fusion.41
  484.8 7.7 convolution_convert_fusion.5
  492.5 11.6 %convolution_convert_fusion.1 = bf16[1536,2048]{1,0:T(8,128)(2,1)} fusion(bf16[1024,1536]{1,0:T(8,128)(2,1)} %all-gather.21.cloned.1.call-done, bf16[1024,1024]{1,0:T(8,128)(2,1)} %copy-done.15, bf16[1024,1024]{1,0:T(8,128)(2,1)} %copy-done.14), kind=kOutput, calls=%fused_computation.1 | convolution fusion | flops 6453985280 | bytes 13631488 | tf_op jit(solution)/shard_map/dot_general | solution.py:18
  504.4 24.1 %all-gather.29.cloned.1.call-done = bf16[1024,1536]{1,0:T(8,128)(2,1)} async-done(((bf16[256,1536]{1,0:T(8,128)(2,1)}), bf16[1024,1536]{1,0:T(8,128)(2,1)}) %all-gather.29.cloned.1.call-update) | async-done | bytes 3145744 | tf_op jit(solution)/shard_map/all_gather | solution.py:170
  528.4 5.9 multiply_convert_fusion.2
  534.3 19.5 %attention_bwd.1 = (bf16[1024,384]{1,0:T(8,128)(2,1)}, bf16[1024,384]{1,0:T(8,128)(2,1)}, bf16[1024,384]{1,0:T(8,128)(2,1)}, f32[3,2,1024]{2,1,0:T(2,128)}, f32[3,1024,2]{2,1,0:T(8,128)}) custom-call(bf16[1024,384]{1,0:T(8,128)(2,1)} %multiply_convert_fusion.4.q_ref, bf16[1024,384]{1,0:T(8,128)(2,1)} %get-tuple-element.41.k_ref, ...), custom_call_target="tpu_custom_call" | custom-call | flops 4026531840 | bytes 5505024 | tf_op jit(solution)/shard_map/attention_bwd/pallas_call | solution.py:146
  553.9 1.9 copy.70
  557.2 1.7 reduce-window.16
  559.2 2.2 constant_dynamic-update-slice_fusion.2
  561.4 5.1 convolution_convert_fusion.7
  566.8 2.2 constant_dynamic-update-slice_fusion.1
  570.7 2.3 constant_dynamic-update-slice_fusion
  573.0 1.6 fusion.44
  574.7 3.1 fusion.27
  578.5 9.9 convolution_convert_fusion
  589.0 53.7 %reduce-scatter.21.cloned.1.call-done = bf16[192,2048]{1,0:T(8,128)(2,1)} async-done(((bf16[1536,2048]{1,0:T(8,128)(2,1)}), bf16[192,2048]{1,0:T(8,128)(2,1)}) %reduce-scatter.21.cloned.1.call-update) | async-done | bytes 786448 | tf_op jit(solution)/shard_map/reduce_scatter | solution.py:174
  642.8 10.1 %convolution_convert_fusion.3 = bf16[1024,1536]{1,0:T(8,128)(2,1)} fusion(bf16[1024,1664]{1,0:T(8,128)(2,1)} %pad_dynamic-update-slice_fusion, bf16[1536,1664]{1,0:T(8,128)(2,1)} %all-gather.17.cloned.1.call-done), kind=kOutput, calls=%fused_computation.12 | convolution fusion | flops 5236064256 | bytes 11665408 | tf_op jit(solution)/shard_map/dot_general | solution.py:24
  652.9 7.6 convolution_convert_fusion.6
  660.7 16.1 %reduce-scatter.19.cloned.1.call-done = bf16[48,1536]{1,0:T(8,128)(2,1)} async-done(((bf16[384,1536]{1,0:T(8,128)(2,1)}), bf16[48,1536]{1,0:T(8,128)(2,1)}) %reduce-scatter.19.cloned.1.call-update) | async-done | bytes 147472 | tf_op jit(solution)/shard_map/reduce_scatter | solution.py:174
  676.8 10.5 %all-gather.1 = bf16[192,1536]{1,0:T(8,128)(2,1)S(1)} all-gather(bf16[48,1536]{1,0:T(8,128)(2,1)} %reduce-scatter.19.cloned.1.call-done), channel_id=3, replica_groups=mesh['seq'=4,'wshard'=8] {'seq'}, dimensions={0}, use_global_device_ids=true | all-gather | bytes 737280 | tf_op jit(solution)/shard_map/all_gather | solution.py:318
  688.5 4.3 all-to-all-start
  692.8 61.3 %reduce-scatter.17.cloned.1.call-done = bf16[192,1664]{1,0:T(8,128)(2,1)} async-done(((bf16[1536,1664]{1,0:T(8,128)(2,1)}), bf16[192,1664]{1,0:T(8,128)(2,1)}) %reduce-scatter.17.cloned.1.call-update) | async-done | bytes 638992 | tf_op jit(solution)/shard_map/reduce_scatter | solution.py:174
  754.2 37.8 %all-gather.31.cloned.1.call-done = bf16[512,1536]{1,0:T(8,128)(2,1)} async-done(((bf16[128,1536]{1,0:T(8,128)(2,1)}), bf16[512,1536]{1,0:T(8,128)(2,1)}) %all-gather.31.cloned.1.call-update) | async-done | bytes 1572880 | tf_op jit(solution)/shard_map/all_gather | solution.py:170
  792.0 3.5 convert_element_type.231
  798.1 39.7 %all-gather.35.cloned.1.call-done = bf16[768,2048]{1,0:T(8,128)(2,1)} async-done(((bf16[192,2048]{1,0:T(8,128)(2,1)}), bf16[768,2048]{1,0:T(8,128)(2,1)}) %all-gather.35.cloned.1.call-update) | async-done | bytes 3145744 | tf_op jit(solution)/shard_map/all_gather | solution.py:329
  837.8 4.3 slice_convert_fusion
  842.8 3.7 copy.104
  846.6 5.3 reshape.188
  851.9 2.8 copy.95
  854.7 3.7 copy.103
  858.4 5.1 reshape.189
  863.5 21.4 %reduce-scatter.15.cloned.1.call-done = bf16[256,1536]{1,0:T(8,128)(2,1)} async-done(((bf16[1024,1536]{1,0:T(8,128)(2,1)}), bf16[256,1536]{1,0:T(8,128)(2,1)}) %reduce-scatter.15.cloned.1.call-update) | async-done | bytes 786448 | tf_op jit(solution)/shard_map/reduce_scatter | solution.py:174
  884.9 1.8 fusion.14
  886.7 40.0 %all-reduce.2 = (f32[1536]{0:T(1024)}, f32[24]{0:T(128)}, f32[1536]{0:T(1024)}) all-reduce(f32[1536]{0:T(1024)S(1)} %get-tuple-element.30, f32[24]{0:T(128)S(1)} %negate_dynamic-update-slice_fusion, f32[1536]{0:T(1024)S(1)} %get-tuple-element.28), channel_id=1, replica_groups=mesh['seq'=4,'wshard'=8] {'seq','wshard'}, use_global_device_ids=true, to_apply=%region_13.14 | all-reduce | flops 3096 | bytes 24768 | tf_op jit(solution)/shard_map/psum | solution.py:344
  926.8 6.0 reduce-scatter.11.cloned.1.call-done
  932.8 4.0 fusion.17
  936.8 37.1 %all-gather.33.cloned.1.call-done = bf16[768,1664]{1,0:T(8,128)(2,1)} async-done(((bf16[192,1664]{1,0:T(8,128)(2,1)}), bf16[768,1664]{1,0:T(8,128)(2,1)}) %all-gather.33.cloned.1.call-update) | async-done | bytes 2555920 | tf_op jit(solution)/shard_map/all_gather | solution.py:328
  973.8 1.9 convert_bitcast_fusion
  (132 shorter events, 34.1 us)
Async XLA Ops:
  7.2 213.6 %copy-start = (bf16[512,1536]{1,0:T(8,128)(2,1)S(1)}, bf16[512,1536]{1,0:T(8,128)(2,1)}, u32[]{:S(2)}) copy-start(bf16[512,1536]{1,0:T(8,128)(2,1)} %param.28) | copy-start | bytes 4718596
  7.2 50.7 %all-gather.15.cloned.1.call-start = ((), (), s32[]{:S(2)}) async-start(), calls=%async_computation.9 | async-start | bytes 3932160 | tf_op jit(solution)/shard_map/all_gather | solution.py:170
  8.7 8.7 copy-start.13
  11.0 104.0 %all-gather.17.cloned.1.call-start = ((), (), s32[]{:S(2)}) async-start(), calls=%async_computation.10 | async-start | bytes 5750784 | tf_op jit(solution)/shard_map/all_gather | solution.py:170
  15.8 0.8 copy-start.8
  16.6 150.6 %all-gather.19.cloned.1.call-start = ((), (), s32[]{:S(2)}) async-start(), calls=%async_computation.11 | async-start | bytes 5308416 | tf_op jit(solution)/shard_map/all_gather | solution.py:170
  17.3 198.3 %reduce-scatter.9.cloned.1.call-start = ((), (), s32[]{:S(2)}) async-start(), calls=%async_computation.12 | async-start | bytes 3932160 | tf_op jit(solution)/shard_map/reduce_scatter | solution.py:174
  125.8 1.7 copy-start.6
  172.7 109.7 %all-gather.23.cloned.1.call-start = ((), (), s32[]{:S(2)}) async-start(), calls=%async_computation.14 | async-start | bytes 7077888 | tf_op jit(solution)/shard_map/all_gather | solution.py:170
  185.9 29.7 %copy-start.2 = (bf16[1,256,1536]{2,1,0:T(8,128)(2,1)S(1)}, bf16[1,256,1536]{2,1,0:T(8,128)(2,1)}, u32[]{:S(2)}) copy-start(bf16[1,256,1536]{2,1,0:T(8,128)(2,1)} %param.15) | copy-start | bytes 2359300
  186.1 31.1 %copy-start.10 = (f32[1536]{0:T(1024)S(1)}, f32[1536]{0:T(1024)}, u32[]{:S(2)}) copy-start(f32[1536]{0:T(1024)} %param.25) | copy-start | bytes 18436
  187.1 140.4 %all-gather.21.cloned.1.call-start = ((), (), s32[]{:S(2)}) async-start(), calls=%async_computation.13 | async-start | bytes 3932160 | tf_op jit(solution)/shard_map/all_gather | solution.py:170
  215.7 1.6 copy-start.3
  218.4 155.4 %all-gather.27.cloned.1.call-start = ((), (), s32[]{:S(2)}) async-start(), calls=%async_computation.17 | async-start | bytes 3932160 | tf_op jit(solution)/shard_map/all_gather | solution.py:170
  220.7 193.7 %all-gather.25.cloned.1.call-start = ((), (), s32[]{:S(2)}) async-start(), calls=%async_computation.15 | async-start | bytes 3538944 | tf_op jit(solution)/shard_map/all_gather | solution.py:170
  221.5 259.2 %reduce-scatter.13.cloned.1.call-start = ((), (), s32[]{:S(2)}) async-start(), calls=%async_computation.18 | async-start | bytes 3932160 | tf_op jit(solution)/shard_map/reduce_scatter | solution.py:174
  425.8 1.4 copy-start.14
  425.8 2.0 copy-start.15
  437.8 44.9 %copy-start.4 = (bf16[1,256,1536]{2,1,0:T(8,128)(2,1)S(1)}, bf16[1,256,1536]{2,1,0:T(8,128)(2,1)}, u32[]{:S(2)}) copy-start(bf16[1,256,1536]{2,1,0:T(8,128)(2,1)} %param.29) | copy-start | bytes 2359300
  437.8 90.6 %all-gather.29.cloned.1.call-start = ((), (), s32[]{:S(2)}) async-start(), calls=%async_computation.19 | async-start | bytes 3932160 | tf_op jit(solution)/shard_map/all_gather | solution.py:170
  480.8 1.9 copy-start.5
  484.3 104.2 %reduce-scatter.23.cloned.1.call-start = ((), (), s32[]{:S(2)}) async-start(), calls=%async_computation.24 | async-start | bytes 3538944 | tf_op jit(solution)/shard_map/reduce_scatter | solution.py:174
  492.5 150.3 %reduce-scatter.21.cloned.1.call-start = ((), (), s32[]{:S(2)}) async-start(), calls=%async_computation.23 | async-start | bytes 7077888 | tf_op jit(solution)/shard_map/reduce_scatter | solution.py:174
  504.1 172.7 %reduce-scatter.19.cloned.1.call-start = ((), (), s32[]{:S(2)}) async-start(), calls=%async_computation.22 | async-start | bytes 1327104 | tf_op jit(solution)/shard_map/reduce_scatter | solution.py:174
  566.6 187.6 %reduce-scatter.17.cloned.1.call-start = ((), (), s32[]{:S(2)}) async-start(), calls=%async_computation.21 | async-start | bytes 5750784 | tf_op jit(solution)/shard_map/reduce_scatter | solution.py:174
  570.7 4.0 copy-start.7
  570.7 4.0 copy-start.9
  574.6 3.9 copy-start.12
  588.4 203.6 %all-gather.31.cloned.1.call-start = ((), (), s32[]{:S(2)}) async-start(), calls=%async_computation.25 | async-start | bytes 1966080 | tf_op jit(solution)/shard_map/all_gather | solution.py:170
  589.0 248.8 %all-gather.35.cloned.1.call-start = ((), (), s32[]{:S(2)}) async-start(), calls=%async_computation.27 | async-start | bytes 3932160 | tf_op jit(solution)/shard_map/all_gather | solution.py:329
  642.8 242.1 %reduce-scatter.15.cloned.1.call-start = ((), (), s32[]{:S(2)}) async-start(), calls=%async_computation.20 | async-start | bytes 3932160 | tf_op jit(solution)/shard_map/reduce_scatter | solution.py:174
  652.9 279.9 %reduce-scatter.11.cloned.1.call-start = ((), (), s32[]{:S(2)}) async-start(), calls=%async_computation.16 | async-start | bytes 3932160 | tf_op jit(solution)/shard_map/reduce_scatter | solution.py:174
  688.5 107.2 %all-to-all-start = ((bf16[8,48,1536]{2,1,0:T(8,128)(2,1)}), bf16[8,48,1536]{2,1,0:T(8,128)(2,1)}, u32[]{:S(2)}, u32[]{:S(2)}) async-start(bf16[8,48,1536]{2,1,0:T(8,128)(2,1)} %bitcast_select_fusion), calls=%async_computation.6 | async-start | bytes 2359296 | tf_op jit(solution)/shard_map/all_to_all | solution.py:323
  692.8 281.1 %all-gather.33.cloned.1.call-start = ((), (), s32[]{:S(2)}) async-start(), calls=%async_computation.26 | async-start | bytes 3194880 | tf_op jit(solution)/shard_map/all_gather | solution.py:328
  858.4 26.5 %copy-start.11 = (f32[1536]{0:T(1024)S(1)}, f32[1536]{0:T(1024)}, u32[]{:S(2)}) copy-start(f32[1536]{0:T(1024)} %param.17) | copy-start | bytes 18436
  979.0 3.1 copy-start.1
Sparse Core Ops, SparseCore 0:
  11.2 46.6 all-gather.14
  60.1 54.9 all-gather.16
  116.7 50.4 all-gather.18
  172.9 42.7 reduce-scatter.8
  217.7 64.7 all-gather.22
  284.8 42.6 all-gather.20
  329.8 43.9 all-gather.26
  376.1 38.2 all-gather.24
  437.9 42.8 reduce-scatter.12
  484.4 43.9 all-gather.28
  531.3 40.3 reduce-scatter.22
  573.8 68.8 reduce-scatter.20
  645.6 31.1 reduce-scatter.18
  679.0 75.0 reduce-scatter.16
  756.0 35.9 all-gather.30
  793.8 43.9 all-gather.34
  840.9 43.9 reduce-scatter.14
  888.0 44.6 reduce-scatter.10
  934.7 39.0 all-gather.32

commit v2 on v1

--- a/solution.py
+++ b/solution.py
@@ -166,12 +166,405 @@
     )(q, k, v, d_out, cum_row, key_col, lse)
 
 
+MESH = pl.DeviceIdType.MESH
+VMEM_LIMIT = 62 << 20
+
+
+def square(groups):
+    return groups == 4
+
+
+def sides():
+    rank = lax.axis_index("seq")
+    return rank, rank + 1 - 2 * lax.rem(rank, 2), lax.rem(rank + 2, 4), 3 - rank
+
+
+def meet(*others):
+    barrier = pltpu.get_barrier_semaphore()
+    for other in others:
+        pl.semaphore_signal(barrier, inc=1, device_id=other, device_id_type=MESH)
+    pl.semaphore_wait(barrier, len(others))
+
+
+def push(source, target, send, recv, device):
+    copy = pltpu.make_async_remote_copy(
+        src_ref=source,
+        dst_ref=target,
+        send_sem=send,
+        recv_sem=recv,
+        device_id=device,
+        device_id_type=MESH,
+    )
+    copy.start()
+    return copy
+
+
+class SquareGather:
+    def __init__(self, own, full, send, recv):
+        self.own, self.full, self.send, self.recv = own, full, send, recv
+        self.rows = own.shape[0]
+        self.half = self.rows // 2
+
+    def place(self, rank, part):
+        return self.full.at[pl.ds(pl.multiple_of(rank * self.rows + part * self.half, self.half), self.half)]
+
+    def start(self):
+        me, side, down, across = sides()
+        mine = [self.own.at[pl.ds(part * self.half, self.half)] for part in (0, 1)]
+        to_side, to_down = {"seq": side}, {"seq": down}
+        self.first = push(mine[0], self.place(me, 0), self.send.at[0], self.recv.at[0], to_side)
+        self.second = push(mine[1], self.place(me, 1), self.send.at[1], self.recv.at[1], to_down)
+        self.third = push(mine[1], self.place(me, 1), self.send.at[2], self.recv.at[2], to_side)
+        self.fourth = push(mine[0], self.place(me, 0), self.send.at[3], self.recv.at[3], to_down)
+
+    def relay(self):
+        me, side, down, across = sides()
+        self.first.wait_recv()
+        self.fifth = push(
+            self.place(side, 0), self.place(side, 0), self.send.at[4], self.recv.at[4], {"seq": down}
+        )
+        self.second.wait_recv()
+        self.sixth = push(
+            self.place(down, 1), self.place(down, 1), self.send.at[5], self.recv.at[5], {"seq": side}
+        )
+
+    def near(self):
+        self.third.wait_recv()
+        self.fourth.wait_recv()
+
+    def far(self):
+        self.fifth.wait_recv()
+        self.sixth.wait_recv()
+
+    def finish(self):
+        for copy in (self.first, self.second, self.third, self.fourth, self.fifth, self.sixth):
+            copy.wait_send()
+
+
+def gather_square(values, collective_id):
+    count = len(values)
+
+    def body(*refs):
+        own, full = refs[:count], refs[count : 2 * count]
+        send, recv, local = refs[2 * count :]
+        me, side, down, across = sides()
+        meet({"seq": side}, {"seq": down})
+        jobs = [SquareGather(own[i], full[i], send.at[i], recv.at[i]) for i in range(count)]
+        keeps = []
+        for i, job in enumerate(jobs):
+            job.start()
+            rows = own[i].shape[0]
+            keep = pltpu.make_async_copy(
+                own[i], full[i].at[pl.ds(pl.multiple_of(me * rows, rows), rows)], local.at[i]
+            )
+            keep.start()
+            keeps.append(keep)
+        for job in jobs:
+            job.relay()
+        for job, keep in zip(jobs, keeps):
+            job.near()
+            job.far()
+            job.finish()
+            keep.wait()
+
+    return pl.pallas_call(
+        body,
+        in_specs=[pl.BlockSpec(memory_space=pltpu.VMEM)] * count,
+        out_specs=[pl.BlockSpec(memory_space=pl.ANY)] * count,
+        out_shape=[jax.ShapeDtypeStruct((4 * v.shape[0],) + v.shape[1:], v.dtype) for v in values],
+        scratch_shapes=[
+            pltpu.SemaphoreType.DMA((count, 6)),
+            pltpu.SemaphoreType.DMA((count, 6)),
+            pltpu.SemaphoreType.DMA((count,)),
+        ],
+        compiler_params=pltpu.CompilerParams(
+            collective_id=collective_id, has_side_effects=True, vmem_limit_bytes=VMEM_LIMIT
+        ),
+        name="gather_square",
+    )(*values)
+
+
+def block_product(left, right, transposed, tile, store):
+    total = right.shape[0] if transposed else right.shape[1]
+
+    def step(number, carry):
+        columns = pl.ds(pl.multiple_of(number * tile, tile), tile)
+        if transposed:
+            store(columns, product_nt(left, right[columns, :]))
+        else:
+            store(columns, product(left, right[:, columns]))
+        return carry
+
+    lax.fori_loop(0, total // tile, step, 0)
+
+
+def gather_product(own, weight, transposed, collective_id):
+    rows, depth = own.shape
+    width = weight.shape[0] if transposed else weight.shape[1]
+    tile = 512 if width % 512 == 0 else 128 * (width // 128 // 3) if width % 384 == 0 else 128
+
+    def body(own_ref, weight_ref, full, out, send, recv):
+        me, side, down, across = sides()
+        meet({"seq": side}, {"seq": down})
+        job = SquareGather(own_ref, full, send, recv)
+        job.start()
+
+        def multiply(rank, block):
+            at = pl.ds(pl.multiple_of(rank * rows, rows), rows)
+
+            def store(columns, value):
+                out[at, columns] = value.astype(out.dtype)
+
+            block_product(block, weight_ref, transposed, tile, store)
+
+        def arrived(rank):
+            return full[pl.ds(pl.multiple_of(rank * rows, rows), rows), :]
+
+        full[pl.ds(pl.multiple_of(me * rows, rows), rows), :] = own_ref[...]
+        multiply(me, own_ref[...])
+        job.relay()
+        job.near()
+        multiply(side, arrived(side))
+        multiply(down, arrived(down))
+        job.far()
+        multiply(across, arrived(across))
+        job.finish()
+
+    vmem = pl.BlockSpec(memory_space=pltpu.VMEM)
+    return pl.pallas_call(
+        body,
+        in_specs=[vmem, vmem],
+        out_specs=[vmem, vmem],
+        out_shape=[
+            jax.ShapeDtypeStruct((4 * rows, depth), own.dtype),
+            jax.ShapeDtypeStruct((4 * rows, width), jnp.float32),
+        ],
+        scratch_shapes=[pltpu.SemaphoreType.DMA((6,)), pltpu.SemaphoreType.DMA((6,))],
+        compiler_params=pltpu.CompilerParams(
+            collective_id=collective_id, has_side_effects=True, vmem_limit_bytes=VMEM_LIMIT
+        ),
+        name="gather_product",
+    )(own, weight)
+
+
+def product_scatter(lefts, rights, transposed, collective_id):
+    count = len(lefts)
+    rows = lefts[0].shape[0] // 4
+    half = rows // 2
+    width = rights[0].shape[0] if transposed else rights[0].shape[1]
+    tile = width // 3 if width % 384 == 0 else width
+
+    def body(*refs):
+        left, right = refs[:count], refs[count : 2 * count]
+        out, far, near, kept, land, carry, send, recv = refs[2 * count :]
+        me, side, down, across = sides()
+        meet({"seq": side}, {"seq": down})
+        to_side, to_down = {"seq": side}, {"seq": down}
+
+        def partial(rank, store):
+            at = pl.ds(pl.multiple_of(rank * rows, rows), rows)
+
+            def step(number, carried):
+                columns = pl.ds(pl.multiple_of(number * tile, tile), tile)
+                value = None
+                for a, b in zip(left, right):
+                    term = product_nt(a[at, :], b[columns, :]) if transposed else product(a[at, :], b[:, columns])
+                    value = term if value is None else value + term
+                store(columns, value)
+                return carried
+
+            lax.fori_loop(0, width // tile, step, 0)
+
+        def store_far(columns, value):
+            far[:, columns] = value.astype(far.dtype)
+
+        def store_side(columns, value):
+            kept[0, :, columns] = value[:half]
+            near[0, :, columns] = value[half:].astype(near.dtype)
+
+        def store_down(columns, value):
+            near[1, :, columns] = value[:half].astype(near.dtype)
+            kept[1, :, columns] = value[half:]
+
+        def store_own(columns, value):
+            out[:, columns] = value
+
+        partial(across, store_far)
+        first = push(far.at[pl.ds(0, half)], land.at[0], send.at[0], recv.at[0], to_down)
+        second = push(far.at[pl.ds(half, half)], land.at[1], send.at[1], recv.at[1], to_side)
+        partial(side, store_side)
+        third = push(near.at[0], land.at[2], send.at[2], recv.at[2], to_side)
+        partial(down, store_down)
+        fourth = push(near.at[1], land.at[3], send.at[3], recv.at[3], to_down)
+        first.wait_recv()
+        carry[0] = (kept[0] + land[0].astype(jnp.float32)).astype(carry.dtype)
+        fifth = push(carry.at[0], land.at[4], send.at[4], recv.at[4], to_side)
+        second.wait_recv()
+        carry[1] = (kept[1] + land[1].astype(jnp.float32)).astype(carry.dtype)
+        sixth = push(carry.at[1], land.at[5], send.at[5], recv.at[5], to_down)
+        partial(me, store_own)
+        third.wait_recv()
+        fourth.wait_recv()
+        fifth.wait_recv()
+        out[:half, :] += land[3].astype(jnp.float32) + land[4].astype(jnp.float32)
+        sixth.wait_recv()
+        out[half:, :] += land[2].astype(jnp.float32) + land[5].astype(jnp.float32)
+        for copy in (first, second, third, fourth, fifth, sixth):
+            copy.wait_send()
+
+    vmem = pl.BlockSpec(memory_space=pltpu.VMEM)
+    low = jnp.bfloat16
+    return pl.pallas_call(
+        body,
+        in_specs=[vmem] * (2 * count),
+        out_specs=vmem,
+        out_shape=jax.ShapeDtypeStruct((rows, width), jnp.float32),
+        scratch_shapes=[
+            pltpu.VMEM((rows, width), low),
+            pltpu.VMEM((2, half, width), low),
+            pltpu.VMEM((2, half, width), jnp.float32),
+            pltpu.VMEM((6, half, width), low),
+            pltpu.VMEM((2, half, width), low),
+            pltpu.SemaphoreType.DMA((6,)),
+            pltpu.SemaphoreType.DMA((6,)),
+        ],
+        compiler_params=pltpu.CompilerParams(
+            collective_id=collective_id, has_side_effects=True, vmem_limit_bytes=VMEM_LIMIT
+        ),
+        name="product_scatter",
+    )(*lefts, *rights)
+
+
+def gather_and_spread(values, block, collective_id):
+    count = len(values)
+    rows, width = block.shape
+
+    def body(*refs):
+        own, mine = refs[:count], refs[count]
+        full, whole = refs[count + 1 : 2 * count + 1], refs[2 * count + 1]
+        send, recv, local, line_send, line_recv = refs[2 * count + 2 :]
+        me, side, down, across = sides()
+        shards = lax.axis_size("wshard")
+        place = lax.axis_index("wshard")
+        chips = shards // 2
+        chip, core = place // 2, lax.rem(place, 2)
+        nexts = {"wshard": lax.rem(place + 2, shards)}
+        before = {"wshard": lax.rem(place + shards - 2, shards)}
+        twin = {"wshard": place + 1 - 2 * core}
+        meet({"seq": side}, {"seq": down}, nexts, before, twin)
+        jobs = [SquareGather(own[i], full[i], send.at[i], recv.at[i]) for i in range(count)]
+        mine_at = whole.at[core]
+
+        def along(index, device):
+            return pltpu.make_async_remote_copy(
+                src_ref=mine_at,
+                dst_ref=mine_at,
+                send_sem=line_send.at[index],
+                recv_sem=line_recv.at[0],
+                device_id=device,
+                device_id_type=MESH,
+            )
+
+        forth, back = along(0, nexts), along(1, before)
+        to_twin = pltpu.make_async_remote_copy(
+            src_ref=mine_at,
+            dst_ref=mine_at,
+            send_sem=line_send.at[2],
+            recv_sem=line_recv.at[1],
+            device_id=twin,
+            device_id_type=MESH,
+        )
+        goes_forth = (chip >= me) & (chip < chips - 1)
+        goes_back = (chip <= me) & (chip > 0)
+        jobs[0].start()
+
+        @pl.when(chip == me)
+        def _():
+            whole[core] = mine[...]
+
+        @pl.when(chip != me)
+        def _():
+            forth.wait_recv()
+
+        @pl.when(goes_forth)
+        def _():
+            forth.start()
+
+        @pl.when(goes_back)
+        def _():
+            back.start()
+
+        to_twin.start()
+        keeps = []
+        for i, job in enumerate(jobs):
+            if i:
+                job.start()
+            size = own[i].shape[0]
+            keep = pltpu.make_async_copy(
+                own[i], full[i].at[pl.ds(pl.multiple_of(me * size, size), size)], local.at[i]
+            )
+            keep.start()
+            keeps.append(keep)
+        for job in jobs:
+            job.relay()
+        for job, keep in zip(jobs, keeps):
+            job.near()
+            job.far()
+            job.finish()
+            keep.wait()
+        to_twin.wait_recv()
+        to_twin.wait_send()
+
+        @pl.when(goes_forth)
+        def _():
+            forth.wait_send()
+
+        @pl.when(goes_back)
+        def _():
+            back.wait_send()
+
+    vmem = pl.BlockSpec(memory_space=pltpu.VMEM)
+    anywhere = pl.BlockSpec(memory_space=pl.ANY)
+    return pl.pallas_call(
+        body,
+        in_specs=[vmem] * (count + 1),
+        out_specs=[anywhere] * count + [vmem],
+        out_shape=[jax.ShapeDtypeStruct((4 * v.shape[0],) + v.shape[1:], v.dtype) for v in values]
+        + [jax.ShapeDtypeStruct((2, rows, width), block.dtype)],
+        scratch_shapes=[
+            pltpu.SemaphoreType.DMA((count, 6)),
+            pltpu.SemaphoreType.DMA((count, 6)),
+            pltpu.SemaphoreType.DMA((count,)),
+            pltpu.SemaphoreType.DMA((3,)),
+            pltpu.SemaphoreType.DMA((2,)),
+        ],
+        compiler_params=pltpu.CompilerParams(
+            collective_id=collective_id, has_side_effects=True, vmem_limit_bytes=VMEM_LIMIT
+        ),
+        name="gather_and_spread",
+    )(*values, block)
+
+
 def gather(value, axis_name):
     return lax.all_gather(value, axis_name, axis=0, tiled=True)
 
 
 def scatter(value, axis_name):
     return lax.psum_scatter(value, axis_name, scatter_dimension=0, tiled=True)
+
+
+def gather_multiply(own, weight, transposed, collective_id):
+    if square(lax.axis_size("seq")):
+        return gather_product(own, weight, transposed, collective_id)
+    whole = gather(own, "seq")
+    return whole, product_nt(whole, weight) if transposed else product(whole, weight)
+
+
+def multiply_scatter(lefts, rights, transposed, collective_id):
+    if square(lax.axis_size("seq")):
+        return product_scatter(lefts, rights, transposed, collective_id)
+    total = sum(product_nt(a, b) if transposed else product(a, b) for a, b in zip(lefts, rights))
+    return scatter(total.astype(jnp.bfloat16), "seq").astype(jnp.float32)
 
 
 def on_device(
@@ -225,23 +618,31 @@
     own_forget = lax.dynamic_slice_in_dim(w_forget, seq_rank * local_heads, local_heads, 1)
     own_forget = jnp.pad(own_forget, ((0, 0), (0, pad_heads - local_heads)))
     mine_attn = jnp.concatenate(
-        [own_columns(w_query), own_columns(w_key), own_columns(w_value), own_columns(w_ogate), own_forget],
+        [own_columns(w_query), own_columns(w_key), own_columns(w_value), own_forget],
         axis=1,
     )
     mine_ffn = jnp.concatenate([own_units(w_gate), own_units(w_up)], axis=1)
     mine_down = lax.dynamic_slice_in_dim(w_down, seq_rank * part, part, 0)
+    fast = square(groups) and shards == 2 * groups
     full_attn = gather(mine_attn, "wshard")
-    full_out = lax.dynamic_slice_in_dim(gather(w_out, "wshard"), seq_rank * columns, columns, 0)
+    full_ogate = gather(own_columns(w_ogate), "wshard")
+    normed_attn_own = rms_norm(inputs, norm_attn).astype(low)
+    if fast:
+        normed_attn, cotangent_all, full_out = gather_and_spread([normed_attn_own, cotangent_low], w_out, 0)
+        full_out = full_out.reshape(columns, width)
+    else:
+        normed_attn = gather(normed_attn_own, "seq")
+        cotangent_all = gather(cotangent_low, "seq")
+        full_out = lax.dynamic_slice_in_dim(gather(w_out, "wshard"), seq_rank * columns, columns, 0)
     full_ffn = gather(mine_ffn, "wshard")
     full_down = gather(mine_down, "wshard")
 
-    normed_attn = gather(rms_norm(inputs, norm_attn).astype(low), "seq")
     projected = product(normed_attn, full_attn)
     queries = projected[:, :columns].astype(low)
     keys = projected[:, columns : 2 * columns].astype(low)
     values = projected[:, 2 * columns : 3 * columns].astype(low)
-    gate_pre = projected[:, 3 * columns : 4 * columns]
-    forget_pre = projected[:, 4 * columns : 4 * columns + local_heads].astype(low)
+    gate_pre = product(normed_attn, full_ogate)
+    forget_pre = projected[:, 3 * columns : 3 * columns + local_heads].astype(low)
     bias_local = lax.dynamic_slice_in_dim(forget_bias, seq_rank * local_heads, local_heads)
     forget_total = forget_pre.astype(jnp.float32) + bias_local
     log_forget, pull_forget = jax.vjp(jax.nn.log_sigmoid, forget_total)
@@ -263,31 +664,26 @@
     attended = attended_low[:, :columns].astype(jnp.float32)
     gated_full, pull_gate = jax.vjp(gate_product, attended, gate_pre)
     gated = gated_full.astype(low)
-    branch = scatter(product(gated, full_out).astype(low), "seq")
-    middle = inputs + branch.astype(jnp.float32)
+    branch = multiply_scatter([gated], [full_out], False, 1)
+    middle = inputs + branch
     normed_ffn_own, pull_ffn_norm = jax.vjp(rms_norm, middle, norm_ffn)
-    normed_ffn = gather(normed_ffn_own.astype(low), "seq")
-    gate_up = product(normed_ffn, full_ffn)
+    normed_ffn, gate_up = gather_multiply(normed_ffn_own.astype(low), full_ffn, False, 2)
     units = shards * part
     hidden_full, pull_swiglu = jax.vjp(swiglu, gate_up[:, :units], gate_up[:, units:])
     hidden = hidden_full.astype(low)
-    lowered = scatter(product(hidden, full_down).astype(low), "seq")
-    layer_output = (middle + lowered.astype(jnp.float32)).astype(low)[None]
-
-    cotangent_all = gather(cotangent_low, "seq")
+
     grad_w_down = product_tn(hidden, cotangent_all).astype(low)
     grad_hidden = product_nt(cotangent_all, full_down)
     grad_gate_full, grad_up_full = pull_swiglu(grad_hidden)
     grad_gate_up = jnp.concatenate([grad_gate_full.astype(low), grad_up_full.astype(low)], axis=1)
     grad_w_ffn = product_tn(normed_ffn, grad_gate_up).astype(low)
-    grad_normed_ffn = scatter(product_nt(grad_gate_up, full_ffn).astype(low), "seq")
+    grad_normed_ffn = multiply_scatter([grad_gate_up], [full_ffn], True, 3)
     share_down = scatter(grad_w_down, "wshard")
     share_ffn = scatter(grad_w_ffn, "wshard")
-    grad_middle_part, grad_norm_ffn = pull_ffn_norm(grad_normed_ffn.astype(jnp.float32))
+    grad_middle_part, grad_norm_ffn = pull_ffn_norm(grad_normed_ffn)
     grad_middle = cotangent + grad_middle_part
-    grad_branch = gather(grad_middle.astype(low), "seq")
+    grad_branch, grad_gated = gather_multiply(grad_middle.astype(low), full_out, True, 4)
     grad_w_out = product_tn(gated, grad_branch).astype(low)
-    grad_gated = product_nt(grad_branch, full_out)
     grad_attended_full, grad_gate_pre_full = pull_gate(grad_gated)
     grad_attended = pad_lanes(grad_attended_full.astype(low))
     grad_gate_pre = grad_gate_pre_full.astype(low)
@@ -304,14 +700,19 @@
         jnp.zeros((heads,), jnp.float32), grad_bias_local, seq_rank * local_heads, 0
     )
     grad_projected = jnp.concatenate(
-        [dq[:, :columns], dk[:, :columns], dv[:, :columns], grad_gate_pre, grad_forget], axis=1
+        [dq[:, :columns], dk[:, :columns], dv[:, :columns], grad_forget, grad_gate_pre], axis=1
     )
     grad_w_attn = product_tn(normed_attn, grad_projected).astype(low)
     share_attn = scatter(grad_w_attn, "wshard")
-    grad_normed_attn = scatter(product_nt(grad_projected, full_attn).astype(low), "seq")
+    front = full_attn.shape[1]
+    grad_normed_attn = multiply_scatter(
+        [grad_projected[:, :front], grad_gate_pre], [full_attn, full_ogate], True, 5
+    )
     unused_normed, pull_attn_norm = jax.vjp(rms_norm, inputs, norm_attn)
-    grad_input_part, grad_norm_attn = pull_attn_norm(grad_normed_attn.astype(jnp.float32))
+    grad_input_part, grad_norm_attn = pull_attn_norm(grad_normed_attn)
     grad_input = (grad_middle + grad_input_part)[None]
+    lowered = multiply_scatter([hidden], [full_down], False, 6)
+    layer_output = (middle + lowered).astype(low)[None]
 
     share_out = scatter(grad_w_out, "wshard")
     rows_out = columns // shards
@@ -325,13 +726,18 @@
     mine_out = lax.dynamic_index_in_dim(moved, shard_rank % per_block, 0, keepdims=False)
     grad_out = mine_out.reshape(columns // per_block, width).astype(jnp.float32)
 
-    every_attn = lax.all_gather(share_attn, "seq", axis=0, tiled=False)
-    every_ffn = lax.all_gather(share_ffn, "seq", axis=0, tiled=False)
-    grad_down = gather(share_down, "seq").astype(jnp.float32)
     rows = share_attn.shape[0]
+    if fast:
+        every_ffn, grad_down = gather_square([share_ffn, share_down], 7)
+        every_attn = gather_square([share_attn], 8)[0]
+    else:
+        every_ffn, grad_down, every_attn = [gather(v, "seq") for v in (share_ffn, share_down, share_attn)]
+    every_ffn = every_ffn.reshape((groups,) + share_ffn.shape)
+    every_attn = every_attn.reshape((groups,) + share_attn.shape)
+    grad_down = grad_down.astype(jnp.float32)
 
     def join(first):
-        taken = every_attn[:, :, first * columns : (first + 1) * columns]
+        taken = every_attn[:, :, first : first + columns]
         return taken.transpose(1, 0, 2).reshape(rows, width).astype(jnp.float32)
 
     def join_units(first):
@@ -339,7 +745,7 @@
         taken = taken.reshape(groups, rows, shards, part).transpose(1, 2, 0, 3)
         return taken.reshape(rows, hidden_size).astype(jnp.float32)
 
-    grad_forget_w = every_attn[:, :, 4 * columns : 4 * columns + local_heads]
+    grad_forget_w = every_attn[:, :, 3 * columns : 3 * columns + local_heads]
     grad_forget_w = grad_forget_w.transpose(1, 0, 2).reshape(rows, heads).astype(jnp.float32)
     small = lax.psum((grad_norm_attn, grad_norm_ffn, grad_bias), ("seq", "wshard"))
     return (
@@ -347,9 +753,9 @@
         grad_input,
         small[0],
         join(0),
-        join(1),
-        join(2),
-        join(3),
+        join(columns),
+        join(2 * columns),
+        join(front),
         grad_forget_w,
         small[2],
         grad_out,

time: 997 us -> 674 us (0.68)
  waiting for transfers between devices: 664 us -> 21.1 us
  Pallas kernels: 33.1 us -> 404 us
  matrix products: 107 us -> 57.8 us
    pallas_call x0 -> x9, Pallas kernels: none -> 371 us  [the longest x4 147 us: product_scatter(): pl.pallas_call(body, in_specs=[vmem] * (2 * count), out_specs=vmem, out_s...]
    all_gather x9 -> x4, waiting for transfers between devices: 356 us -> 0.05 us  [gather(): return lax.all_gather(value, axis_name, axis=0, tiled=True)]
    reduce_scatter x8 -> x4, waiting for transfers between devices: 230 us -> 20.9 us  [scatter(): return lax.psum_scatter(value, axis_name, scatter_dimension=0, tiled=True)]
    all_gather x2 -> x0, waiting for transfers between devices: 76.8 us -> none  [the longest x1 39.7 us: on_device(): every_ffn = lax.all_gather(share_ffn, 'seq', axis=0, tiled=False)]
    dot_general x4 -> x1, matrix products: 37.3 us -> 11.4 us  [product_nt(): lax.dot_general(left, right, (((1,), (1,)), ((), ())), preferred_element_...]
    dot_general x4 -> x2, matrix products: 35.5 us -> 13.2 us  [product(): return jnp.dot(left, right, preferred_element_type=jnp.float32)]
  transfers between devices with their start and end apart: 20 -> 9, of which waited for: 18 -> 1; matrix products, arithmetic and copies ran while one was open for 17% -> 15% of each run, Pallas kernels for 3% -> 42%
where the time goes in v2:
time: 674 us; the launch traced here: 667 us
  Pallas kernels  404 us (60%)
  local copies, waits for them, and re-layouts  65.8 us (10%)
  matrix products  57.8 us (9%)
  blocking collectives  51.2 us (8%)
  other arithmetic  46.5 us (7%)
  waiting for transfers between devices  21.1 us (3%)
  between operations  15.7 us (2%)
    pallas_call x4, Pallas kernels, product_scatter(): pl.pallas_call(body, in_specs=[vmem] * (2 * count), out_specs=vmem, out_s...  147 us
    pallas_call x1, Pallas kernels, gather_and_spread(): pl.pallas_call(body, in_specs=[vmem] * (count + 1), out_specs=[anywhere]...  94 us
    pallas_call x2, Pallas kernels, gather_square(): pl.pallas_call(body, in_specs=[pl.BlockSpec(memory_space=pltpu.VMEM)] * c...  65.4 us
    pallas_call x2, Pallas kernels, gather_product(): pl.pallas_call(body, in_specs=[vmem, vmem], out_specs=[vmem, vmem], out_s...  64.7 us
    psum x1, blocking collectives, on_device(): lax.psum((grad_norm_attn, grad_norm_ffn, grad_bias), ('seq', 'wshard'))  41.3 us
    dot_general x4, matrix products, product_tn(): lax.dot_general(left, right, (((0,), (0,)), ((), ())), preferred_element_...  33.1 us
    reduce_scatter x4, waiting for transfers between devices, scatter(): return lax.psum_scatter(value, axis_name, scatter_dimension=0, tiled=True)  20.9 us
    pallas_call x1, Pallas kernels, attention_bwd(): pl.pallas_call(body, grid=(pairs,), in_specs=[lane, lane, lane, lane, row...  19.7 us
  transfers between devices with their start and end apart: 9, of which 1 were waited for; matrix products, arithmetic and copies ran while one was open for 15% of the time, Pallas kernels for 42%

profile of v2, /device:TPU:0, one launch (start us, length us, event | category | flops | bytes accessed | tf_op | source)
XLA Modules:
  0.0 666.8 jit_solution(3335827232039962216)
XLA Ops:
  9.2 1.0 constant_dynamic-slice_fusion.4
  11.1 1.6 constant_dynamic-slice_fusion.2
  12.7 2.8 reshape.182
  15.6 3.8 reshape.184
  19.4 6.2 dynamic-slice_reduce_fusion
  28.7 1.0 bitcast_select_fusion.1.refs_1_
  29.7 1.1 fusion.6.refs_0_
  30.8 94.0 %gather_and_spread.1 = (bf16[1024,1536]{1,0:T(8,128)(2,1)}, bf16[1024,1536]{1,0:T(8,128)(2,1)}, bf16[2,192,1536]{2,1,0:T(8,128)(2,1)}) custom-call(bf16[256,1536]{1,0:T(8,128)(2,1)} %fusion.6.refs_0_, bf16[256,1536]{1,0:T(8,128)(2,1)} %bitcast_select_fusion.1.refs_1_, bf16[192,1536]{1,0:T(8,128)(2,1)} %refs_2_.1), custom_call_target="tpu_custom_call" | custom-call | tf_op jit(solution)/shard_map/gather_and_spread/pallas_call | solution.py:528
  124.9 7.4 %convolution_convert_fusion.2 = bf16[1024,1280]{1,0:T(8,128)(2,1)S(1)} fusion(bf16[1024,1536]{1,0:T(8,128)(2,1)} %get-tuple-element.30, bf16[1536,1280]{1,0:T(8,128)(2,1)} %all-gather.6.cloned.1.call-done.refs_2_), kind=kOutput, calls=%fused_computation.11 | convolution fusion | flops 4027842560 | bytes 9699328 | tf_op jit(solution)/shard_map/dot_general | solution.py:14
  132.3 1.5 copy-done.9
  134.3 1.7 reduce-window.14
  136.5 1.7 copy.63
  138.8 2.2 multiply_convert_fusion.4.q_ref
  141.0 2.7 fusion.30
  143.7 13.5 %attention_fwd.1 = (bf16[1024,384]{1,0:T(8,128)(2,1)}, f32[3,2,1024]{2,1,0:T(2,128)}) custom-call(bf16[1024,384]{1,0:T(8,128)(2,1)} %multiply_convert_fusion.4.q_ref, bf16[1024,384]{1,0:T(8,128)(2,1)} %get-tuple-element.65.k_ref, bf16[1024,384]{1,0:T(8,128)(2,1)} %get-tuple-element.64.v_ref, f32[3,2,1024]{2,1,0:T(2,128)} %reduce_window_sum.30.row_ref, ...), custom_call_target="tpu_custom_call" | custom-call | flops 1610612736 | bytes 3145728 | tf_op jit(solution)/shard_map/attention_fwd/pallas_call | solution.py:76
  157.2 5.8 fusion.8
  163.0 45.8 %product_scatter.4 = f32[256,1536]{1,0:T(8,128)} custom-call(bf16[1024,384]{1,0:T(8,128)(2,1)} %get-tuple-element.74.refs_0_, bf16[384,1536]{1,0:T(8,128)(2,1)} %bitcast.129), custom_call_target="tpu_custom_call" | custom-call | tf_op jit(solution)/shard_map/product_scatter/pallas_call | solution.py:417
  208.8 1.9 multiply_reduce_fusion.2
  210.7 1.1 multiply_convert_fusion.3.own_ref
  211.8 35.9 %gather_product.2 = (bf16[1024,1536]{1,0:T(8,128)(2,1)}, f32[1024,2048]{1,0:T(8,128)}) custom-call(bf16[256,1536]{1,0:T(8,128)(2,1)} %multiply_convert_fusion.3.own_ref, bf16[1536,2048]{1,0:T(8,128)(2,1)} %all-gather.10.cloned.1.call-done.weight_ref.refs_1_), custom_call_target="tpu_custom_call" | custom-call | tf_op jit(solution)/shard_map/gather_product/pallas_call | solution.py:334
  247.7 11.4 %fusion.2 = (bf16[1024,1024]{1,0:T(8,128)(2,1)S(1)}, bf16[1024,1024]{1,0:T(8,128)(2,1)S(1)}, bf16[1024,1024]{1,0:T(8,128)(2,1)}) fusion(f32[1024,2048]{1,0:T(8,128)} %get-tuple-element.33, bf16[1024,1536]{1,0:T(8,128)(2,1)} %get-tuple-element.34, bf16[1024,1536]{1,0:T(8,128)(2,1)} %all-gather.12.cloned.1.call-done.refs_1_), kind=kOutput, calls=%fused_computation.5 | convolution fusion | flops 3238002688 | bytes 20971520 | tf_op jit(solution)/shard_map/dot_general | solution.py:24
  259.1 1.3 copy-done.14
  261.1 2.4 pad_maximum_fusion.refs_0_
  263.5 32.6 %product_scatter.6 = f32[256,1536]{1,0:T(8,128)} custom-call(bf16[1024,2048]{1,0:T(8,128)(2,1)} %pad_maximum_fusion.refs_0_, bf16[1536,2048]{1,0:T(8,128)(2,1)} %all-gather.10.cloned.1.call-done.weight_ref.refs_1_), custom_call_target="tpu_custom_call" | custom-call | tf_op jit(solution)/shard_map/product_scatter/pallas_call | solution.py:417
  296.1 1.9 multiply_reduce_fusion
  298.2 1.4 fusion.26.own_ref
  299.6 28.8 %gather_product.3 = (bf16[1024,1536]{1,0:T(8,128)(2,1)}, f32[1024,384]{1,0:T(8,128)}) custom-call(bf16[256,1536]{1,0:T(8,128)(2,1)} %fusion.26.own_ref, bf16[384,1536]{1,0:T(8,128)(2,1)} %bitcast.130), custom_call_target="tpu_custom_call" | custom-call | tf_op jit(solution)/shard_map/gather_product/pallas_call | solution.py:334
  328.4 2.9 multiply_convert_fusion.2.do_ref
  331.3 19.7 %attention_bwd.1 = (bf16[1024,384]{1,0:T(8,128)(2,1)}, bf16[1024,384]{1,0:T(8,128)(2,1)}, bf16[1024,384]{1,0:T(8,128)(2,1)}, f32[3,2,1024]{2,1,0:T(2,128)}, f32[3,1024,2]{2,1,0:T(8,128)}) custom-call(bf16[1024,384]{1,0:T(8,128)(2,1)} %multiply_convert_fusion.4.q_ref, bf16[1024,384]{1,0:T(8,128)(2,1)} %get-tuple-element.65.k_ref, ...), custom_call_target="tpu_custom_call" | custom-call | flops 4026531840 | bytes 5505024 | tf_op jit(solution)/shard_map/attention_bwd/pallas_call | solution.py:146
  351.1 2.0 copy.69
  354.5 1.7 reduce-window.16
  357.2 1.0 copy.70
  359.2 4.4 convolution_convert_fusion.4
  365.8 2.0 fusion.28
  368.7 1.5 constant_dynamic-update-slice_fusion
  371.1 9.7 %convolution_convert_fusion = bf16[1536,1664]{1,0:T(8,128)(2,1)} fusion(bf16[1024,1536]{1,0:T(8,128)(2,1)S(1)} %copy-done.21, bf16[1024,1664]{1,0:T(8,128)(2,1)} %get-tuple-element.53), kind=kOutput, calls=%fused_computation | convolution fusion | flops 5237047296 | bytes 11665408 | tf_op jit(solution)/shard_map/dot_general | solution.py:18
  381.1 7.7 %convolution_convert_fusion.3 = bf16[1024,1536]{1,0:T(8,128)(2,1)} fusion(bf16[1024,1024]{1,0:T(8,128)(2,1)} %get-tuple-element.61.refs_0_, bf16[1024,1536]{1,0:T(8,128)(2,1)} %get-tuple-element.34), kind=kOutput, calls=%fused_computation.12 | convolution fusion | flops 3222798336 | bytes 8388608 | tf_op jit(solution)/shard_map/dot_general | solution.py:18
  388.9 11.4 %convolution_convert_fusion.1 = bf16[1536,2048]{1,0:T(8,128)(2,1)} fusion(bf16[1024,1536]{1,0:T(8,128)(2,1)} %get-tuple-element.43, bf16[1024,1024]{1,0:T(8,128)(2,1)} %copy-done.15, bf16[1024,1024]{1,0:T(8,128)(2,1)} %copy-done.14), kind=kOutput, calls=%fused_computation.1 | convolution fusion | flops 6453985280 | bytes 13631488 | tf_op jit(solution)/shard_map/dot_general | solution.py:18
  400.4 9.9 %all-gather = bf16[192,1536]{1,0:T(8,128)(2,1)S(1)} all-gather(bf16[48,1536]{1,0:T(8,128)(2,1)} %reduce-scatter.7.cloned.1.call-done), channel_id=2, replica_groups=mesh['seq'=4,'wshard'=8] {'seq'}, dimensions={0}, use_global_device_ids=true | all-gather | bytes 737280 | tf_op jit(solution)/shard_map/all_gather | solution.py:719
  410.3 1.2 bitcast_select_fusion
  411.4 4.3 all-to-all-start
  415.7 33.7 %product_scatter.5 = f32[256,1536]{1,0:T(8,128)} custom-call(bf16[1024,1024]{1,0:T(8,128)(2,1)} %get-tuple-element.61.refs_0_, bf16[1024,1536]{1,0:T(8,128)(2,1)} %all-gather.12.cloned.1.call-done.refs_1_), custom_call_target="tpu_custom_call" | custom-call | tf_op jit(solution)/shard_map/product_scatter/pallas_call | solution.py:417
  449.4 2.8 pad_maximum_fusion.1.refs_0_
  452.2 34.5 %product_scatter.7 = f32[256,1536]{1,0:T(8,128)} custom-call(bf16[1024,1280]{1,0:T(8,128)(2,1)} %pad_maximum_fusion.1.refs_0_, bf16[1024,384]{1,0:T(8,128)(2,1)} %get-tuple-element.54.refs_1_, bf16[1536,1280]{1,0:T(8,128)(2,1)} %all-gather.6.cloned.1.call-done.refs_2_, bf16[1536,384]{1,0:T(8,128)(2,1)} %all-gather.8.cloned.1.call-done.refs_3_), custom_call_target="tpu_custom_call" | custom-call | tf_op jit(solution)/shard_map/product_scatter/pallas_call | solution.py:417
  486.8 2.2 fusion.7
  489.0 41.3 %all-reduce.2 = (f32[1536]{0:T(1024)}, f32[24]{0:T(128)}, f32[1536]{0:T(1024)}) all-reduce(f32[1536]{0:T(1024)S(1)} %get-tuple-element.48, f32[24]{0:T(128)S(1)} %negate_dynamic-update-slice_fusion, f32[1536]{0:T(1024)S(1)} %get-tuple-element.46), channel_id=1, replica_groups=mesh['seq'=4,'wshard'=8] {'seq','wshard'}, use_global_device_ids=true, to_apply=%region_9.10 | all-reduce | flops 3096 | bytes 24768 | tf_op jit(solution)/shard_map/psum | solution.py:750
  530.3 4.7 fusion.13
  535.1 1.1 constant_dynamic-slice_fusion
  536.2 1.2 bitcast_convert_fusion
  537.3 24.7 %gather_square.2 = bf16[768,1664]{1,0:T(8,128)(2,1)} custom-call(bf16[192,1664]{1,0:T(8,128)(2,1)} %reduce-scatter.5.cloned.1.call-done.refs_0_), custom_call_target="tpu_custom_call" | custom-call | tf_op jit(solution)/shard_map/gather_square/pallas_call | solution.py:270
  563.0 2.1 convert_bitcast_fusion
  565.2 1.2 copy.84
  566.3 1.2 copy.85
  567.5 1.2 copy.86
  568.6 1.2 copy.87
  570.6 20.9 %reduce-scatter.9.cloned.1.call-done.refs_0_ = bf16[192,2048]{1,0:T(8,128)(2,1)} async-done(((bf16[1536,2048]{1,0:T(8,128)(2,1)}), bf16[192,2048]{1,0:T(8,128)(2,1)}) %reduce-scatter.9.cloned.1.call-update) | async-done | bytes 786448 | tf_op jit(solution)/shard_map/reduce_scatter | solution.py:553
  591.5 40.7 %gather_square.3 = (bf16[768,2048]{1,0:T(8,128)(2,1)}, bf16[512,1536]{1,0:T(8,128)(2,1)}) custom-call(bf16[192,2048]{1,0:T(8,128)(2,1)} %reduce-scatter.9.cloned.1.call-done.refs_0_, bf16[128,1536]{1,0:T(8,128)(2,1)} %reduce-scatter.11.cloned.1.call-done.refs_1_), custom_call_target="tpu_custom_call" | custom-call | tf_op jit(solution)/shard_map/gather_square/pallas_call | solution.py:270
  632.2 4.3 slice_convert_fusion
  637.2 3.7 copy.103
  640.9 5.0 reshape.200
  645.9 2.6 copy.94
  648.6 3.7 copy.102
  652.2 5.2 reshape.201
  657.4 2.1 convert_element_type.199
  (119 shorter events, 18.1 us)
Async XLA Ops:
  7.2 19.6 %copy-start = (bf16[512,1536]{1,0:T(8,128)(2,1)S(1)}, bf16[512,1536]{1,0:T(8,128)(2,1)}, u32[]{:S(2)}) copy-start(bf16[512,1536]{1,0:T(8,128)(2,1)} %param.28) | copy-start | bytes 4718596
  7.2 117.7 %all-gather.6.cloned.1.call-start = ((), (), s32[]{:S(2)}) async-start(), calls=%async_computation.5 | async-start | bytes 4423680 | tf_op jit(solution)/shard_map/all_gather | solution.py:549
  11.0 146.2 %all-gather.8.cloned.1.call-start = ((), (), s32[]{:S(2)}) async-start(), calls=%async_computation.6 | async-start | bytes 1327104 | tf_op jit(solution)/shard_map/all_gather | solution.py:549
  12.7 199.1 %all-gather.10.cloned.1.call-start = ((), (), s32[]{:S(2)}) async-start(), calls=%async_computation.7 | async-start | bytes 7077888 | tf_op jit(solution)/shard_map/all_gather | solution.py:549
  25.7 2.6 copy-start.4
  25.8 2.8 copy-start.22
  25.8 2.9 copy-start.5
  26.7 3.0 copy-start.20
  26.8 220.9 %all-gather.12.cloned.1.call-start = ((), (), s32[]{:S(2)}) async-start(), calls=%async_computation.8 | async-start | bytes 3538944 | tf_op jit(solution)/shard_map/all_gather | solution.py:549
  27.6 372.8 %reduce-scatter.7.cloned.1.call-start = ((), (), s32[]{:S(2)}) async-start(), calls=%async_computation.10 | async-start | bytes 1327104 | tf_op jit(solution)/shard_map/reduce_scatter | solution.py:553
  132.3 1.5 copy-start.9
  208.8 1.9 copy-start.19
  259.1 1.3 copy-start.14
  259.1 2.0 copy-start.15
  296.1 2.0 copy-start.2
  296.1 2.1 copy-start.6
  351.1 7.1 %copy-start.10 = (bf16[1024,384]{1,0:T(8,128)(2,1)S(1)}, bf16[1024,384]{1,0:T(8,128)(2,1)}, u32[]{:S(2)}) copy-start(bf16[1024,384]{1,0:T(8,128)(2,1)} %get-tuple-element.37) | copy-start | bytes 2359300
  351.1 8.1 %copy-start.17 = (bf16[1024,384]{1,0:T(8,128)(2,1)S(1)}, bf16[1024,384]{1,0:T(8,128)(2,1)}, u32[]{:S(2)}) copy-start(bf16[1024,384]{1,0:T(8,128)(2,1)} %get-tuple-element.74.refs_0_) | copy-start | bytes 2359300
  359.2 4.5 copy-start.11
  363.6 1.2 copy-start.12
  363.6 173.7 %reduce-scatter.5.cloned.1.call-start = ((), (), s32[]{:S(2)}) async-start(), calls=%async_computation.9 | async-start | bytes 5750784 | tf_op jit(solution)/shard_map/reduce_scatter | solution.py:553
  363.7 2.2 copy-start.13
  364.8 3.8 copy-start.7
  364.8 3.8 copy-start.8
  364.8 3.8 copy-start.18
  368.7 2.5 copy-start.21
  380.9 189.7 %reduce-scatter.11.cloned.1.call-start = ((), (), s32[]{:S(2)}) async-start(), calls=%async_computation.12 | async-start | bytes 3538944 | tf_op jit(solution)/shard_map/reduce_scatter | solution.py:553
  388.8 202.6 %reduce-scatter.9.cloned.1.call-start = ((), (), s32[]{:S(2)}) async-start(), calls=%async_computation.11 | async-start | bytes 7077888 | tf_op jit(solution)/shard_map/reduce_scatter | solution.py:553
  411.4 123.6 %all-to-all-start = ((bf16[8,48,1536]{2,1,0:T(8,128)(2,1)}), bf16[8,48,1536]{2,1,0:T(8,128)(2,1)}, u32[]{:S(2)}, u32[]{:S(2)}) async-start(bf16[8,48,1536]{2,1,0:T(8,128)(2,1)} %bitcast_select_fusion), calls=%async_computation.2 | async-start | bytes 2359296 | tf_op jit(solution)/shard_map/all_to_all | solution.py:724
  486.7 43.6 %copy-start.3 = (f32[256,1536]{1,0:T(8,128)S(1)}, f32[256,1536]{1,0:T(8,128)}, u32[]{:S(2)}) copy-start(f32[256,1536]{1,0:T(8,128)} %product_scatter.6) | copy-start | bytes 4718596
  652.2 5.2 copy-start.16
  657.4 2.1 copy-start.1
Sparse Core Ops, SparseCore 0:
  11.1 55.4 all-gather.5
  68.9 27.8 all-gather.7
  99.0 65.0 all-gather.9
  166.2 36.9 all-gather.11
  363.7 30.0 reduce-scatter.6
  396.0 75.3 reduce-scatter.4
  474.4 45.9 reduce-scatter.10
  522.8 68.6 reduce-scatter.8

commit v3 on v2

--- a/solution.py
+++ b/solution.py
@@ -347,8 +347,23 @@
     )(own, weight)
 
 
-def product_scatter(lefts, rights, transposed, collective_id):
+def transposed_product(left, right, out):
+    tall = 512 if out.shape[0] % 512 == 0 else 384
+    wide = 512 if out.shape[1] % 512 == 0 else 384
+    across = out.shape[1] // wide
+
+    def step(number, carry):
+        rows = pl.ds(pl.multiple_of((number // across) * tall, tall), tall)
+        columns = pl.ds(pl.multiple_of(lax.rem(number, across) * wide, wide), wide)
+        out[rows, columns] = product_tn(left[:, rows], right[:, columns]).astype(out.dtype)
+        return carry
+
+    lax.fori_loop(0, (out.shape[0] // tall) * across, step, 0)
+
+
+def product_scatter(lefts, rights, transposed, collective_id, extras=()):
     count = len(lefts)
+    more = len(extras)
     rows = lefts[0].shape[0] // 4
     half = rows // 2
     width = rights[0].shape[0] if transposed else rights[0].shape[1]
@@ -356,7 +371,10 @@
 
     def body(*refs):
         left, right = refs[:count], refs[count : 2 * count]
-        out, far, near, kept, land, carry, send, recv = refs[2 * count :]
+        sides_in = refs[2 * count : 2 * count + 2 * more]
+        out = refs[2 * count + 2 * more]
+        sides_out = refs[2 * count + 2 * more + 1 : 2 * count + 3 * more + 1]
+        far, near, kept, land, carry, send, recv = refs[2 * count + 3 * more + 1 :]
         me, side, down, across = sides()
         meet({"seq": side}, {"seq": down})
         to_side, to_down = {"seq": side}, {"seq": down}
@@ -403,6 +421,8 @@
         carry[1] = (kept[1] + land[1].astype(jnp.float32)).astype(carry.dtype)
         sixth = push(carry.at[1], land.at[5], send.at[5], recv.at[5], to_down)
         partial(me, store_own)
+        for index in range(more):
+            transposed_product(sides_in[2 * index], sides_in[2 * index + 1], sides_out[index])
         third.wait_recv()
         fourth.wait_recv()
         fifth.wait_recv()
@@ -416,9 +436,10 @@
     low = jnp.bfloat16
     return pl.pallas_call(
         body,
-        in_specs=[vmem] * (2 * count),
-        out_specs=vmem,
-        out_shape=jax.ShapeDtypeStruct((rows, width), jnp.float32),
+        in_specs=[vmem] * (2 * count + 2 * more),
+        out_specs=[vmem] * (1 + more),
+        out_shape=[jax.ShapeDtypeStruct((rows, width), jnp.float32)]
+        + [jax.ShapeDtypeStruct((a.shape[1], b.shape[1]), low) for a, b in extras],
         scratch_shapes=[
             pltpu.VMEM((rows, width), low),
             pltpu.VMEM((2, half, width), low),
@@ -432,117 +453,335 @@
             collective_id=collective_id, has_side_effects=True, vmem_limit_bytes=VMEM_LIMIT
         ),
         name="product_scatter",
-    )(*lefts, *rights)
-
-
-def gather_and_spread(values, block, collective_id):
-    count = len(values)
-    rows, width = block.shape
-
-    def body(*refs):
-        own, mine = refs[:count], refs[count]
-        full, whole = refs[count + 1 : 2 * count + 1], refs[2 * count + 1]
-        send, recv, local, line_send, line_recv = refs[2 * count + 2 :]
-        me, side, down, across = sides()
-        shards = lax.axis_size("wshard")
-        place = lax.axis_index("wshard")
-        chips = shards // 2
-        chip, core = place // 2, lax.rem(place, 2)
-        nexts = {"wshard": lax.rem(place + 2, shards)}
-        before = {"wshard": lax.rem(place + shards - 2, shards)}
-        twin = {"wshard": place + 1 - 2 * core}
-        meet({"seq": side}, {"seq": down}, nexts, before, twin)
-        jobs = [SquareGather(own[i], full[i], send.at[i], recv.at[i]) for i in range(count)]
-        mine_at = whole.at[core]
-
-        def along(index, device):
-            return pltpu.make_async_remote_copy(
-                src_ref=mine_at,
-                dst_ref=mine_at,
-                send_sem=line_send.at[index],
-                recv_sem=line_recv.at[0],
-                device_id=device,
-                device_id_type=MESH,
-            )
-
-        forth, back = along(0, nexts), along(1, before)
-        to_twin = pltpu.make_async_remote_copy(
-            src_ref=mine_at,
-            dst_ref=mine_at,
-            send_sem=line_send.at[2],
-            recv_sem=line_recv.at[1],
-            device_id=twin,
+    )(*lefts, *rights, *(value for pair in extras for value in pair))
+
+
+def line():
+    shards, place = lax.axis_size("wshard"), lax.axis_index("wshard")
+    chips = shards // 2
+    chip, core = place // 2, lax.rem(place, 2)
+    forth = {"wshard": lax.rem(place + 2, shards)}
+    back = {"wshard": lax.rem(place + shards - 2, shards)}
+    twin = {"wshard": place + 1 - 2 * core}
+    return chips, chip, core, forth, back, twin
+
+
+class LineGather:
+    def __init__(self, own, full, forth_send, back_send, twin_send, recv, local):
+        self.own, self.full, self.local = own, full, local
+        self.sends = (forth_send, back_send, twin_send)
+        self.recv = recv
+        self.rows = own.shape[0]
+        self.chips, self.chip, self.core, *self.devices = line()
+
+    def place(self, chip, core):
+        return self.full.at[pl.ds(pl.multiple_of((2 * chip + core) * self.rows, self.rows), self.rows)]
+
+    def copy(self, way, chip, source=None):
+        target = self.place(chip, self.core)
+        return pltpu.make_async_remote_copy(
+            src_ref=target if source is None else source,
+            dst_ref=target,
+            send_sem=self.sends[way].at[chip],
+            recv_sem=self.recv.at[2 * chip + self.core],
+            device_id=self.devices[way],
             device_id_type=MESH,
         )
-        goes_forth = (chip >= me) & (chip < chips - 1)
-        goes_back = (chip <= me) & (chip > 0)
-        jobs[0].start()
-
-        @pl.when(chip == me)
+
+    def wait_for(self, chip, core):
+        target = self.place(chip, core)
+        pltpu.make_async_remote_copy(
+            src_ref=target,
+            dst_ref=target,
+            send_sem=self.sends[2].at[0],
+            recv_sem=self.recv.at[2 * chip + core],
+            device_id=self.devices[2],
+            device_id_type=MESH,
+        ).wait_recv()
+
+    def start(self):
+        @pl.when(self.chip < self.chips - 1)
         def _():
-            whole[core] = mine[...]
-
-        @pl.when(chip != me)
+            self.copy(0, self.chip, self.own).start()
+
+        @pl.when(self.chip > 0)
         def _():
-            forth.wait_recv()
-
-        @pl.when(goes_forth)
+            self.copy(1, self.chip, self.own).start()
+
+        self.copy(2, self.chip, self.own).start()
+        self.keep = pltpu.make_async_copy(self.own, self.place(self.chip, self.core), self.local)
+        self.keep.start()
+
+    def step(self, number):
+        left, right = self.chip - number, self.chip + number
+
+        @pl.when(left >= 0)
         def _():
-            forth.start()
-
-        @pl.when(goes_back)
+            self.wait_for(left, self.core)
+
+            @pl.when(self.chip < self.chips - 1)
+            def _():
+                self.copy(0, left).start()
+
+            self.copy(2, left).start()
+
+        @pl.when(right < self.chips)
         def _():
-            back.start()
-
-        to_twin.start()
+            self.wait_for(right, self.core)
+
+            @pl.when(self.chip > 0)
+            def _():
+                self.copy(1, right).start()
+
+            self.copy(2, right).start()
+
+    def finish(self):
+        for chip in range(self.chips):
+            self.wait_for(chip, 1 - self.core)
+            self.copy(2, chip).wait_send()
+
+            @pl.when((chip <= self.chip) & (self.chip < self.chips - 1))
+            def _():
+                self.copy(0, chip).wait_send()
+
+            @pl.when((chip >= self.chip) & (self.chip > 0))
+            def _():
+                self.copy(1, chip).wait_send()
+
+        self.keep.wait()
+
+
+class LineSpread:
+    pieces = 4
+
+    def __init__(self, own, whole, send, recv):
+        self.own, self.whole, self.send, self.recv = own, whole, send, recv
+        self.rows = own.shape[0] // self.pieces
+        self.source = lax.axis_index("seq")
+        self.chips, self.chip, self.core, *self.devices = line()
+        self.goes = (
+            (self.chip >= self.source) & (self.chip < self.chips - 1),
+            (self.chip <= self.source) & (self.chip > 0),
+        )
+
+    def copy(self, way, piece):
+        target = self.whole.at[self.core, pl.ds(piece * self.rows, self.rows)]
+        return pltpu.make_async_remote_copy(
+            src_ref=target,
+            dst_ref=target,
+            send_sem=self.send.at[way, piece],
+            recv_sem=self.recv.at[way // 2, piece],
+            device_id=self.devices[way],
+            device_id_type=MESH,
+        )
+
+    def start(self):
+        @pl.when(self.chip == self.source)
+        def _():
+            self.whole[self.core] = self.own[...]
+
+    def step(self, piece):
+        @pl.when(self.chip != self.source)
+        def _():
+            self.copy(0, piece).wait_recv()
+
+        for way in (0, 1):
+
+            @pl.when(self.goes[way])
+            def _():
+                self.copy(way, piece).start()
+
+        self.copy(2, piece).start()
+
+    def finish(self):
+        for piece in range(self.pieces):
+            other = self.whole.at[1 - self.core, pl.ds(piece * self.rows, self.rows)]
+            pltpu.make_async_remote_copy(
+                src_ref=other,
+                dst_ref=other,
+                send_sem=self.send.at[2, piece],
+                recv_sem=self.recv.at[1, piece],
+                device_id=self.devices[2],
+                device_id_type=MESH,
+            ).wait_recv()
+            self.copy(2, piece).wait_send()
+            for way in (0, 1):
+
+                @pl.when(self.goes[way])
+                def _():
+                    self.copy(way, piece).wait_send()
+
+
+def first_gather(first, second, weights, block, collective_id):
+    rows, width = block.shape
+    shards = 2 * lax.axis_size("seq")
+    chips = shards // 2
+
+    def body(first_ref, second_ref, weights_ref, block_ref, first_full, second_full, weights_full, whole,
+             send, recv, local, line_send, line_recv, spread_send, spread_recv):
+        me, side, down, across = sides()
+        line_chips, chip, core, forth, back, twin = line()
+        meet({"seq": side}, {"seq": down}, forth, back, twin)
+        one = SquareGather(first_ref, first_full, send.at[0], recv.at[0])
+        two = SquareGather(second_ref, second_full, send.at[1], recv.at[1])
+        run = LineGather(
+            weights_ref, weights_full, line_send.at[0], line_send.at[1], line_send.at[2], line_recv, local.at[2]
+        )
+        spread = LineSpread(block_ref, whole, spread_send, spread_recv)
+        spread.start()
+        one.start()
+        run.start()
         keeps = []
-        for i, job in enumerate(jobs):
-            if i:
-                job.start()
-            size = own[i].shape[0]
+        for index, (own, full) in enumerate(((first_ref, first_full), (second_ref, second_full))):
+            size = own.shape[0]
             keep = pltpu.make_async_copy(
-                own[i], full[i].at[pl.ds(pl.multiple_of(me * size, size), size)], local.at[i]
+                own, full.at[pl.ds(pl.multiple_of(me * size, size), size)], local.at[index]
             )
             keep.start()
             keeps.append(keep)
-        for job in jobs:
-            job.relay()
-        for job, keep in zip(jobs, keeps):
+        two.start()
+        spread.step(0)
+        run.step(1)
+        one.relay()
+        spread.step(1)
+        run.step(2)
+        two.relay()
+        spread.step(2)
+        run.step(3)
+        spread.step(3)
+        for job, keep in zip((one, two), keeps):
             job.near()
             job.far()
             job.finish()
             keep.wait()
-        to_twin.wait_recv()
-        to_twin.wait_send()
-
-        @pl.when(goes_forth)
-        def _():
-            forth.wait_send()
-
-        @pl.when(goes_back)
-        def _():
-            back.wait_send()
+        run.finish()
+        spread.finish()
 
     vmem = pl.BlockSpec(memory_space=pltpu.VMEM)
     anywhere = pl.BlockSpec(memory_space=pl.ANY)
+    dma = pltpu.SemaphoreType.DMA
     return pl.pallas_call(
         body,
-        in_specs=[vmem] * (count + 1),
-        out_specs=[anywhere] * count + [vmem],
-        out_shape=[jax.ShapeDtypeStruct((4 * v.shape[0],) + v.shape[1:], v.dtype) for v in values]
-        + [jax.ShapeDtypeStruct((2, rows, width), block.dtype)],
+        in_specs=[vmem] * 4,
+        out_specs=[anywhere] * 3 + [vmem],
+        out_shape=[
+            jax.ShapeDtypeStruct((4 * first.shape[0],) + first.shape[1:], first.dtype),
+            jax.ShapeDtypeStruct((4 * second.shape[0],) + second.shape[1:], second.dtype),
+            jax.ShapeDtypeStruct((shards * weights.shape[0],) + weights.shape[1:], weights.dtype),
+            jax.ShapeDtypeStruct((2, rows, width), block.dtype),
+        ],
         scratch_shapes=[
-            pltpu.SemaphoreType.DMA((count, 6)),
-            pltpu.SemaphoreType.DMA((count, 6)),
-            pltpu.SemaphoreType.DMA((count,)),
-            pltpu.SemaphoreType.DMA((3,)),
-            pltpu.SemaphoreType.DMA((2,)),
+            dma((2, 6)),
+            dma((2, 6)),
+            dma((3,)),
+            dma((3, chips)),
+            dma((shards,)),
+            dma((3, LineSpread.pieces)),
+            dma((2, LineSpread.pieces)),
         ],
         compiler_params=pltpu.CompilerParams(
             collective_id=collective_id, has_side_effects=True, vmem_limit_bytes=VMEM_LIMIT
         ),
-        name="gather_and_spread",
-    )(*values, block)
+        name="first_gather",
+    )(first, second, weights, block)
+
+
+def add_everywhere(values, collective_id):
+    shape = values.shape
+    groups, shards = 4, 8
+
+    def body(values_ref, out, ranks, total, places, send, recv):
+        rank, place = lax.axis_index("seq"), lax.axis_index("wshard")
+        others = [{"seq": lax.rem(rank + k, groups)} for k in range(1, groups)]
+        along = [{"wshard": lax.rem(place + k, shards)} for k in range(1, shards)]
+        meet(*others, *along)
+        copies = [
+            push(values_ref, ranks.at[rank], send.at[k], recv.at[k], other) for k, other in enumerate(others)
+        ]
+        ranks[rank] = values_ref[...]
+        for copy in copies:
+            copy.wait()
+        total[...] = (ranks[0] + ranks[1]) + (ranks[2] + ranks[3])
+        copies = [
+            push(total, places.at[place], send.at[groups + k], recv.at[groups + k], other)
+            for k, other in enumerate(along)
+        ]
+        places[place] = total[...]
+        for copy in copies:
+            copy.wait()
+        sums = [places[k] + places[k + 1] for k in range(0, shards, 2)]
+        out[...] = (sums[0] + sums[1]) + (sums[2] + sums[3])
+
+    vmem = pl.BlockSpec(memory_space=pltpu.VMEM)
+    return pl.pallas_call(
+        body,
+        in_specs=[vmem],
+        out_specs=vmem,
+        out_shape=jax.ShapeDtypeStruct(shape, jnp.float32),
+        scratch_shapes=[
+            pltpu.VMEM((groups,) + shape, jnp.float32),
+            pltpu.VMEM(shape, jnp.float32),
+            pltpu.VMEM((shards,) + shape, jnp.float32),
+            pltpu.SemaphoreType.DMA((groups + shards,)),
+            pltpu.SemaphoreType.DMA((groups + shards,)),
+        ],
+        compiler_params=pltpu.CompilerParams(collective_id=collective_id, has_side_effects=True),
+        name="add_everywhere",
+    )(values)
+
+
+def join_units(every, down, part):
+    groups, rows, both = every.shape
+    units = both // 2
+    blocks = units // part
+    steps = 4
+    tall = rows // steps
+
+    def body(every_ref, down_ref, gate_ref, up_ref, down_out):
+        for half, out in enumerate((gate_ref, up_ref)):
+            for group in range(groups):
+                for block in range(blocks):
+                    at = half * units + block * part
+                    to = (block * groups + group) * part
+                    out[:, to : to + part] = every_ref[group, :, at : at + part].astype(jnp.float32)
+        down_out[...] = down_ref[...].astype(jnp.float32)
+
+    wide = jax.ShapeDtypeStruct((rows, groups * units), jnp.float32)
+    return pl.pallas_call(
+        body,
+        grid=(steps,),
+        in_specs=[
+            pl.BlockSpec((groups, tall, both), lambda i: (0, i, 0)),
+            pl.BlockSpec((down.shape[0] // steps, down.shape[1]), lambda i: (i, 0)),
+        ],
+        out_specs=[pl.BlockSpec((tall, groups * units), lambda i: (i, 0))] * 2
+        + [pl.BlockSpec((down.shape[0] // steps, down.shape[1]), lambda i: (i, 0))],
+        out_shape=[wide, wide, jax.ShapeDtypeStruct(down.shape, jnp.float32)],
+        name="join_units",
+    )(every, down)
+
+
+def join_columns(every, columns, starts):
+    groups, rows, lanes = every.shape
+    steps = 4
+    tall = rows // steps
+
+    def body(every_ref, *outs):
+        for start, out in zip(starts, outs):
+            for group in range(groups):
+                out[:, group * columns : (group + 1) * columns] = every_ref[
+                    group, :, start : start + columns
+                ].astype(jnp.float32)
+
+    wide = jax.ShapeDtypeStruct((rows, groups * columns), jnp.float32)
+    return pl.pallas_call(
+        body,
+        grid=(steps,),
+        in_specs=[pl.BlockSpec((groups, tall, lanes), lambda i: (0, i, 0))],
+        out_specs=[pl.BlockSpec((tall, groups * columns), lambda i: (i, 0))] * len(starts),
+        out_shape=[wide] * len(starts),
+        name="join_columns",
+    )(every)
 
 
 def gather(value, axis_name):
@@ -560,11 +799,14 @@
     return whole, product_nt(whole, weight) if transposed else product(whole, weight)
 
 
-def multiply_scatter(lefts, rights, transposed, collective_id):
+def multiply_scatter(lefts, rights, transposed, collective_id, extras=()):
     if square(lax.axis_size("seq")):
-        return product_scatter(lefts, rights, transposed, collective_id)
+        summed, *products = product_scatter(lefts, rights, transposed, collective_id, extras)
+        return (summed, *products) if extras else summed
+    products = [product_tn(a, b).astype(jnp.bfloat16) for a, b in extras]
     total = sum(product_nt(a, b) if transposed else product(a, b) for a, b in zip(lefts, rights))
-    return scatter(total.astype(jnp.bfloat16), "seq").astype(jnp.float32)
+    summed = scatter(total.astype(jnp.bfloat16), "seq").astype(jnp.float32)
+    return (summed, *products) if extras else summed
 
 
 def on_device(
@@ -621,19 +863,23 @@
         [own_columns(w_query), own_columns(w_key), own_columns(w_value), own_forget],
         axis=1,
     )
-    mine_ffn = jnp.concatenate([own_units(w_gate), own_units(w_up)], axis=1)
-    mine_down = lax.dynamic_slice_in_dim(w_down, seq_rank * part, part, 0)
     fast = square(groups) and shards == 2 * groups
-    full_attn = gather(mine_attn, "wshard")
-    full_ogate = gather(own_columns(w_ogate), "wshard")
     normed_attn_own = rms_norm(inputs, norm_attn).astype(low)
     if fast:
-        normed_attn, cotangent_all, full_out = gather_and_spread([normed_attn_own, cotangent_low], w_out, 0)
+        normed_attn, cotangent_all, full_attn, full_out = first_gather(
+            normed_attn_own, cotangent_low, mine_attn, w_out, 0
+        )
         full_out = full_out.reshape(columns, width)
+        later = lax.optimization_barrier((full_out, w_ogate, w_gate, w_up, w_down))
+        full_out, w_ogate, w_gate, w_up, w_down = later
     else:
+        full_attn = gather(mine_attn, "wshard")
         normed_attn = gather(normed_attn_own, "seq")
         cotangent_all = gather(cotangent_low, "seq")
         full_out = lax.dynamic_slice_in_dim(gather(w_out, "wshard"), seq_rank * columns, columns, 0)
+    full_ogate = gather(own_columns(w_ogate), "wshard")
+    mine_ffn = jnp.concatenate([own_units(w_gate), own_units(w_up)], axis=1)
+    mine_down = lax.dynamic_slice_in_dim(w_down, seq_rank * part, part, 0)
     full_ffn = gather(mine_ffn, "wshard")
     full_down = gather(mine_down, "wshard")
 
@@ -672,12 +918,12 @@
     hidden_full, pull_swiglu = jax.vjp(swiglu, gate_up[:, :units], gate_up[:, units:])
     hidden = hidden_full.astype(low)
 
-    grad_w_down = product_tn(hidden, cotangent_all).astype(low)
     grad_hidden = product_nt(cotangent_all, full_down)
     grad_gate_full, grad_up_full = pull_swiglu(grad_hidden)
     grad_gate_up = jnp.concatenate([grad_gate_full.astype(low), grad_up_full.astype(low)], axis=1)
-    grad_w_ffn = product_tn(normed_ffn, grad_gate_up).astype(low)
-    grad_normed_ffn = multiply_scatter([grad_gate_up], [full_ffn], True, 3)
+    grad_normed_ffn, grad_w_down, grad_w_ffn = multiply_scatter(
+        [grad_gate_up], [full_ffn], True, 3, [(hidden, cotangent_all), (normed_ffn, grad_gate_up)]
+    )
     share_down = scatter(grad_w_down, "wshard")
     share_ffn = scatter(grad_w_ffn, "wshard")
     grad_middle_part, grad_norm_ffn = pull_ffn_norm(grad_normed_ffn)
@@ -734,34 +980,42 @@
         every_ffn, grad_down, every_attn = [gather(v, "seq") for v in (share_ffn, share_down, share_attn)]
     every_ffn = every_ffn.reshape((groups,) + share_ffn.shape)
     every_attn = every_attn.reshape((groups,) + share_attn.shape)
-    grad_down = grad_down.astype(jnp.float32)
-
-    def join(first):
-        taken = every_attn[:, :, first : first + columns]
-        return taken.transpose(1, 0, 2).reshape(rows, width).astype(jnp.float32)
-
-    def join_units(first):
-        taken = every_ffn[:, :, first * units : (first + 1) * units]
-        taken = taken.reshape(groups, rows, shards, part).transpose(1, 2, 0, 3)
-        return taken.reshape(rows, hidden_size).astype(jnp.float32)
+    if fast:
+        grad_w_gate, grad_w_up, grad_down = join_units(every_ffn, grad_down, part)
+        grads = join_columns(every_attn, columns, (0, columns, 2 * columns, front))
+        vector = jnp.concatenate([grad_norm_attn, grad_norm_ffn, grad_bias])
+        vector = jnp.pad(vector, (0, -vector.shape[0] % 1024)).reshape(-1, 128)
+        vector = add_everywhere(vector, 9).reshape(-1)
+        small = vector[:width], vector[width : 2 * width], vector[2 * width : 2 * width + heads]
+    else:
+
+        def join(first):
+            taken = every_attn[:, :, first : first + columns]
+            return taken.transpose(1, 0, 2).reshape(rows, width).astype(jnp.float32)
+
+        def join_own_units(first):
+            taken = every_ffn[:, :, first * units : (first + 1) * units]
+            taken = taken.reshape(groups, rows, shards, part).transpose(1, 2, 0, 3)
+            return taken.reshape(rows, hidden_size).astype(jnp.float32)
+
+        grads = [join(first) for first in (0, columns, 2 * columns, front)]
+        grad_w_gate, grad_w_up = join_own_units(0), join_own_units(1)
+        grad_down = grad_down.astype(jnp.float32)
+        small = lax.psum((grad_norm_attn, grad_norm_ffn, grad_bias), ("seq", "wshard"))
 
     grad_forget_w = every_attn[:, :, 3 * columns : 3 * columns + local_heads]
     grad_forget_w = grad_forget_w.transpose(1, 0, 2).reshape(rows, heads).astype(jnp.float32)
-    small = lax.psum((grad_norm_attn, grad_norm_ffn, grad_bias), ("seq", "wshard"))
     return (
         layer_output,
         grad_input,
         small[0],
-        join(0),
-        join(columns),
-        join(2 * columns),
-        join(front),
+        *grads,
         grad_forget_w,
         small[2],
         grad_out,
         small[1],
-        join_units(0),
-        join_units(1),
+        grad_w_gate,
+        grad_w_up,
         grad_down,
     )
 

time: 674 us -> 605 us (0.90)
  blocking collectives: 51.2 us -> 10.3 us
  waiting for transfers between devices: 21.1 us -> 53.9 us
  local copies, waits for them, and re-layouts: 65.8 us -> 34.4 us
  matrix products: 57.8 us -> 37 us
    psum x1 -> x0, blocking collectives: 41.3 us -> none  [on_device(): lax.psum((grad_norm_attn, grad_norm_ffn, grad_bias), ('seq', 'wshard'))]
    reduce_scatter x4, waiting for transfers between devices: 20.9 us -> 52.2 us  [scatter(): return lax.psum_scatter(value, axis_name, scatter_dimension=0, tiled=True)]
    convert_element_type x8 -> x0, local copies, waits for them, and re-layouts: 22.2 us -> none  [the longest x4 17.6 us: join_units(): return taken.reshape(rows, hidden_size).astype(jnp.float32)]
    dot_general x4 -> x2, matrix products: 33.1 us -> 12.4 us  [product_tn(): lax.dot_general(left, right, (((0,), (0,)), ((), ())), preferred_element_...]
    pallas_call x5 -> x8, Pallas kernels: 241 us -> 231 us  [the longest x4 147 us: product_scatter(): pl.pallas_call(body, in_specs=[vmem] * (2 * count + 2 * more), out_specs=...]
    unnamed x58 -> x55, local copies, waits for them, and re-layouts: 12.3 us -> 5.44 us
  transfers between devices with their start and end apart: 9 -> 8, of which waited for: 1 -> 2; matrix products, arithmetic and copies ran while one was open for 15% -> 13% of each run, Pallas kernels for 42% -> 36%
where the time goes in v3:
time: 605 us; the launch traced here: 597 us
  Pallas kernels  401 us (66%)
  waiting for transfers between devices  53.9 us (9%)
  other arithmetic  39.9 us (7%)
  matrix products  37 us (6%)
  local copies, waits for them, and re-layouts  34.4 us (6%)
  between operations  15.9 us (3%)
  blocking collectives  10.3 us (2%)
    pallas_call x4, Pallas kernels, product_scatter(): pl.pallas_call(body, in_specs=[vmem] * (2 * count + 2 * more), out_specs=...  147 us
    pallas_call x2, Pallas kernels, gather_product(): pl.pallas_call(body, in_specs=[vmem, vmem], out_specs=[vmem, vmem], out_s...  71.4 us
    pallas_call x2, Pallas kernels, gather_square(): pl.pallas_call(body, in_specs=[pl.BlockSpec(memory_space=pltpu.VMEM)] * c...  64.6 us
    pallas_call x1, Pallas kernels, first_gather(): pl.pallas_call(body, in_specs=[vmem] * 4, out_specs=[anywhere] * 3 + [vme...  61 us
    reduce_scatter x4, waiting for transfers between devices, scatter(): return lax.psum_scatter(value, axis_name, scatter_dimension=0, tiled=True)  52.2 us
    pallas_call x1, Pallas kernels, attention_bwd(): pl.pallas_call(body, grid=(pairs,), in_specs=[lane, lane, lane, lane, row...  19.8 us
    pallas_call x1, Pallas kernels, attention_fwd(): pl.pallas_call(body, grid=(pairs,), in_specs=[lane, lane, lane, row, col]...  13.6 us
    dot_general x2, matrix products, product(): return jnp.dot(left, right, preferred_element_type=jnp.float32)  13.2 us
  transfers between devices with their start and end apart: 8, of which 2 were waited for; matrix products, arithmetic and copies ran while one was open for 13% of the time, Pallas kernels for 36%

profile of v3, /device:TPU:0, one launch (start us, length us, event | category | flops | bytes accessed | tf_op | source)
XLA Modules:
  0.0 597.5 jit_solution(13447597206494493307)
XLA Ops:
  8.1 1.4 fusion.14
  9.5 0.7 constant_dynamic-slice_fusion.3
  10.4 0.9 constant_dynamic-slice_fusion.6
  11.4 1.0 constant_dynamic-slice_fusion.4
  12.4 1.1 fusion.6.first_ref
  13.5 1.0 bitcast_select_fusion.1.second_ref
  14.5 0.8 fusion.22.weights_ref
  15.4 61.0 %first_gather.1 = (bf16[1024,1536]{1,0:T(8,128)(2,1)}, bf16[1024,1536]{1,0:T(8,128)(2,1)}, bf16[1536,1280]{1,0:T(8,128)(2,1)}, bf16[2,192,1536]{2,1,0:T(8,128)(2,1)}) custom-call(bf16[256,1536]{1,0:T(8,128)(2,1)} %fusion.6.first_ref, bf16[256,1536]{1,0:T(8,128)(2,1)} %bitcast_select_fusion.1.second_ref, bf16[192,1280]{1,0:T(8,128)(2,1)} %fusion.22.weights_ref, ...), custom_call_target="tpu_custom_call" | custom-call | tf_op jit(solution)/shard_map/first_gather/pallas_call | solution.py:663
  76.4 1.6 constant_dynamic-slice_fusion.2
  78.1 2.8 reshape.166
  80.9 2.3 dynamic-slice_reduce_fusion.1
  83.3 2.8 reshape.168
  86.2 2.3 dynamic-slice_reduce_fusion
  88.6 0.9 pad_maximum_fusion.2
  89.7 0.8 constant_dynamic-slice_fusion.1
  91.1 7.3 %convolution_convert_fusion.1 = bf16[1024,1280]{1,0:T(8,128)(2,1)S(1)} fusion(bf16[1024,1536]{1,0:T(8,128)(2,1)} %get-tuple-element.46, bf16[1536,1280]{1,0:T(8,128)(2,1)} %get-tuple-element.47.refs_2_), kind=kOutput, calls=%fused_computation.10 | convolution fusion | flops 4027842560 | bytes 9699328 | tf_op jit(solution)/shard_map/dot_general | solution.py:14
  98.4 1.5 copy-done.8
  100.4 1.7 reduce-window.14
  103.3 1.7 copy.50
  105.0 2.2 multiply_convert_fusion.4.q_ref
  107.1 2.7 fusion.31
  109.8 13.6 %attention_fwd.1 = (bf16[1024,384]{1,0:T(8,128)(2,1)}, f32[3,2,1024]{2,1,0:T(2,128)}) custom-call(bf16[1024,384]{1,0:T(8,128)(2,1)} %multiply_convert_fusion.4.q_ref, bf16[1024,384]{1,0:T(8,128)(2,1)} %get-tuple-element.92.k_ref, bf16[1024,384]{1,0:T(8,128)(2,1)} %get-tuple-element.91.v_ref, f32[3,2,1024]{2,1,0:T(2,128)} %reduce_window_sum.30.row_ref, ...), custom_call_target="tpu_custom_call" | custom-call | flops 1610612736 | bytes 3145728 | tf_op jit(solution)/shard_map/attention_fwd/pallas_call | solution.py:76
  123.4 5.9 fusion.8
  129.3 34.5 %product_scatter.4 = f32[256,1536]{1,0:T(8,128)} custom-call(bf16[1024,384]{1,0:T(8,128)(2,1)} %get-tuple-element.99.refs_0_, bf16[384,1536]{1,0:T(8,128)(2,1)} %bitcast.97), custom_call_target="tpu_custom_call" | custom-call | tf_op jit(solution)/shard_map/product_scatter/pallas_call | solution.py:437
  163.8 1.9 multiply_reduce_fusion.2
  165.7 1.1 multiply_convert_fusion.3.own_ref
  167.2 39.0 %gather_product.2 = (bf16[1024,1536]{1,0:T(8,128)(2,1)}, f32[1024,2048]{1,0:T(8,128)}) custom-call(bf16[256,1536]{1,0:T(8,128)(2,1)} %multiply_convert_fusion.3.own_ref, bf16[1536,2048]{1,0:T(8,128)(2,1)} %all-gather.7.cloned.1.call-done.weight_ref.refs_1_), custom_call_target="tpu_custom_call" | custom-call | tf_op jit(solution)/shard_map/gather_product/pallas_call | solution.py:334
  206.3 11.4 %fusion.2 = (bf16[1024,1024]{1,0:T(8,128)(2,1)S(1)}, bf16[1024,1024]{1,0:T(8,128)(2,1)S(1)}, bf16[1024,1024]{1,0:T(8,128)(2,1)}) fusion(f32[1024,2048]{1,0:T(8,128)} %get-tuple-element.54, bf16[1024,1536]{1,0:T(8,128)(2,1)} %get-tuple-element.56.refs_3_, bf16[1024,1536]{1,0:T(8,128)(2,1)} %all-gather.9.cloned.1.call-done.refs_1_), kind=kOutput, calls=%fused_computation.4 | convolution fusion | flops 3238002688 | bytes 20971520 | tf_op jit(solution)/shard_map/dot_general | solution.py:24
  217.7 2.4 pad_maximum_fusion.refs_0_.refs_5_
  220.1 42.8 %product_scatter.6 = (f32[256,1536]{1,0:T(8,128)}, bf16[1024,1536]{1,0:T(8,128)(2,1)}, bf16[1536,2048]{1,0:T(8,128)(2,1)}) custom-call(bf16[1024,2048]{1,0:T(8,128)(2,1)} %pad_maximum_fusion.refs_0_.refs_5_, bf16[1536,2048]{1,0:T(8,128)(2,1)} %all-gather.7.cloned.1.call-done.weight_ref.refs_1_, bf16[1024,1024]{1,0:T(8,128)(2,1)} %get-tuple-element.90.refs_0_.refs_2_, ...), custom_call_target="tpu_custom_call" | custom-call | tf_op jit(solution)/shard_map/product_scatter/pallas_call | solution.py:437
  262.9 1.9 multiply_reduce_fusion
  265.0 1.4 fusion.27.own_ref
  266.4 32.4 %gather_product.3 = (bf16[1024,1536]{1,0:T(8,128)(2,1)}, f32[1024,384]{1,0:T(8,128)}) custom-call(bf16[256,1536]{1,0:T(8,128)(2,1)} %fusion.27.own_ref, bf16[384,1536]{1,0:T(8,128)(2,1)} %bitcast.98), custom_call_target="tpu_custom_call" | custom-call | tf_op jit(solution)/shard_map/gather_product/pallas_call | solution.py:334
  298.8 4.7 convolution_convert_fusion.2
  303.5 2.4 multiply_convert_fusion.2.do_ref
  306.0 19.8 %attention_bwd.1 = (bf16[1024,384]{1,0:T(8,128)(2,1)}, bf16[1024,384]{1,0:T(8,128)(2,1)}, bf16[1024,384]{1,0:T(8,128)(2,1)}, f32[3,2,1024]{2,1,0:T(2,128)}, f32[3,1024,2]{2,1,0:T(8,128)}) custom-call(bf16[1024,384]{1,0:T(8,128)(2,1)} %multiply_convert_fusion.4.q_ref, bf16[1024,384]{1,0:T(8,128)(2,1)} %get-tuple-element.92.k_ref, ...), custom_call_target="tpu_custom_call" | custom-call | flops 4026531840 | bytes 5505024 | tf_op jit(solution)/shard_map/attention_bwd/pallas_call | solution.py:146
  325.8 1.9 copy.56
  328.4 1.7 reduce-window.16
  331.0 1.0 copy.57
  332.1 1.3 constant_dynamic-update-slice_fusion.4
  333.9 0.7 copy-done.13
  334.6 1.6 fusion.29
  336.4 1.3 constant_dynamic-update-slice_fusion
  337.7 0.9 copy-done.21
  338.5 7.7 %convolution_convert_fusion = bf16[1536,1664]{1,0:T(8,128)(2,1)} fusion(bf16[1024,1536]{1,0:T(8,128)(2,1)S(1)} %copy-done.21, bf16[1024,1664]{1,0:T(8,128)(2,1)S(1)} %get-tuple-element.82), kind=kOutput, calls=%fused_computation | convolution fusion | flops 5237047296 | bytes 11665408 | tf_op jit(solution)/shard_map/dot_general | solution.py:18
  346.9 0.7 reduce-scatter.9.cloned.1.call-update
  347.8 10.3 %all-gather = bf16[192,1536]{1,0:T(8,128)(2,1)S(1)} all-gather(bf16[48,1536]{1,0:T(8,128)(2,1)} %reduce-scatter.7.cloned.1.call-done), channel_id=2, replica_groups=mesh['seq'=4,'wshard'=8] {'seq'}, dimensions={0}, use_global_device_ids=true | all-gather | bytes 737280 | tf_op jit(solution)/shard_map/all_gather | solution.py:965
  358.1 1.2 bitcast_select_fusion
  359.3 4.6 all-to-all-start
  363.9 2.6 pad_maximum_fusion.1.refs_0_
  366.5 35.3 %product_scatter.7 = f32[256,1536]{1,0:T(8,128)} custom-call(bf16[1024,1280]{1,0:T(8,128)(2,1)} %pad_maximum_fusion.1.refs_0_, bf16[1024,384]{1,0:T(8,128)(2,1)} %get-tuple-element.83.refs_1_, bf16[1536,1280]{1,0:T(8,128)(2,1)} %get-tuple-element.47.refs_2_, bf16[1536,384]{1,0:T(8,128)(2,1)} %all-gather.5.cloned.1.call-done.refs_3_), custom_call_target="tpu_custom_call" | custom-call | tf_op jit(solution)/shard_map/product_scatter/pallas_call | solution.py:437
  402.0 2.1 fusion.7
  404.7 12.5 %add_everywhere.1 = f32[32,128]{1,0:T(8,128)} custom-call(f32[32,128]{1,0:T(8,128)} %fusion.24.values_ref), custom_call_target="tpu_custom_call" | custom-call | tf_op jit(solution)/shard_map/add_everywhere/pallas_call | solution.py:716
  417.2 1.2 slice.77
  418.4 34.1 %product_scatter.5 = f32[256,1536]{1,0:T(8,128)} custom-call(bf16[1024,1024]{1,0:T(8,128)(2,1)} %get-tuple-element.90.refs_0_.refs_2_, bf16[1024,1536]{1,0:T(8,128)(2,1)} %all-gather.9.cloned.1.call-done.refs_1_), custom_call_target="tpu_custom_call" | custom-call | tf_op jit(solution)/shard_map/product_scatter/pallas_call | solution.py:437
  453.1 5.2 fusion.13
  458.3 1.1 constant_dynamic-slice_fusion
  459.5 1.2 bitcast_convert_fusion
  460.7 23.9 %gather_square.2 = bf16[768,1664]{1,0:T(8,128)(2,1)} custom-call(bf16[192,1664]{1,0:T(8,128)(2,1)} %reduce-scatter.5.cloned.1.call-done.refs_0_), custom_call_target="tpu_custom_call" | custom-call | tf_op jit(solution)/shard_map/gather_square/pallas_call | solution.py:270
  484.6 4.4 join_columns.1
  489.0 1.0 convert_bitcast_fusion
  490.7 52.2 %reduce-scatter.9.cloned.1.call-done.refs_0_ = bf16[192,2048]{1,0:T(8,128)(2,1)} async-done(((bf16[1536,2048]{1,0:T(8,128)(2,1)}), bf16[192,2048]{1,0:T(8,128)(2,1)}) %reduce-scatter.9.cloned.1.call-update) | async-done | bytes 786448 | tf_op jit(solution)/shard_map/reduce_scatter | solution.py:792
  542.9 40.7 %gather_square.3 = (bf16[768,2048]{1,0:T(8,128)(2,1)}, bf16[512,1536]{1,0:T(8,128)(2,1)}) custom-call(bf16[192,2048]{1,0:T(8,128)(2,1)} %reduce-scatter.9.cloned.1.call-done.refs_0_, bf16[128,1536]{1,0:T(8,128)(2,1)} %reduce-scatter.11.cloned.1.call-done.refs_1_), custom_call_target="tpu_custom_call" | custom-call | tf_op jit(solution)/shard_map/gather_square/pallas_call | solution.py:270
  583.7 6.5 %join_units.1 = (f32[192,4096]{1,0:T(8,128)}, f32[192,4096]{1,0:T(8,128)}, f32[512,1536]{1,0:T(8,128)}) custom-call(bf16[4,192,2048]{2,1,0:T(8,128)(2,1)} %bitcast.99, bf16[512,1536]{1,0:T(8,128)(2,1)} %get-tuple-element.74.down_ref), custom_call_target="tpu_custom_call" | custom-call | tf_op jit(solution)/shard_map/join_units/pallas_call | solution.py:750
  (106 shorter events, 8.6 us)
Async XLA Ops:
  7.2 82.5 %copy-start = (bf16[512,1536]{1,0:T(8,128)(2,1)S(1)}, bf16[512,1536]{1,0:T(8,128)(2,1)}, u32[]{:S(2)}) copy-start(bf16[512,1536]{1,0:T(8,128)(2,1)} %param.28) | copy-start | bytes 4718596
  7.2 5.2 copy-start.2
  7.2 5.2 copy-start.16
  7.2 116.2 %all-gather.5.cloned.1.call-start = ((), (), s32[]{:S(2)}) async-start(), calls=%async_computation.5 | async-start | bytes 1327104 | tf_op jit(solution)/shard_map/all_gather | solution.py:788
  8.1 5.5 copy-start.4
  10.4 4.1 copy-start.19
  78.0 89.2 %all-gather.7.cloned.1.call-start = ((), (), s32[]{:S(2)}) async-start(), calls=%async_computation.6 | async-start | bytes 7077888 | tf_op jit(solution)/shard_map/all_gather | solution.py:788
  88.6 2.4 copy-start.22
  89.6 116.7 %all-gather.9.cloned.1.call-start = ((), (), s32[]{:S(2)}) async-start(), calls=%async_computation.7 | async-start | bytes 3538944 | tf_op jit(solution)/shard_map/all_gather | solution.py:788
  90.5 257.3 %reduce-scatter.7.cloned.1.call-start = ((), (), s32[]{:S(2)}) async-start(), calls=%async_computation.9 | async-start | bytes 1327104 | tf_op jit(solution)/shard_map/reduce_scatter | solution.py:792
  98.4 1.5 copy-start.8
  163.8 1.9 copy-start.15
  262.9 2.0 copy-start.3
  262.9 2.1 copy-start.5
  262.9 2.1 copy-start.20
  298.8 4.8 copy-start.6
  303.5 157.2 %reduce-scatter.5.cloned.1.call-start = ((), (), s32[]{:S(2)}) async-start(), calls=%async_computation.8 | async-start | bytes 5750784 | tf_op jit(solution)/shard_map/reduce_scatter | solution.py:792
  325.8 1.9 copy-start.18
  332.1 1.4 copy-start.10
  332.1 1.6 copy-start.12
  333.5 1.1 copy-start.13
  334.6 1.8 copy-start.7
  334.6 1.8 copy-start.14
  336.4 2.2 copy-start.21
  346.3 144.5 %reduce-scatter.11.cloned.1.call-start = ((), (), s32[]{:S(2)}) async-start(), calls=%async_computation.11 | async-start | bytes 3538944 | tf_op jit(solution)/shard_map/reduce_scatter | solution.py:792
  346.9 196.1 %reduce-scatter.9.cloned.1.call-start = ((), (), s32[]{:S(2)}) async-start(), calls=%async_computation.10 | async-start | bytes 7077888 | tf_op jit(solution)/shard_map/reduce_scatter | solution.py:792
  359.3 4.7 copy-start.9
  359.3 4.7 copy-start.11
  359.3 99.1 %all-to-all-start = ((bf16[8,48,1536]{2,1,0:T(8,128)(2,1)}), bf16[8,48,1536]{2,1,0:T(8,128)(2,1)}, u32[]{:S(2)}, u32[]{:S(2)}) async-start(bf16[8,48,1536]{2,1,0:T(8,128)(2,1)} %bitcast_select_fusion), calls=%async_computation.2 | async-start | bytes 2359296 | tf_op jit(solution)/shard_map/all_to_all | solution.py:970
  418.4 34.1 %copy-start.17 = (f32[32,128]{1,0:T(8,128)S(1)}, f32[32,128]{1,0:T(8,128)}, u32[]{:S(2)}) copy-start(f32[32,128]{1,0:T(8,128)} %add_everywhere.1) | copy-start | bytes 49156
  583.6 6.6 %copy-start.1 = (bf16[512,1536]{1,0:T(8,128)(2,1)S(1)}, bf16[512,1536]{1,0:T(8,128)(2,1)}, u32[]{:S(2)}) copy-start(bf16[512,1536]{1,0:T(8,128)(2,1)} %param.28) | copy-start | bytes 4718596
Sparse Core Ops, SparseCore 0:
  78.2 22.2 all-gather.4
  102.7 64.5 all-gather.6
  168.9 36.9 all-gather.8
  303.6 30.7 reduce-scatter.6
  346.4 77.2 reduce-scatter.4
  426.0 45.5 reduce-scatter.10
  474.0 68.9 reduce-scatter.8

commit v4 on v3

--- a/solution.py
+++ b/solution.py
@@ -38,89 +38,156 @@
     return jax.nn.silu(gate) * upward
 
 
-def attention_fwd(q, k, v, cum_row, key_col, heads_half):
-    slots, width = q.shape
-    pairs = width // PAIR
+def low_triangle(size):
+    rows = lax.broadcasted_iota(jnp.int32, (size, size), 0)
+    return rows <= lax.broadcasted_iota(jnp.int32, (size, size), 1)
+
+
+def exact(left, right):
+    return jnp.dot(left, right, precision=lax.Precision.HIGHEST, preferred_element_type=jnp.float32)
+
+
+def attention_fwd(joined, bias, length, head_size, scale):
+    slots = joined.shape[0]
+    pairs = (joined.shape[1] // PAIR - 1) // 3
     tile = min(256, slots)
-    half = heads_half
-
-    def body(q_ref, k_ref, v_ref, row_ref, col_ref, o_ref, lse_ref):
+    some = 8
+
+    def body(length_ref, q_ref, k_ref, v_ref, f_ref, bias_ref, o_ref, offset_ref, col_ref, logit_ref, row):
+        pair = pl.program_id(0)
+
+        @pl.when(pair == 0)
+        def _():
+            logits = f_ref[...].astype(jnp.float32) + bias_ref[...]
+            logit_rows = logits.T[:some]
+            logit_ref[...] = logit_rows
+            logs = jnp.minimum(logit_rows, 0.0) - jnp.log1p(jnp.exp(-jnp.abs(logit_rows)))
+            ones = low_triangle(tile).astype(jnp.float32)
+            carry = jnp.zeros((some, 1), jnp.float32)
+            for first in range(0, slots, tile):
+                sums = exact(logs[:, first : first + tile], ones) + carry
+                row[:, first : first + tile] = sums
+                carry = sums[:, tile - 1 : tile]
+            wide = jnp.concatenate([row[...], jnp.zeros((PAIR - some, slots), jnp.float32)], axis=0).T
+            usable = lax.broadcasted_iota(jnp.int32, (slots, PAIR), 0) < length_ref[0]
+            col_ref[...] = jnp.where(usable, wide, -NEG_FILL)
+
         key_all = k_ref[...]
         value_t = v_ref[...].T
-        query_t = q_ref[...].T
+        query_t = (q_ref[...].astype(jnp.float32) * scale).astype(jnp.bfloat16).T
         sub = lax.broadcasted_iota(jnp.int32, (PAIR, tile), 0)
-        diag = lax.broadcasted_iota(jnp.int32, (tile, tile), 0) <= lax.broadcasted_iota(
-            jnp.int32, (tile, tile), 1
-        )
+        lanes = lax.broadcasted_iota(jnp.int32, (slots, PAIR), 1)
+        diag = low_triangle(tile)
+        columns = [
+            jnp.sum(jnp.where(lanes == 2 * pair + a, col_ref[...], 0.0), axis=1, keepdims=True) for a in range(2)
+        ]
         for number in range(slots // tile):
             first, last = number * tile, (number + 1) * tile
             outs = []
             for a in range(2):
-                mine = (sub >= a * half) & (sub < (a + 1) * half)
+                mine = (sub >= a * head_size) & (sub < (a + 1) * head_size)
                 query = jnp.where(mine, query_t[:, first:last], jnp.zeros((), query_t.dtype))
                 scores = product(key_all[:last], query)
-                scores = scores + (row_ref[0, a : a + 1, first:last] - col_ref[0, :last, a : a + 1])
+                own_row = row[pl.ds(2 * pair + a, 1), first:last]
+                scores = scores + (own_row - columns[a][:last])
                 tail = jnp.where(diag, scores[first:], NEG_FILL)
                 scores = tail if number == 0 else jnp.concatenate([scores[:first], tail], axis=0)
                 top = jnp.max(scores, axis=0, keepdims=True)
                 weights = jnp.exp(scores - top)
                 total = jnp.sum(weights, axis=0, keepdims=True)
-                mixed = product(value_t[a * half : (a + 1) * half, :last], weights.astype(jnp.bfloat16))
+                mixed = product(
+                    value_t[a * head_size : (a + 1) * head_size, :last], weights.astype(jnp.bfloat16)
+                )
                 outs.append(mixed / total)
-                lse_ref[0, a : a + 1, first:last] = top + jnp.log(total)
+                offset_ref[pl.ds(2 * pair + a, 1), first:last] = own_row - (top + jnp.log(total))
             o_ref[first:last, :] = jnp.concatenate(outs, axis=0).T.astype(o_ref.dtype)
 
-    lane = pl.BlockSpec((slots, PAIR), lambda p: (0, p))
-    row = pl.BlockSpec((1, 2, slots), lambda p: (p, 0, 0))
-    col = pl.BlockSpec((1, slots, 2), lambda p: (p, 0, 0))
+    def lane(start):
+        return pl.BlockSpec((slots, PAIR), lambda p, start=start: (0, start + p))
+
+    def fixed(shape):
+        return pl.BlockSpec(shape, lambda p: (0, 0))
+
+    rows = jax.ShapeDtypeStruct((some, slots), jnp.float32)
     return pl.pallas_call(
         body,
         grid=(pairs,),
-        in_specs=[lane, lane, lane, row, col],
-        out_specs=[lane, row],
+        in_specs=[
+            pl.BlockSpec(memory_space=pltpu.SMEM),
+            lane(0),
+            lane(pairs),
+            lane(2 * pairs),
+            pl.BlockSpec((slots, PAIR), lambda p: (0, 3 * pairs)),
+            fixed((1, PAIR)),
+        ],
+        out_specs=[lane(0), fixed((some, slots)), fixed((slots, PAIR)), fixed((some, slots))],
         out_shape=[
-            jax.ShapeDtypeStruct((slots, width), jnp.bfloat16),
-            jax.ShapeDtypeStruct((pairs, 2, slots), jnp.float32),
+            jax.ShapeDtypeStruct((slots, pairs * PAIR), jnp.bfloat16),
+            rows,
+            jax.ShapeDtypeStruct((slots, PAIR), jnp.float32),
+            rows,
         ],
+        scratch_shapes=[pltpu.VMEM((some, slots), jnp.float32)],
         compiler_params=pltpu.CompilerParams(vmem_limit_bytes=56 << 20),
         cost_estimate=pl.CostEstimate(
-            flops=4 * slots * slots * width, bytes_accessed=8 * slots * width, transcendentals=0
+            flops=4 * slots * slots * pairs * PAIR, bytes_accessed=8 * slots * pairs * PAIR, transcendentals=0
         ),
         name="attention_fwd",
-    )(q, k, v, cum_row, key_col)
-
-
-def attention_bwd(q, k, v, d_out, cum_row, key_col, lse, heads_half, scale):
-    slots, width = q.shape
-    pairs = width // PAIR
-    tile = min(256, slots)
-    half = heads_half
-
-    def body(q_ref, k_ref, v_ref, do_ref, row_ref, col_ref, lse_ref,
-             dq_ref, dk_ref, dv_ref, drow_ref, dcol_ref, dk_acc, dv_acc, dcol_acc):
-        key_all = k_ref[...]
-        value_all = v_ref[...]
-        query_t = q_ref[...].T
-        key_t = k_ref[...].T
-        dout_t = do_ref[...].T
+    )(length, joined, joined, joined, joined, bias)
+
+
+def backward_scratch(slots):
+    return [
+        pltpu.VMEM((slots, PAIR), jnp.float32),
+        pltpu.VMEM((slots, PAIR), jnp.float32),
+        pltpu.VMEM((slots, PAIR), jnp.float32),
+        pltpu.VMEM((8, slots), jnp.float32),
+    ]
+
+
+class Backward:
+    def __init__(self, joined, d_out, offset, col, logit, grads, dk_acc, dv_acc, dcol, drow, head_size, scale):
+        self.joined, self.d_out, self.offset, self.col = joined, d_out, offset, col
+        self.logit, self.grads, self.dk_acc, self.dv_acc = logit, grads, dk_acc, dv_acc
+        self.dcol, self.drow, self.head_size, self.scale = dcol, drow, head_size, scale
+        self.slots = joined.shape[0]
+        self.pairs = (joined.shape[1] // PAIR - 1) // 3
+        self.tile = min(256, self.slots)
+
+    def start(self):
+        self.dcol[...] = jnp.zeros_like(self.dcol)
+        self.drow[...] = jnp.zeros_like(self.drow)
+
+    def lanes(self, pair, part=0):
+        return pl.ds(pl.multiple_of((part * self.pairs + pair) * PAIR, PAIR), PAIR)
+
+    def pair(self, pair):
+        slots, tile, half = self.slots, self.tile, self.head_size
+        dk_acc, dv_acc, dcol, drow = self.dk_acc, self.dv_acc, self.dcol, self.drow
+        queries = (self.joined[:, self.lanes(pair)].astype(jnp.float32) * self.scale).astype(jnp.bfloat16)
+        key_all = self.joined[:, self.lanes(pair, 1)]
+        value_all = self.joined[:, self.lanes(pair, 2)]
+        d_out = self.d_out[:, self.lanes(pair)]
+        query_t, key_t, dout_t = queries.T, key_all.T, d_out.T
         sub = lax.broadcasted_iota(jnp.int32, (PAIR, tile), 0)
         lanes = lax.broadcasted_iota(jnp.int32, (tile, PAIR), 1)
-        diag = lax.broadcasted_iota(jnp.int32, (tile, tile), 0) <= lax.broadcasted_iota(
-            jnp.int32, (tile, tile), 1
-        )
+        wide = lax.broadcasted_iota(jnp.int32, (slots, PAIR), 1)
+        diag = low_triangle(tile)
         zero = jnp.zeros((), jnp.bfloat16)
+        columns = [
+            jnp.sum(jnp.where(wide == 2 * pair + a, self.col[...], 0.0), axis=1, keepdims=True) for a in range(2)
+        ]
         dk_acc[...] = jnp.zeros_like(dk_acc)
         dv_acc[...] = jnp.zeros_like(dv_acc)
-        dcol_acc[...] = jnp.zeros_like(dcol_acc)
         for number in range(slots // tile):
             first, last = number * tile, (number + 1) * tile
             outs = []
             for a in range(2):
                 mine = (sub >= a * half) & (sub < (a + 1) * half)
                 own = (lanes >= a * half) & (lanes < (a + 1) * half)
+                at = pl.ds(2 * pair + a, 1)
                 scores = product(key_all[:last], jnp.where(mine, query_t[:, first:last], zero))
-                offset = row_ref[0, a : a + 1, first:last] - lse_ref[0, a : a + 1, first:last]
-                scores = scores + (offset - col_ref[0, :last, a : a + 1])
+                scores = scores + (self.offset[at, first:last] - columns[a][:last])
                 tail = jnp.where(diag, scores[first:], NEG_FILL)
                 scores = tail if number == 0 else jnp.concatenate([scores[:first], tail], axis=0)
                 probs = jnp.exp(scores)
@@ -128,42 +195,70 @@
                 dot = jnp.sum(d_probs * probs, axis=0, keepdims=True)
                 d_full = probs * (d_probs - dot)
                 d_scores = d_full.astype(jnp.bfloat16)
-                drow_ref[0, a : a + 1, first:last] = jnp.sum(d_full, axis=0, keepdims=True)
-                dcol_acc[:last, a : a + 1] += jnp.sum(d_full, axis=1, keepdims=True)
-                outs.append(product(key_t[a * half : (a + 1) * half, :last], d_scores) * scale)
-                dk_acc[:last, :] += product(d_scores, jnp.where(own, q_ref[first:last, :], zero))
+                drow[at, first:last] = jnp.sum(d_full, axis=0, keepdims=True)
+                sums = jnp.sum(d_full, axis=1, keepdims=True)
+                dcol[:last, :] += jnp.where(wide[:last] == 2 * pair + a, sums, 0.0)
+                outs.append(product(key_t[a * half : (a + 1) * half, :last], d_scores) * self.scale)
+                dk_acc[:last, :] += product(d_scores, jnp.where(own, queries[first:last, :], zero))
                 dv_acc[:last, :] += product(
-                    probs.astype(jnp.bfloat16), jnp.where(own, do_ref[first:last, :], zero)
+                    probs.astype(jnp.bfloat16), jnp.where(own, d_out[first:last, :], zero)
                 )
-            dq_ref[first:last, :] = jnp.concatenate(outs, axis=0).T.astype(dq_ref.dtype)
-        dk_ref[...] = dk_acc[...].astype(dk_ref.dtype)
-        dv_ref[...] = dv_acc[...].astype(dv_ref.dtype)
-        dcol_ref[0] = dcol_acc[...]
-
-    lane = pl.BlockSpec((slots, PAIR), lambda p: (0, p))
-    row = pl.BlockSpec((1, 2, slots), lambda p: (p, 0, 0))
-    col = pl.BlockSpec((1, slots, 2), lambda p: (p, 0, 0))
+            self.grads[first:last, self.lanes(pair)] = jnp.concatenate(outs, axis=0).T.astype(self.grads.dtype)
+        self.grads[:, self.lanes(pair, 1)] = dk_acc[...].astype(self.grads.dtype)
+        self.grads[:, self.lanes(pair, 2)] = dv_acc[...].astype(self.grads.dtype)
+
+    def end(self, bias_grad):
+        slots, tile, some = self.slots, self.tile, 8
+        change = self.drow[...] - self.dcol[...].T[:some]
+        rows = lax.broadcasted_iota(jnp.int32, (tile, tile), 0)
+        ones = (rows >= lax.broadcasted_iota(jnp.int32, (tile, tile), 1)).astype(jnp.float32)
+        carry = jnp.zeros((some, 1), jnp.float32)
+        pieces = []
+        for first in reversed(range(0, slots, tile)):
+            sums = exact(change[:, first : first + tile], ones) + carry
+            carry = sums[:, :1]
+            pieces.insert(0, sums)
+        grad = jnp.concatenate(pieces, axis=1) * jax.nn.sigmoid(-self.logit[...])
+        heads = lax.broadcasted_iota(jnp.int32, (some, slots), 0)
+        grad = jnp.where(heads < 2 * self.pairs, grad, 0.0)
+        bias_grad[...] = jnp.broadcast_to(jnp.sum(grad, axis=1, keepdims=True), bias_grad.shape)
+        wide = jnp.concatenate([grad, jnp.zeros((PAIR - some, slots), jnp.float32)], axis=0).T
+        self.grads[:, 3 * self.pairs * PAIR : (3 * self.pairs + 1) * PAIR] = wide.astype(self.grads.dtype)
+
+
+def attention_bwd(joined, d_out, offset, col, logit, head_size, scale):
+    slots, width = joined.shape
+    pairs = (width // PAIR - 1) // 3
+
+    def body(joined_ref, d_out_ref, offset_ref, col_ref, logit_ref, grads, bias_grad, *scratch):
+        work = Backward(
+            joined_ref, d_out_ref, offset_ref, col_ref, logit_ref, grads, *scratch, head_size, scale
+        )
+        work.start()
+
+        def step(pair, carry):
+            work.pair(pair)
+            return carry
+
+        lax.fori_loop(0, pairs, step, 0)
+        work.end(bias_grad)
+
+    vmem = pl.BlockSpec(memory_space=pltpu.VMEM)
     return pl.pallas_call(
         body,
-        grid=(pairs,),
-        in_specs=[lane, lane, lane, lane, row, col, row],
-        out_specs=[lane, lane, lane, row, col],
-        out_shape=[jax.ShapeDtypeStruct((slots, width), jnp.bfloat16)] * 3
-        + [
-            jax.ShapeDtypeStruct((pairs, 2, slots), jnp.float32),
-            jax.ShapeDtypeStruct((pairs, slots, 2), jnp.float32),
+        in_specs=[vmem] * 5,
+        out_specs=[vmem] * 2,
+        out_shape=[
+            jax.ShapeDtypeStruct((slots, width), jnp.bfloat16),
+            jax.ShapeDtypeStruct((8, PAIR), jnp.float32),
         ],
-        scratch_shapes=[
-            pltpu.VMEM((slots, PAIR), jnp.float32),
-            pltpu.VMEM((slots, PAIR), jnp.float32),
-            pltpu.VMEM((slots, 2), jnp.float32),
-        ],
+        scratch_shapes=backward_scratch(slots),
         compiler_params=pltpu.CompilerParams(vmem_limit_bytes=56 << 20),
         cost_estimate=pl.CostEstimate(
-            flops=10 * slots * slots * width, bytes_accessed=14 * slots * width, transcendentals=0
+            flops=10 * slots * slots * pairs * PAIR, bytes_accessed=14 * slots * pairs * PAIR, transcendentals=0
         ),
         name="attention_bwd",
-    )(q, k, v, d_out, cum_row, key_col, lse)
+    )(joined, d_out, offset, col, logit)
 
 
 MESH = pl.DeviceIdType.MESH
@@ -349,7 +444,7 @@
 
 def transposed_product(left, right, out):
     tall = 512 if out.shape[0] % 512 == 0 else 384
-    wide = 512 if out.shape[1] % 512 == 0 else 384
+    wide = next(size for size in (512, 384, 640, 128) if out.shape[1] % size == 0)
     across = out.shape[1] // wide
 
     def step(number, carry):
@@ -359,101 +454,6 @@
         return carry
 
     lax.fori_loop(0, (out.shape[0] // tall) * across, step, 0)
-
-
-def product_scatter(lefts, rights, transposed, collective_id, extras=()):
-    count = len(lefts)
-    more = len(extras)
-    rows = lefts[0].shape[0] // 4
-    half = rows // 2
-    width = rights[0].shape[0] if transposed else rights[0].shape[1]
-    tile = width // 3 if width % 384 == 0 else width
-
-    def body(*refs):
-        left, right = refs[:count], refs[count : 2 * count]
-        sides_in = refs[2 * count : 2 * count + 2 * more]
-        out = refs[2 * count + 2 * more]
-        sides_out = refs[2 * count + 2 * more + 1 : 2 * count + 3 * more + 1]
-        far, near, kept, land, carry, send, recv = refs[2 * count + 3 * more + 1 :]
-        me, side, down, across = sides()
-        meet({"seq": side}, {"seq": down})
-        to_side, to_down = {"seq": side}, {"seq": down}
-
-        def partial(rank, store):
-            at = pl.ds(pl.multiple_of(rank * rows, rows), rows)
-
-            def step(number, carried):
-                columns = pl.ds(pl.multiple_of(number * tile, tile), tile)
-                value = None
-                for a, b in zip(left, right):
-                    term = product_nt(a[at, :], b[columns, :]) if transposed else product(a[at, :], b[:, columns])
-                    value = term if value is None else value + term
-                store(columns, value)
-                return carried
-
-            lax.fori_loop(0, width // tile, step, 0)
-
-        def store_far(columns, value):
-            far[:, columns] = value.astype(far.dtype)
-
-        def store_side(columns, value):
-            kept[0, :, columns] = value[:half]
-            near[0, :, columns] = value[half:].astype(near.dtype)
-
-        def store_down(columns, value):
-            near[1, :, columns] = value[:half].astype(near.dtype)
-            kept[1, :, columns] = value[half:]
-
-        def store_own(columns, value):
-            out[:, columns] = value
-
-        partial(across, store_far)
-        first = push(far.at[pl.ds(0, half)], land.at[0], send.at[0], recv.at[0], to_down)
-        second = push(far.at[pl.ds(half, half)], land.at[1], send.at[1], recv.at[1], to_side)
-        partial(side, store_side)
-        third = push(near.at[0], land.at[2], send.at[2], recv.at[2], to_side)
-        partial(down, store_down)
-        fourth = push(near.at[1], land.at[3], send.at[3], recv.at[3], to_down)
-        first.wait_recv()
-        carry[0] = (kept[0] + land[0].astype(jnp.float32)).astype(carry.dtype)
-        fifth = push(carry.at[0], land.at[4], send.at[4], recv.at[4], to_side)
-        second.wait_recv()
-        carry[1] = (kept[1] + land[1].astype(jnp.float32)).astype(carry.dtype)
-        sixth = push(carry.at[1], land.at[5], send.at[5], recv.at[5], to_down)
-        partial(me, store_own)
-        for index in range(more):
-            transposed_product(sides_in[2 * index], sides_in[2 * index + 1], sides_out[index])
-        third.wait_recv()
-        fourth.wait_recv()
-        fifth.wait_recv()
-        out[:half, :] += land[3].astype(jnp.float32) + land[4].astype(jnp.float32)
-        sixth.wait_recv()
-        out[half:, :] += land[2].astype(jnp.float32) + land[5].astype(jnp.float32)
-        for copy in (first, second, third, fourth, fifth, sixth):
-            copy.wait_send()
-
-    vmem = pl.BlockSpec(memory_space=pltpu.VMEM)
-    low = jnp.bfloat16
-    return pl.pallas_call(
-        body,
-        in_specs=[vmem] * (2 * count + 2 * more),
-        out_specs=[vmem] * (1 + more),
-        out_shape=[jax.ShapeDtypeStruct((rows, width), jnp.float32)]
-        + [jax.ShapeDtypeStruct((a.shape[1], b.shape[1]), low) for a, b in extras],
-        scratch_shapes=[
-            pltpu.VMEM((rows, width), low),
-            pltpu.VMEM((2, half, width), low),
-            pltpu.VMEM((2, half, width), jnp.float32),
-            pltpu.VMEM((6, half, width), low),
-            pltpu.VMEM((2, half, width), low),
-            pltpu.SemaphoreType.DMA((6,)),
-            pltpu.SemaphoreType.DMA((6,)),
-        ],
-        compiler_params=pltpu.CompilerParams(
-            collective_id=collective_id, has_side_effects=True, vmem_limit_bytes=VMEM_LIMIT
-        ),
-        name="product_scatter",
-    )(*lefts, *rights, *(value for pair in extras for value in pair))
 
 
 def line():
@@ -612,13 +612,16 @@
                     self.copy(way, piece).wait_send()
 
 
-def first_gather(first, second, weights, block, collective_id):
+def first_gather(first, second, weights, block, w_gate, w_up, part, collective_id):
     rows, width = block.shape
     shards = 2 * lax.axis_size("seq")
     chips = shards // 2
-
-    def body(first_ref, second_ref, weights_ref, block_ref, first_full, second_full, weights_full, whole,
-             send, recv, local, line_send, line_recv, spread_send, spread_recv):
+    units = w_gate.shape[1] // 4
+    blocks = units // part
+
+    def body(first_ref, second_ref, weights_ref, block_ref, gate_ref, up_ref,
+             first_full, second_full, weights_full, whole, picked,
+             send, recv, local, line_send, line_recv, spread_send, spread_recv, pick):
         me, side, down, across = sides()
         line_chips, chip, core, forth, back, twin = line()
         meet({"seq": side}, {"seq": down}, forth, back, twin)
@@ -641,6 +644,16 @@
             keeps.append(keep)
         two.start()
         spread.step(0)
+        for index, source in enumerate((gate_ref, up_ref)):
+            for number in range(blocks):
+                column = pl.multiple_of((number * 4 + me) * part, part)
+                taken = pltpu.make_async_copy(
+                    source.at[:, pl.ds(column, part)],
+                    picked.at[:, pl.ds(index * units + number * part, part)],
+                    pick.at[index, number],
+                )
+                taken.start()
+                keeps.append(taken)
         run.step(1)
         one.relay()
         spread.step(1)
@@ -649,10 +662,11 @@
         spread.step(2)
         run.step(3)
         spread.step(3)
-        for job, keep in zip((one, two), keeps):
+        for job in (one, two):
             job.near()
             job.far()
             job.finish()
+        for keep in keeps:
             keep.wait()
         run.finish()
         spread.finish()
@@ -662,13 +676,14 @@
     dma = pltpu.SemaphoreType.DMA
     return pl.pallas_call(
         body,
-        in_specs=[vmem] * 4,
-        out_specs=[anywhere] * 3 + [vmem],
+        in_specs=[vmem] * 4 + [anywhere] * 2,
+        out_specs=[anywhere] * 3 + [vmem] * 2,
         out_shape=[
             jax.ShapeDtypeStruct((4 * first.shape[0],) + first.shape[1:], first.dtype),
             jax.ShapeDtypeStruct((4 * second.shape[0],) + second.shape[1:], second.dtype),
             jax.ShapeDtypeStruct((shards * weights.shape[0],) + weights.shape[1:], weights.dtype),
             jax.ShapeDtypeStruct((2, rows, width), block.dtype),
+            jax.ShapeDtypeStruct((w_gate.shape[0], 2 * units), w_gate.dtype),
         ],
         scratch_shapes=[
             dma((2, 6)),
@@ -678,56 +693,109 @@
             dma((shards,)),
             dma((3, LineSpread.pieces)),
             dma((2, LineSpread.pieces)),
+            dma((2, blocks)),
         ],
         compiler_params=pltpu.CompilerParams(
             collective_id=collective_id, has_side_effects=True, vmem_limit_bytes=VMEM_LIMIT
         ),
         name="first_gather",
-    )(first, second, weights, block)
-
-
-def add_everywhere(values, collective_id):
-    shape = values.shape
-    groups, shards = 4, 8
-
-    def body(values_ref, out, ranks, total, places, send, recv):
-        rank, place = lax.axis_index("seq"), lax.axis_index("wshard")
-        others = [{"seq": lax.rem(rank + k, groups)} for k in range(1, groups)]
-        along = [{"wshard": lax.rem(place + k, shards)} for k in range(1, shards)]
-        meet(*others, *along)
-        copies = [
-            push(values_ref, ranks.at[rank], send.at[k], recv.at[k], other) for k, other in enumerate(others)
+    )(first, second, weights, block, w_gate, w_up)
+
+
+class Everywhere:
+    def __init__(self, values, out, ranks, total, places, send, recv):
+        self.values, self.out, self.ranks, self.total, self.places = values, out, ranks, total, places
+        self.send, self.recv = send, recv
+        self.groups, self.shards = ranks.shape[0], places.shape[0]
+        self.rank, self.place = lax.axis_index("seq"), lax.axis_index("wshard")
+
+    def others(self):
+        return [{"seq": lax.rem(self.rank + k, self.groups)} for k in range(1, self.groups)]
+
+    def along(self):
+        return [{"wshard": lax.rem(self.place + k, self.shards)} for k in range(1, self.shards)]
+
+    def start(self):
+        self.first = [
+            push(self.values, self.ranks.at[self.rank], self.send.at[k], self.recv.at[k], other)
+            for k, other in enumerate(self.others())
         ]
-        ranks[rank] = values_ref[...]
-        for copy in copies:
+        self.ranks[self.rank] = self.values[...]
+
+    def relay(self):
+        for copy in self.first:
             copy.wait()
-        total[...] = (ranks[0] + ranks[1]) + (ranks[2] + ranks[3])
-        copies = [
-            push(total, places.at[place], send.at[groups + k], recv.at[groups + k], other)
-            for k, other in enumerate(along)
+        ranks, groups = self.ranks, self.groups
+        self.total[...] = (ranks[0] + ranks[1]) + (ranks[2] + ranks[3])
+        self.second = [
+            push(self.total, self.places.at[self.place], self.send.at[groups + k], self.recv.at[groups + k], other)
+            for k, other in enumerate(self.along())
         ]
-        places[place] = total[...]
-        for copy in copies:
+        self.places[self.place] = self.total[...]
+
+    def end(self):
+        for copy in self.second:
             copy.wait()
-        sums = [places[k] + places[k + 1] for k in range(0, shards, 2)]
-        out[...] = (sums[0] + sums[1]) + (sums[2] + sums[3])
+        sums = [self.places[k] + self.places[k + 1] for k in range(0, self.shards, 2)]
+        self.out[...] = (sums[0] + sums[1]) + (sums[2] + sums[3])
+
+
+def last_gather(values, small, collective_id):
+    count = len(values)
+    groups = lax.axis_size("seq")
+    shards = 2 * groups
+
+    def body(*refs):
+        own, small_ref = refs[:count], refs[count]
+        full, small_out = refs[count + 1 : 2 * count + 1], refs[2 * count + 1]
+        send, recv, local = refs[2 * count + 2 : 2 * count + 5]
+        me, side, down, across = sides()
+        total = Everywhere(small_ref, small_out, *refs[2 * count + 5 :])
+        meet(*total.others(), *total.along())
+        jobs = [SquareGather(own[i], full[i], send.at[i], recv.at[i]) for i in range(count)]
+        total.start()
+        keeps = []
+        for i, job in enumerate(jobs):
+            job.start()
+            rows = own[i].shape[0]
+            keep = pltpu.make_async_copy(
+                own[i], full[i].at[pl.ds(pl.multiple_of(me * rows, rows), rows)], local.at[i]
+            )
+            keep.start()
+            keeps.append(keep)
+        total.relay()
+        for job in jobs:
+            job.relay()
+        total.end()
+        for job, keep in zip(jobs, keeps):
+            job.near()
+            job.far()
+            job.finish()
+            keep.wait()
 
     vmem = pl.BlockSpec(memory_space=pltpu.VMEM)
+    dma = pltpu.SemaphoreType.DMA
     return pl.pallas_call(
         body,
-        in_specs=[vmem],
-        out_specs=vmem,
-        out_shape=jax.ShapeDtypeStruct(shape, jnp.float32),
+        in_specs=[vmem] * (count + 1),
+        out_specs=[pl.BlockSpec(memory_space=pl.ANY)] * count + [vmem],
+        out_shape=[jax.ShapeDtypeStruct((4 * v.shape[0],) + v.shape[1:], v.dtype) for v in values]
+        + [jax.ShapeDtypeStruct(small.shape, jnp.float32)],
         scratch_shapes=[
-            pltpu.VMEM((groups,) + shape, jnp.float32),
-            pltpu.VMEM(shape, jnp.float32),
-            pltpu.VMEM((shards,) + shape, jnp.float32),
-            pltpu.SemaphoreType.DMA((groups + shards,)),
-            pltpu.SemaphoreType.DMA((groups + shards,)),
+            dma((count, 6)),
+            dma((count, 6)),
+            dma((count,)),
+            pltpu.VMEM((groups,) + small.shape, jnp.float32),
+            pltpu.VMEM(small.shape, jnp.float32),
+            pltpu.VMEM((shards,) + small.shape, jnp.float32),
+            dma((groups + shards,)),
+            dma((groups + shards,)),
         ],
-        compiler_params=pltpu.CompilerParams(collective_id=collective_id, has_side_effects=True),
-        name="add_everywhere",
-    )(values)
+        compiler_params=pltpu.CompilerParams(
+            collective_id=collective_id, has_side_effects=True, vmem_limit_bytes=VMEM_LIMIT
+        ),
+        name="last_gather",
+    )(*values, small)
 
 
 def join_units(every, down, part):
@@ -784,6 +852,532 @@
     )(every)
 
 
+class SquareScatter:
+    @staticmethod
+    def scratch(rows, width):
+        half = rows // 2
+        low = jnp.bfloat16
+        return [
+            pltpu.VMEM((rows, width), low),
+            pltpu.VMEM((2, half, width), low),
+            pltpu.VMEM((2, half, width), jnp.float32),
+            pltpu.VMEM((6, half, width), low),
+            pltpu.VMEM((2, half, width), low),
+            pltpu.SemaphoreType.DMA((6,)),
+            pltpu.SemaphoreType.DMA((6,)),
+        ]
+
+    def __init__(self, lefts, rights, transposed, out, far, near, kept, land, carry, send, recv):
+        self.lefts, self.rights, self.transposed, self.out = lefts, rights, transposed, out
+        self.far, self.near, self.kept, self.land, self.carry = far, near, kept, land, carry
+        self.send, self.recv = send, recv
+        self.rows, self.width = out.shape
+        self.half = self.rows // 2
+        self.tile = self.width // 3 if self.width % 384 == 0 else self.width
+
+    def copy(self, index):
+        me, side, down, across = sides()
+        source = (
+            self.far.at[pl.ds(0, self.half)],
+            self.far.at[pl.ds(self.half, self.half)],
+            self.near.at[0],
+            self.near.at[1],
+            self.carry.at[0],
+            self.carry.at[1],
+        )[index]
+        return pltpu.make_async_remote_copy(
+            src_ref=source,
+            dst_ref=self.land.at[index],
+            send_sem=self.send.at[index],
+            recv_sem=self.recv.at[index],
+            device_id={"seq": down if index in (0, 3, 5) else side},
+            device_id_type=MESH,
+        )
+
+    def partial(self, rank, store):
+        at = pl.ds(pl.multiple_of(rank * self.rows, self.rows), self.rows)
+
+        def step(number, carried):
+            columns = pl.ds(pl.multiple_of(number * self.tile, self.tile), self.tile)
+            value = None
+            for a, b in zip(self.lefts, self.rights):
+                if self.transposed:
+                    term = product_nt(a[at, :], b[columns, :])
+                else:
+                    term = product(a[at, :], b[:, columns])
+                value = term if value is None else value + term
+            store(columns, value)
+            return carried
+
+        lax.fori_loop(0, self.width // self.tile, step, 0)
+
+    def begin(self):
+        me, side, down, across = sides()
+        half, far, near, kept = self.half, self.far, self.near, self.kept
+
+        def store_far(columns, value):
+            far[:, columns] = value.astype(far.dtype)
+
+        def store_side(columns, value):
+            kept[0, :, columns] = value[:half]
+            near[0, :, columns] = value[half:].astype(near.dtype)
+
+        def store_down(columns, value):
+            near[1, :, columns] = value[:half].astype(near.dtype)
+            kept[1, :, columns] = value[half:]
+
+        self.partial(across, store_far)
+        self.copy(0).start()
+        self.copy(1).start()
+        self.partial(side, store_side)
+        self.copy(2).start()
+        self.partial(down, store_down)
+        self.copy(3).start()
+
+    def relay(self):
+        for index in (0, 1):
+            self.copy(index).wait_recv()
+            total = self.kept[index] + self.land[index].astype(jnp.float32)
+            self.carry[index] = total.astype(self.carry.dtype)
+            self.copy(4 + index).start()
+
+    def own(self):
+        out = self.out
+
+        def store_own(columns, value):
+            out[:, columns] = value
+
+        self.partial(lax.axis_index("seq"), store_own)
+
+    def end(self):
+        for index in (2, 3, 4, 5):
+            self.copy(index).wait_recv()
+        land, half = self.land, self.half
+        self.out[:half, :] += land[3].astype(jnp.float32) + land[4].astype(jnp.float32)
+        self.out[half:, :] += land[2].astype(jnp.float32) + land[5].astype(jnp.float32)
+        for index in range(6):
+            self.copy(index).wait_send()
+
+
+class LineScatter:
+    @staticmethod
+    def scratch(chips, rows, width):
+        low = jnp.bfloat16
+        dma = pltpu.SemaphoreType.DMA
+        return [pltpu.VMEM((chips, rows, width), low)] * 3 + [dma((2, chips)), dma((3, chips))]
+
+    def __init__(self, terms, out, twin_in, forth_in, back_in, send, recv):
+        self.terms, self.out, self.twin_in = terms, out, twin_in
+        self.forth_in, self.back_in, self.send, self.recv = forth_in, back_in, send, recv
+        self.chips, self.chip, self.core, *self.devices = line()
+        self.rows = twin_in.shape[1]
+
+    def term(self, chip, core):
+        return self.terms.at[pl.ds(pl.multiple_of((2 * chip + core) * self.rows, self.rows), self.rows)]
+
+    def swap(self, chip):
+        return pltpu.make_async_remote_copy(
+            src_ref=self.term(chip, 1 - self.core),
+            dst_ref=self.twin_in.at[chip],
+            send_sem=self.send.at[0, chip],
+            recv_sem=self.recv.at[0, chip],
+            device_id=self.devices[2],
+            device_id_type=MESH,
+        )
+
+    def hop(self, way, chip):
+        return pltpu.make_async_remote_copy(
+            src_ref=self.twin_in.at[chip],
+            dst_ref=(self.forth_in, self.back_in)[way].at[chip],
+            send_sem=self.send.at[1, chip],
+            recv_sem=self.recv.at[1 + way, chip],
+            device_id=self.devices[way],
+            device_id_type=MESH,
+        )
+
+    def start(self):
+        for chip in (self.chips - 1, 0, *range(1, self.chips - 1)):
+            self.swap(chip).start()
+
+    def pair(self, chip):
+        return self.term(chip, self.core)[...].astype(jnp.float32) + self.twin_in[chip].astype(jnp.float32)
+
+    def pass_on(self, way, chip, first):
+        self.swap(chip).wait_recv()
+        source = (self.forth_in, self.back_in)[way]
+
+        @pl.when(first)
+        def _():
+            self.twin_in[chip] = self.pair(chip).astype(self.twin_in.dtype)
+
+        @pl.when(jnp.logical_not(first))
+        def _():
+            self.hop(way, chip).wait_recv()
+            total = self.pair(chip) + source[chip].astype(jnp.float32)
+            self.twin_in[chip] = total.astype(self.twin_in.dtype)
+
+        self.hop(way, chip).start()
+
+    def step(self, number):
+        forth, back = self.chips - number, number - 1
+        low_end = self.chip < self.chips // 2
+
+        @pl.when(low_end & (forth > self.chip))
+        def _():
+            self.pass_on(0, forth, self.chip == 0)
+
+        @pl.when(back < self.chip)
+        def _():
+            self.pass_on(1, back, self.chip == self.chips - 1)
+
+        @pl.when(jnp.logical_not(low_end) & (forth > self.chip))
+        def _():
+            self.pass_on(0, forth, self.chip == 0)
+
+    def end(self):
+        for chip in range(self.chips):
+
+            @pl.when(self.chip == chip)
+            def _():
+                self.swap(chip).wait_recv()
+                total = self.pair(chip)
+                if chip > 0:
+                    self.hop(0, chip).wait_recv()
+                    total = total + self.forth_in[chip].astype(jnp.float32)
+                if chip < self.chips - 1:
+                    self.hop(1, chip).wait_recv()
+                    total = total + self.back_in[chip].astype(jnp.float32)
+                self.out[...] = total.astype(self.out.dtype)
+
+            self.swap(chip).wait_send()
+
+            @pl.when(self.chip != chip)
+            def _():
+                self.hop(0, chip).wait_send()
+
+
+class LineCollect:
+    pieces = 2
+
+    @staticmethod
+    def scratch(rows, width):
+        low = jnp.bfloat16
+        dma = pltpu.SemaphoreType.DMA
+        pieces = LineCollect.pieces
+        return [pltpu.VMEM((rows, width), low)] * 3 + [dma((2, pieces)), dma((3, pieces))]
+
+    def __init__(self, terms, out, twin_in, forth_in, back_in, send, recv):
+        self.terms, self.out, self.twin_in = terms, out, twin_in
+        self.forth_in, self.back_in, self.send, self.recv = forth_in, back_in, send, recv
+        self.target = lax.axis_index("seq")
+        self.chips, self.chip, self.core, *self.devices = line()
+        self.rows = twin_in.shape[0]
+        self.tall = self.rows // self.pieces
+
+    def at(self, piece):
+        return pl.ds(piece * self.tall, self.tall)
+
+    def term(self, piece, core):
+        start = pl.multiple_of(core * self.rows + piece * self.tall, self.tall)
+        return self.terms.at[pl.ds(start, self.tall)]
+
+    def swap(self, piece):
+        return pltpu.make_async_remote_copy(
+            src_ref=self.term(piece, 1 - self.core),
+            dst_ref=self.twin_in.at[self.at(piece)],
+            send_sem=self.send.at[0, piece],
+            recv_sem=self.recv.at[0, piece],
+            device_id=self.devices[2],
+            device_id_type=MESH,
+        )
+
+    def hop(self, way, piece):
+        return pltpu.make_async_remote_copy(
+            src_ref=self.out.at[self.at(piece)],
+            dst_ref=(self.forth_in, self.back_in)[way].at[self.at(piece)],
+            send_sem=self.send.at[1, piece],
+            recv_sem=self.recv.at[1 + way, piece],
+            device_id=self.devices[way],
+            device_id_type=MESH,
+        )
+
+    def start(self):
+        for piece in range(self.pieces):
+            self.swap(piece).start()
+
+    def add(self, piece):
+        low = self.out.dtype
+        self.swap(piece).wait_recv()
+        total = self.term(piece, self.core)[...].astype(jnp.float32)
+        total = total + self.twin_in[self.at(piece), :].astype(jnp.float32)
+        self.out[self.at(piece), :] = total.astype(low)
+        for way, there in enumerate(
+            (
+                (self.chip <= self.target) & (self.chip > 0),
+                (self.chip >= self.target) & (self.chip < self.chips - 1),
+            )
+        ):
+
+            @pl.when(there)
+            def _():
+                self.hop(way, piece).wait_recv()
+                more = (self.forth_in, self.back_in)[way][self.at(piece), :].astype(jnp.float32)
+                self.out[self.at(piece), :] = (self.out[self.at(piece), :].astype(jnp.float32) + more).astype(low)
+
+    def level(self, number):
+        for way, goes in enumerate(
+            (
+                (self.chip < self.target) & (self.chip == number),
+                (self.chip > self.target) & (self.chips - 1 - self.chip == number),
+            )
+        ):
+
+            @pl.when(goes)
+            def _():
+                for piece in range(self.pieces):
+                    self.add(piece)
+                    self.hop(way, piece).start()
+
+    def end(self):
+        @pl.when(self.chip == self.target)
+        def _():
+            for piece in range(self.pieces):
+                self.add(piece)
+
+        for piece in range(self.pieces):
+            self.swap(piece).wait_send()
+
+            @pl.when(self.chip != self.target)
+            def _():
+                self.hop(0, piece).wait_send()
+
+
+class SquareSpread:
+    def __init__(self, own, out, send, recv):
+        self.own, self.out, self.send, self.recv = own, out, send, recv
+        self.chip = line()[1]
+        self.half = own.shape[0] // 2
+
+    def copy(self, index):
+        me, side, down, across = sides()
+        if index < 2:
+            source, target = self.own, self.out
+        else:
+            source = target = self.out.at[pl.ds((index - 2) * self.half, self.half)]
+        return pltpu.make_async_remote_copy(
+            src_ref=source,
+            dst_ref=target,
+            send_sem=self.send.at[index],
+            recv_sem=self.recv.at[index],
+            device_id={"seq": (side, down, down, side)[index]},
+            device_id_type=MESH,
+        )
+
+    def roles(self):
+        me, side, down, across = sides()
+        return [self.chip == rank for rank in (me, side, down, across)]
+
+    def start(self):
+        @pl.when(self.roles()[0])
+        def _():
+            self.copy(0).start()
+            self.copy(1).start()
+            self.out[...] = self.own[...]
+
+    def relay(self):
+        for index in (0, 1):
+
+            @pl.when(self.roles()[1 + index])
+            def _():
+                self.copy(index).wait_recv()
+                self.copy(2 + index).start()
+
+    def end(self):
+        mine, by_side, by_down, far = self.roles()
+
+        @pl.when(mine)
+        def _():
+            self.copy(0).wait_send()
+            self.copy(1).wait_send()
+
+        @pl.when(by_side)
+        def _():
+            self.copy(2).wait_send()
+
+        @pl.when(by_down)
+        def _():
+            self.copy(3).wait_send()
+
+        @pl.when(far)
+        def _():
+            self.copy(2).wait_recv()
+            self.copy(3).wait_recv()
+
+
+def product_scatter(lefts, rights, transposed, collective_id, extras=()):
+    count = len(lefts)
+    more = len(extras)
+    rows = lefts[0].shape[0] // 4
+    width = rights[0].shape[0] if transposed else rights[0].shape[1]
+
+    def body(*refs):
+        left, right = refs[:count], refs[count : 2 * count]
+        sides_in = refs[2 * count : 2 * count + 2 * more]
+        out = refs[2 * count + 2 * more]
+        sides_out = refs[2 * count + 2 * more + 1 : 2 * count + 3 * more + 1]
+        me, side, down, across = sides()
+        meet({"seq": side}, {"seq": down})
+        job = SquareScatter(left, right, transposed, out, *refs[2 * count + 3 * more + 1 :])
+        job.begin()
+        job.relay()
+        job.own()
+        for index in range(more):
+            transposed_product(sides_in[2 * index], sides_in[2 * index + 1], sides_out[index])
+        job.end()
+
+    vmem = pl.BlockSpec(memory_space=pltpu.VMEM)
+    return pl.pallas_call(
+        body,
+        in_specs=[vmem] * (2 * count + 2 * more),
+        out_specs=[vmem] * (1 + more),
+        out_shape=[jax.ShapeDtypeStruct((rows, width), jnp.float32)]
+        + [jax.ShapeDtypeStruct((a.shape[1], b.shape[1]), jnp.bfloat16) for a, b in extras],
+        scratch_shapes=SquareScatter.scratch(rows, width),
+        compiler_params=pltpu.CompilerParams(
+            collective_id=collective_id, has_side_effects=True, vmem_limit_bytes=VMEM_LIMIT
+        ),
+        name="product_scatter",
+    )(*lefts, *rights, *(value for pair in extras for value in pair))
+
+
+def middle_backward(joined, d_out, offset, col, logit, hidden, w_down, gated, grad_branch,
+                    head_size, scale, collective_id):
+    slots, lanes = joined.shape
+    width = w_down.shape[1]
+    tokens = slots // 4
+    columns = gated.shape[1]
+
+    def body(joined_ref, d_out_ref, offset_ref, col_ref, logit_ref, hidden_ref, down_ref, gated_ref, branch_ref,
+             grads, bias_grad, lowered, collected, terms, *scratch):
+        me, side, down, across = sides()
+        chips, chip, core, forth, back, twin = line()
+        meet({"seq": side}, {"seq": down}, forth, back, twin)
+        work = Backward(
+            joined_ref, d_out_ref, offset_ref, col_ref, logit_ref, grads, *scratch[:4], head_size, scale
+        )
+        job = SquareScatter([hidden_ref], [down_ref], False, lowered, *scratch[4:11])
+        collect = LineCollect(terms, collected, *scratch[11:])
+        transposed_product(gated_ref, branch_ref, terms)
+        collect.start()
+        job.begin()
+        work.start()
+        collect.level(0)
+
+        def step(pair, carry):
+            work.pair(pair)
+
+            @pl.when(pair == 0)
+            def _():
+                job.relay()
+
+            @pl.when(pair == 1)
+            def _():
+                collect.level(1)
+
+            return carry
+
+        lax.fori_loop(0, work.pairs, step, 0)
+        collect.level(2)
+        job.own()
+        work.end(bias_grad)
+        job.end()
+        collect.end()
+
+    vmem = pl.BlockSpec(memory_space=pltpu.VMEM)
+    low = jnp.bfloat16
+    return pl.pallas_call(
+        body,
+        in_specs=[vmem] * 9,
+        out_specs=[vmem] * 4,
+        out_shape=[
+            jax.ShapeDtypeStruct((slots, lanes), low),
+            jax.ShapeDtypeStruct((8, PAIR), jnp.float32),
+            jax.ShapeDtypeStruct((tokens, width), jnp.float32),
+            jax.ShapeDtypeStruct((columns // 2, width), low),
+        ],
+        scratch_shapes=[pltpu.VMEM((columns, width), low)]
+        + backward_scratch(slots)
+        + SquareScatter.scratch(tokens, width)
+        + LineCollect.scratch(columns // 2, width),
+        compiler_params=pltpu.CompilerParams(
+            collective_id=collective_id, has_side_effects=True, vmem_limit_bytes=VMEM_LIMIT
+        ),
+        name="middle_backward",
+    )(joined, d_out, offset, col, logit, hidden, w_down, gated, grad_branch)
+
+
+def last_backward(grads, grad_gate_pre, normed, weights, collected, collective_id):
+    slots, depth = normed.shape
+    front = grads.shape[1]
+    lanes = weights.shape[1]
+    tokens = slots // 4
+    shards = 2 * lax.axis_size("seq")
+    rows = depth // shards
+
+    def body(grads_ref, gate_ref, normed_ref, weights_ref, collected_ref, summed, share, spread_out, terms,
+             spread_send, spread_recv, *scratch):
+        me, side, down, across = sides()
+        chips, chip, core, forth, back, twin = line()
+        meet({"seq": side}, {"seq": down}, forth, back, twin)
+        job = SquareScatter(
+            [grads_ref, gate_ref],
+            [weights_ref.at[:, pl.ds(0, front)], weights_ref.at[:, pl.ds(front, lanes - front)]],
+            True,
+            summed,
+            *scratch[:7],
+        )
+        run = LineScatter(terms, share, *scratch[7:])
+        spread = SquareSpread(collected_ref, spread_out, spread_send, spread_recv)
+        transposed_product(normed_ref, grads_ref, terms.at[:, pl.ds(0, front)])
+        transposed_product(normed_ref, gate_ref, terms.at[:, pl.ds(front, lanes - front)])
+        run.start()
+        spread.start()
+        job.begin()
+        run.step(1)
+        job.relay()
+        spread.relay()
+        run.step(2)
+        run.step(3)
+        job.own()
+        job.end()
+        spread.end()
+        run.end()
+
+    vmem = pl.BlockSpec(memory_space=pltpu.VMEM)
+    low = jnp.bfloat16
+    return pl.pallas_call(
+        body,
+        in_specs=[vmem] * 5,
+        out_specs=[vmem] * 3,
+        out_shape=[
+            jax.ShapeDtypeStruct((tokens, depth), jnp.float32),
+            jax.ShapeDtypeStruct((rows, lanes), low),
+            jax.ShapeDtypeStruct(collected.shape, low),
+        ],
+        scratch_shapes=[
+            pltpu.VMEM((depth, lanes), low),
+            pltpu.SemaphoreType.DMA((4,)),
+            pltpu.SemaphoreType.DMA((4,)),
+        ]
+        + SquareScatter.scratch(tokens, depth)
+        + LineScatter.scratch(shards // 2, rows, lanes),
+        compiler_params=pltpu.CompilerParams(
+            collective_id=collective_id, has_side_effects=True, vmem_limit_bytes=VMEM_LIMIT
+        ),
+        name="last_backward",
+    )(grads, grad_gate_pre, normed, weights, collected)
+
+
 def gather(value, axis_name):
     return lax.all_gather(value, axis_name, axis=0, tiled=True)
 
@@ -801,12 +1395,10 @@
 
 def multiply_scatter(lefts, rights, transposed, collective_id, extras=()):
     if square(lax.axis_size("seq")):
-        summed, *products = product_scatter(lefts, rights, transposed, collective_id, extras)
-        return (summed, *products) if extras else summed
+        return product_scatter(lefts, rights, transposed, collective_id, extras)
     products = [product_tn(a, b).astype(jnp.bfloat16) for a, b in extras]
     total = sum(product_nt(a, b) if transposed else product(a, b) for a, b in zip(lefts, rights))
-    summed = scatter(total.astype(jnp.bfloat16), "seq").astype(jnp.float32)
-    return (summed, *products) if extras else summed
+    return [scatter(total.astype(jnp.bfloat16), "seq").astype(jnp.float32), *products]
 
 
 def on_device(
@@ -831,12 +1423,16 @@
     heads = forget_bias.shape[0]
     groups = lax.axis_size("seq")
     shards = lax.axis_size("wshard")
+    fast = square(groups) and shards == 2 * groups
     local_heads = heads // groups
     head_size = width // heads
     columns = width // groups
+    lanes = columns + -columns % PAIR
+    front = 3 * lanes + PAIR
     slots = tokens * groups
     hidden_size = w_gate.shape[1]
     part = hidden_size // (groups * shards)
+    units = shards * part
     scale = head_size ** (-0.5)
     length = lengths[0]
     seq_rank = lax.axis_index("seq")
@@ -847,146 +1443,123 @@
     inputs = layer_input[0].astype(jnp.float32)
     cotangent_low = jnp.where(valid_slots, output_grad[0], jnp.zeros((), low))
     cotangent = cotangent_low.astype(jnp.float32)
-    pad_heads = PAIR
-
-    def own_columns(weight):
-        return lax.dynamic_slice_in_dim(weight, seq_rank * columns, columns, 1)
+
+    def own_columns(weight, size):
+        taken = lax.dynamic_slice_in_dim(weight, seq_rank * columns, columns, 1)
+        return jnp.pad(taken, ((0, 0), (0, size - columns))) if size > columns else taken
 
     def own_units(weight):
         split = weight.reshape(weight.shape[0], shards, groups, part)
         mine = lax.dynamic_index_in_dim(split, seq_rank, 2, keepdims=False)
-        return mine.reshape(weight.shape[0], shards * part)
+        return mine.reshape(weight.shape[0], units)
 
     own_forget = lax.dynamic_slice_in_dim(w_forget, seq_rank * local_heads, local_heads, 1)
-    own_forget = jnp.pad(own_forget, ((0, 0), (0, pad_heads - local_heads)))
+    own_forget = jnp.pad(own_forget, ((0, 0), (0, PAIR - local_heads)))
+    own_bias = lax.dynamic_slice_in_dim(forget_bias, seq_rank * local_heads, local_heads)
+    own_bias = jnp.pad(own_bias, (0, PAIR - local_heads))[None]
     mine_attn = jnp.concatenate(
-        [own_columns(w_query), own_columns(w_key), own_columns(w_value), own_forget],
+        [*(own_columns(w, lanes) for w in (w_query, w_key, w_value)), own_forget, own_columns(w_ogate, columns)],
         axis=1,
     )
-    fast = square(groups) and shards == 2 * groups
+    mine_down = lax.dynamic_slice_in_dim(w_down, seq_rank * part, part, 0)
     normed_attn_own = rms_norm(inputs, norm_attn).astype(low)
     if fast:
-        normed_attn, cotangent_all, full_attn, full_out = first_gather(
-            normed_attn_own, cotangent_low, mine_attn, w_out, 0
+        normed_attn, cotangent_all, full_attn, full_out, mine_ffn = first_gather(
+            normed_attn_own, cotangent_low, mine_attn, w_out, w_gate, w_up, part, 0
         )
         full_out = full_out.reshape(columns, width)
-        later = lax.optimization_barrier((full_out, w_ogate, w_gate, w_up, w_down))
-        full_out, w_ogate, w_gate, w_up, w_down = later
+        mine_ffn, mine_down = lax.optimization_barrier((mine_ffn, mine_down))
     else:
         full_attn = gather(mine_attn, "wshard")
         normed_attn = gather(normed_attn_own, "seq")
         cotangent_all = gather(cotangent_low, "seq")
         full_out = lax.dynamic_slice_in_dim(gather(w_out, "wshard"), seq_rank * columns, columns, 0)
-    full_ogate = gather(own_columns(w_ogate), "wshard")
-    mine_ffn = jnp.concatenate([own_units(w_gate), own_units(w_up)], axis=1)
-    mine_down = lax.dynamic_slice_in_dim(w_down, seq_rank * part, part, 0)
+        mine_ffn = jnp.concatenate([own_units(w_gate), own_units(w_up)], axis=1)
     full_ffn = gather(mine_ffn, "wshard")
     full_down = gather(mine_down, "wshard")
 
-    projected = product(normed_attn, full_attn)
-    queries = projected[:, :columns].astype(low)
-    keys = projected[:, columns : 2 * columns].astype(low)
-    values = projected[:, 2 * columns : 3 * columns].astype(low)
-    gate_pre = product(normed_attn, full_ogate)
-    forget_pre = projected[:, 3 * columns : 3 * columns + local_heads].astype(low)
-    bias_local = lax.dynamic_slice_in_dim(forget_bias, seq_rank * local_heads, local_heads)
-    forget_total = forget_pre.astype(jnp.float32) + bias_local
-    log_forget, pull_forget = jax.vjp(jax.nn.log_sigmoid, forget_total)
-    cumulative = jnp.cumsum(log_forget, axis=0)
-    even = -local_heads % 2
-
-    def pad_lanes(value):
-        return jnp.pad(value, ((0, 0), (0, even * head_size))) if even else value
-
-    pairs = (local_heads + even) // 2
-    cum = jnp.pad(cumulative, ((0, 0), (0, even))) if even else cumulative
-    usable = (jnp.arange(slots, dtype=jnp.int32) < length)[:, None]
-    cum_row = cum.T.reshape(pairs, 2, slots)
-    key_col = jnp.where(usable, cum, -NEG_FILL).reshape(slots, pairs, 2).transpose(1, 0, 2)
-    q_in = pad_lanes((queries.astype(jnp.float32) * scale).astype(low))
-    k_in = pad_lanes(keys)
-    v_in = pad_lanes(values)
-    attended_low, log_total = attention_fwd(q_in, k_in, v_in, cum_row, key_col, head_size)
+    joined = product(normed_attn, full_attn[:, :front]).astype(low)
+    gate_pre = product(normed_attn, full_attn[:, front:])
+    attended_low, offset, col, logit = attention_fwd(joined, own_bias, lengths, head_size, scale)
     attended = attended_low[:, :columns].astype(jnp.float32)
     gated_full, pull_gate = jax.vjp(gate_product, attended, gate_pre)
     gated = gated_full.astype(low)
-    branch = multiply_scatter([gated], [full_out], False, 1)
+    (branch,) = multiply_scatter([gated], [full_out], False, 1)
     middle = inputs + branch
     normed_ffn_own, pull_ffn_norm = jax.vjp(rms_norm, middle, norm_ffn)
     normed_ffn, gate_up = gather_multiply(normed_ffn_own.astype(low), full_ffn, False, 2)
-    units = shards * part
     hidden_full, pull_swiglu = jax.vjp(swiglu, gate_up[:, :units], gate_up[:, units:])
     hidden = hidden_full.astype(low)
 
+    grad_w_down = product_tn(hidden, cotangent_all).astype(low)
+    share_down = scatter(grad_w_down, "wshard")
     grad_hidden = product_nt(cotangent_all, full_down)
     grad_gate_full, grad_up_full = pull_swiglu(grad_hidden)
     grad_gate_up = jnp.concatenate([grad_gate_full.astype(low), grad_up_full.astype(low)], axis=1)
-    grad_normed_ffn, grad_w_down, grad_w_ffn = multiply_scatter(
-        [grad_gate_up], [full_ffn], True, 3, [(hidden, cotangent_all), (normed_ffn, grad_gate_up)]
+    grad_gate_up, grad_w_down = lax.optimization_barrier((grad_gate_up, grad_w_down))
+    grad_normed_ffn, grad_w_ffn = multiply_scatter(
+        [grad_gate_up], [full_ffn], True, 3, [(normed_ffn, grad_gate_up)]
     )
-    share_down = scatter(grad_w_down, "wshard")
     share_ffn = scatter(grad_w_ffn, "wshard")
     grad_middle_part, grad_norm_ffn = pull_ffn_norm(grad_normed_ffn)
     grad_middle = cotangent + grad_middle_part
     grad_branch, grad_gated = gather_multiply(grad_middle.astype(low), full_out, True, 4)
-    grad_w_out = product_tn(gated, grad_branch).astype(low)
     grad_attended_full, grad_gate_pre_full = pull_gate(grad_gated)
-    grad_attended = pad_lanes(grad_attended_full.astype(low))
+    grad_attended = grad_attended_full.astype(low)
     grad_gate_pre = grad_gate_pre_full.astype(low)
-    dq, dk, dv, drow, dcol = attention_bwd(
-        q_in, k_in, v_in, grad_attended, cum_row, key_col, log_total, head_size, scale
-    )
-    grad_cum = drow.reshape(2 * pairs, slots).T - dcol.transpose(1, 0, 2).reshape(slots, 2 * pairs)
-    grad_cum = grad_cum[:, :local_heads]
-    grad_log_forget = jnp.flip(jnp.cumsum(jnp.flip(grad_cum, 0), axis=0), 0)
-    grad_forget_total = pull_forget(grad_log_forget)[0]
-    grad_bias_local = jnp.sum(grad_forget_total, axis=0)
-    grad_forget = jnp.pad(grad_forget_total.astype(low), ((0, 0), (0, pad_heads - local_heads)))
+    if lanes > columns:
+        grad_attended = jnp.pad(grad_attended, ((0, 0), (0, lanes - columns)))
+    if fast:
+        grads, bias_rows, lowered, collected = middle_backward(
+            joined, grad_attended, offset, col, logit, hidden, full_down, gated, grad_branch, head_size, scale, 5
+        )
+        grad_normed_attn, share_attn, grad_out = last_backward(
+            grads, grad_gate_pre, normed_attn, full_attn, collected, 6
+        )
+        grad_out = grad_out.astype(jnp.float32)
+    else:
+        grads, bias_rows = attention_bwd(joined, grad_attended, offset, col, logit, head_size, scale)
+        grad_projected = jnp.concatenate([grads, grad_gate_pre], axis=1)
+        share_attn = scatter(product_tn(normed_attn, grad_projected).astype(low), "wshard")
+        grad_normed_attn = scatter(product_nt(grad_projected, full_attn).astype(low), "seq").astype(jnp.float32)
+        lowered = scatter(product(hidden, full_down).astype(low), "seq").astype(jnp.float32)
+        share_out = scatter(product_tn(gated, grad_branch).astype(low), "wshard")
+        rows_out = columns // shards
+        pieces_out = lax.all_gather(share_out, "seq", axis=0, tiled=False)
+        takes = shards // per_block
+        slots_out = jnp.where(
+            (jnp.arange(per_block) == shard_rank // takes)[None, :, None, None],
+            pieces_out[:, None],
+            jnp.zeros((), low),
+        ).reshape(shards, rows_out, width)
+        moved = lax.all_to_all(slots_out, "wshard", split_axis=0, concat_axis=0, tiled=True)
+        moved = moved.reshape(per_block, takes, rows_out, width)
+        mine_out = lax.dynamic_index_in_dim(moved, shard_rank % per_block, 0, keepdims=False)
+        grad_out = mine_out.reshape(columns // per_block, width).astype(jnp.float32)
+    layer_output = (middle + lowered).astype(low)[None]
     grad_bias = lax.dynamic_update_slice_in_dim(
-        jnp.zeros((heads,), jnp.float32), grad_bias_local, seq_rank * local_heads, 0
-    )
-    grad_projected = jnp.concatenate(
-        [dq[:, :columns], dk[:, :columns], dv[:, :columns], grad_forget, grad_gate_pre], axis=1
-    )
-    grad_w_attn = product_tn(normed_attn, grad_projected).astype(low)
-    share_attn = scatter(grad_w_attn, "wshard")
-    front = full_attn.shape[1]
-    grad_normed_attn = multiply_scatter(
-        [grad_projected[:, :front], grad_gate_pre], [full_attn, full_ogate], True, 5
+        jnp.zeros((heads,), jnp.float32), bias_rows[:local_heads, 0], seq_rank * local_heads, 0
     )
     unused_normed, pull_attn_norm = jax.vjp(rms_norm, inputs, norm_attn)
     grad_input_part, grad_norm_attn = pull_attn_norm(grad_normed_attn)
     grad_input = (grad_middle + grad_input_part)[None]
-    lowered = multiply_scatter([hidden], [full_down], False, 6)
-    layer_output = (middle + lowered).astype(low)[None]
-
-    share_out = scatter(grad_w_out, "wshard")
-    rows_out = columns // shards
-    pieces_out = lax.all_gather(share_out, "seq", axis=0, tiled=False)
-    lane_of = shard_rank // (shards // per_block)
-    slots_out = jnp.where(
-        (jnp.arange(per_block) == lane_of)[None, :, None, None], pieces_out[:, None], jnp.zeros((), low)
-    ).reshape(shards, rows_out, width)
-    moved = lax.all_to_all(slots_out, "wshard", split_axis=0, concat_axis=0, tiled=True)
-    moved = moved.reshape(per_block, shards // per_block, rows_out, width)
-    mine_out = lax.dynamic_index_in_dim(moved, shard_rank % per_block, 0, keepdims=False)
-    grad_out = mine_out.reshape(columns // per_block, width).astype(jnp.float32)
 
     rows = share_attn.shape[0]
     if fast:
-        every_ffn, grad_down = gather_square([share_ffn, share_down], 7)
-        every_attn = gather_square([share_attn], 8)[0]
+        vector = jnp.concatenate([grad_norm_attn, grad_norm_ffn, grad_bias])
+        vector = jnp.pad(vector, (0, -vector.shape[0] % 1024)).reshape(-1, 128)
+        every_attn, every_ffn, grad_down, vector = last_gather([share_attn, share_ffn, share_down], vector, 7)
+        vector = vector.reshape(-1)
+        small = vector[:width], vector[width : 2 * width], vector[2 * width : 2 * width + heads]
     else:
-        every_ffn, grad_down, every_attn = [gather(v, "seq") for v in (share_ffn, share_down, share_attn)]
+        every_attn, every_ffn, grad_down = [gather(v, "seq") for v in (share_attn, share_ffn, share_down)]
+        small = lax.psum((grad_norm_attn, grad_norm_ffn, grad_bias), ("seq", "wshard"))
     every_ffn = every_ffn.reshape((groups,) + share_ffn.shape)
     every_attn = every_attn.reshape((groups,) + share_attn.shape)
+    starts = (0, lanes, 2 * lanes, front)
     if fast:
         grad_w_gate, grad_w_up, grad_down = join_units(every_ffn, grad_down, part)
-        grads = join_columns(every_attn, columns, (0, columns, 2 * columns, front))
-        vector = jnp.concatenate([grad_norm_attn, grad_norm_ffn, grad_bias])
-        vector = jnp.pad(vector, (0, -vector.shape[0] % 1024)).reshape(-1, 128)
-        vector = add_everywhere(vector, 9).reshape(-1)
-        small = vector[:width], vector[width : 2 * width], vector[2 * width : 2 * width + heads]
+        weight_grads = join_columns(every_attn, columns, starts)
     else:
 
         def join(first):
@@ -998,18 +1571,17 @@
             taken = taken.reshape(groups, rows, shards, part).transpose(1, 2, 0, 3)
             return taken.reshape(rows, hidden_size).astype(jnp.float32)
 
-        grads = [join(first) for first in (0, columns, 2 * columns, front)]
+        weight_grads = [join(first) for first in starts]
         grad_w_gate, grad_w_up = join_own_units(0), join_own_units(1)
         grad_down = grad_down.astype(jnp.float32)
-        small = lax.psum((grad_norm_attn, grad_norm_ffn, grad_bias), ("seq", "wshard"))
-
-    grad_forget_w = every_attn[:, :, 3 * columns : 3 * columns + local_heads]
+
+    grad_forget_w = every_attn[:, :, 3 * lanes : 3 * lanes + local_heads]
     grad_forget_w = grad_forget_w.transpose(1, 0, 2).reshape(rows, heads).astype(jnp.float32)
     return (
         layer_output,
         grad_input,
         small[0],
-        *grads,
+        *weight_grads,
         grad_forget_w,
         small[2],
         grad_out,

time: 605 us -> 526 us (0.87)
  waiting for transfers between devices: 53.9 us -> 0.77 us
  Pallas kernels: 401 us -> 432 us
  local copies, waits for them, and re-layouts: 34.4 us -> 15.2 us
  other arithmetic: 39.9 us -> 26.9 us
  blocking collectives: 10.3 us -> 0 us
    pallas_call x6 -> x5, Pallas kernels: 172 us -> 267 us  [the longest x1 72.3 us: last_gather(): pl.pallas_call(body, in_specs=[vmem] * (count + 1), out_specs=[pl.BlockSp...]
    pallas_call x4 -> x2, Pallas kernels: 147 us -> 84 us  [product_scatter(): pl.pallas_call(body, in_specs=[vmem] * (2 * count + 2 * more), out_specs=...]
    reduce_scatter x4 -> x2, waiting for transfers between devices: 52.2 us -> 0.01 us  [scatter(): return lax.psum_scatter(value, axis_name, scatter_dimension=0, tiled=True)]
    all_gather x1 -> x0, blocking collectives: 10.3 us -> none  [on_device(): pieces_out = lax.all_gather(share_out, 'seq', axis=0, tiled=False)]
    dynamic_slice x6 -> x0, local copies, waits for them, and re-layouts: 9.36 us -> none  [the longest x2 4.7 us: own_units(): mine = lax.dynamic_index_in_dim(split, seq_rank, 2, keepdims=False)]
    reshape x7 -> x0, local copies, waits for them, and re-layouts: 7.58 us -> none  [the longest x2 5.66 us: own_units(): split = weight.reshape(weight.shape[0], shards, groups, part)]
    dot_general x2 -> x1, matrix products: 12.4 us -> 5.49 us  [product_tn(): lax.dot_general(left, right, (((0,), (0,)), ((), ())), preferred_element_...]
  transfers between devices with their start and end apart: 8 -> 4, of which waited for: 2 -> 0; matrix products, arithmetic and copies ran while one was open for 13% -> 7% of each run, Pallas kernels for 36% -> 55%
where the time goes in v4:
time: 526 us; the launch traced here: 522 us
  Pallas kernels  432 us (82%)
  matrix products  31.4 us (6%)
  other arithmetic  26.9 us (5%)
  local copies, waits for them, and re-layouts  15.2 us (3%)
  between operations  14.9 us (3%)
    pallas_call x2, Pallas kernels, product_scatter(): pl.pallas_call(body, in_specs=[vmem] * (2 * count + 2 * more), out_specs=...  84 us
    pallas_call x1, Pallas kernels, last_gather(): pl.pallas_call(body, in_specs=[vmem] * (count + 1), out_specs=[pl.BlockSp...  72.3 us
    pallas_call x2, Pallas kernels, gather_product(): pl.pallas_call(body, in_specs=[vmem, vmem], out_specs=[vmem, vmem], out_s...  69.9 us
    pallas_call x1, Pallas kernels, last_backward(): pl.pallas_call(body, in_specs=[vmem] * 5, out_specs=[vmem] * 3, out_shape...  63.1 us
    pallas_call x1, Pallas kernels, first_gather(): pl.pallas_call(body, in_specs=[vmem] * 4 + [anywhere] * 2, out_specs=[any...  61.6 us
    pallas_call x1, Pallas kernels, middle_backward(): pl.pallas_call(body, in_specs=[vmem] * 9, out_specs=[vmem] * 4, out_shape...  55.6 us
    pallas_call x1, Pallas kernels, attention_fwd(): pl.pallas_call(body, grid=(pairs,), in_specs=[pl.BlockSpec(memory_space=p...  15 us
    dot_general x2, matrix products, product(): return jnp.dot(left, right, preferred_element_type=jnp.float32)  13.6 us
  transfers between devices with their start and end apart: 4, of which 0 were waited for; matrix products, arithmetic and copies ran while one was open for 7% of the time, Pallas kernels for 55%

profile of v4, /device:TPU:0, one launch (start us, length us, event | category | flops | bytes accessed | tf_op | source)
XLA Modules:
  0.0 521.5 jit_solution(6553274705626056961)
XLA Ops:
  7.2 0.0 copy-start
  7.2 0.0 copy-start.6
  7.2 0.0 all-gather.5.cloned.1.call-start
  7.3 0.9 constant_dynamic-slice_fusion.1
  8.1 0.1 copy.37
  8.9 1.4 fusion.19
  10.3 0.0 copy-start.12
  10.3 1.7 dynamic-slice_dynamic-update-slice_fusion.3
  12.0 1.6 dynamic-slice_dynamic-update-slice_fusion.2
  13.6 1.6 dynamic-slice_dynamic-update-slice_fusion.1
  15.2 0.6 pad_dynamic-update-slice_fusion
  15.8 1.6 dynamic-slice_dynamic-update-slice_fusion.weights_ref
  17.4 1.0 bitcast_select_fusion.second_ref
  18.4 1.1 fusion.11.first_ref
  19.5 0.8 constant_dynamic-slice_fusion
  20.3 61.6 %first_gather.1 = (bf16[1024,1536]{1,0:T(8,128)(2,1)}, bf16[1024,1536]{1,0:T(8,128)(2,1)}, bf16[1536,1664]{1,0:T(8,128)(2,1)}, bf16[2,192,1536]{2,1,0:T(8,128)(2,1)}, bf16[192,2048]{1,0:T(8,128)(2,1)}) custom-call(bf16[256,1536]{1,0:T(8,128)(2,1)} %fusion.11.first_ref, bf16[256,1536]{1,0:T(8,128)(2,1)} %bitcast_select_fusion.second_ref, ...), custom_call_target="tpu_custom_call" | custom-call | tf_op jit(solution)/shard_map/first_gather/pallas_call | solution.py:677
  81.9 0.0 all-gather.5.cloned.1.call-update
  81.9 0.0 all-gather.3.cloned.1.call-start
  82.0 0.7 all-gather.3.cloned.1.call-update
  82.7 0.0 reduce-scatter.5.cloned.1.call-start
  82.7 0.1 dynamic_slice.26
  82.8 0.5 pad_bitcast_fusion.bias_ref
  83.3 8.8 %fusion.6.q_ref.k_ref.v_ref.f_ref.joined_ref = bf16[1024,1280]{1,0:T(8,128)(2,1)} fusion(bf16[1024,1536]{1,0:T(8,128)(2,1)} %get-tuple-element.50.normed_ref, bf16[1536,1664]{1,0:T(8,128)(2,1)} %get-tuple-element.51.weights_ref), kind=kOutput, calls=%fused_computation.11 | convolution fusion | flops 4027842560 | bytes 9699328 | tf_op jit(solution)/shard_map/dot_general | solution.py:14
  92.1 15.0 %attention_fwd.1 = (bf16[1024,384]{1,0:T(8,128)(2,1)}, f32[8,1024]{1,0:T(8,128)}, f32[1024,128]{1,0:T(8,128)}, f32[8,1024]{1,0:T(8,128)}) custom-call(s32[1]{0:T(128)} %copy.43.length_ref, bf16[1024,1280]{1,0:T(8,128)(2,1)} %fusion.6.q_ref.k_ref.v_ref.f_ref.joined_ref, bf16[1024,1280]{1,0:T(8,128)(2,1)} %fusion.6.q_ref.k_ref.v_ref.f_ref.joined_ref, ...), custom_call_target="tpu_custom_call" | custom-call | flops 1610612736 | bytes 3145728 | tf_op jit(solution)/shard_map/attention_fwd/pallas_call | solution.py:112
  107.1 4.8 fusion.13
  111.9 43.9 %product_scatter.2 = f32[256,1536]{1,0:T(8,128)} custom-call(bf16[1024,384]{1,0:T(8,128)(2,1)} %get-tuple-element.101.refs_0_.gated_ref, bf16[384,1536]{1,0:T(8,128)(2,1)} %bitcast.43), custom_call_target="tpu_custom_call" | custom-call | tf_op jit(solution)/shard_map/product_scatter/pallas_call | solution.py:1239
  155.8 0.0 copy-start.11
  155.8 1.9 multiply_reduce_fusion.2
  157.7 0.0 copy-done.11
  157.8 1.1 multiply_convert_fusion.3.own_ref
  158.8 37.3 %gather_product.2 = (bf16[1024,1536]{1,0:T(8,128)(2,1)}, f32[1024,2048]{1,0:T(8,128)}) custom-call(bf16[256,1536]{1,0:T(8,128)(2,1)} %multiply_convert_fusion.3.own_ref, bf16[1536,2048]{1,0:T(8,128)(2,1)} %all-gather.5.cloned.1.call-done.weight_ref.refs_1_), custom_call_target="tpu_custom_call" | custom-call | tf_op jit(solution)/shard_map/gather_product/pallas_call | solution.py:429
  196.1 0.0 all-gather.3.cloned.1.call-done.down_ref
  196.2 12.3 %fusion.2 = (bf16[1024,1024]{1,0:T(8,128)(2,1)}, bf16[1024,1024]{1,0:T(8,128)(2,1)}, bf16[1024,1024]{1,0:T(8,128)(2,1)S(1)}) fusion(f32[1024,2048]{1,0:T(8,128)} %get-tuple-element.58, bf16[1024,1536]{1,0:T(8,128)(2,1)} %get-tuple-element.54, bf16[1024,1536]{1,0:T(8,128)(2,1)} %all-gather.3.cloned.1.call-done.down_ref), kind=kOutput, calls=%fused_computation.3 | convolution fusion | flops 3238002688 | bytes 20971520 | tf_op jit(solution)/shard_map/dot_general | solution.py:24
  208.5 1.3 copy-done.10
  209.8 5.5 %convolution_convert_fusion = bf16[1024,1536]{1,0:T(8,128)(2,1)} fusion(bf16[1024,1024]{1,0:T(8,128)(2,1)S(1)} %get-tuple-element.94.hidden_ref, bf16[1024,1536]{1,0:T(8,128)(2,1)S(1)} %copy-done.15), kind=kOutput, calls=%fused_computation.12 | convolution fusion | flops 3222798336 | bytes 8388608 | tf_op jit(solution)/shard_map/dot_general | solution.py:18
  215.3 0.0 reduce-scatter.5.cloned.1.call-update
  215.3 0.0 reduce-scatter.3.cloned.1.call-start
  215.4 4.7 pad_maximum_fusion.refs_0_.refs_3_
  220.1 40.1 %product_scatter.3 = (f32[256,1536]{1,0:T(8,128)}, bf16[1536,2048]{1,0:T(8,128)(2,1)}) custom-call(bf16[1024,2048]{1,0:T(8,128)(2,1)} %pad_maximum_fusion.refs_0_.refs_3_, bf16[1536,2048]{1,0:T(8,128)(2,1)} %all-gather.5.cloned.1.call-done.weight_ref.refs_1_, bf16[1024,1536]{1,0:T(8,128)(2,1)} %get-tuple-element.60.refs_2_, ...), custom_call_target="tpu_custom_call" | custom-call | tf_op jit(solution)/shard_map/product_scatter/pallas_call | solution.py:1239
  260.2 0.0 reduce-scatter.3.cloned.1.call-update
  260.2 1.4 copy-done.4
  261.6 0.4 multiply_reduce_fusion
  262.0 0.7 copy-done.7
  262.7 1.4 fusion.26.own_ref
  264.1 32.6 %gather_product.3 = (bf16[1024,1536]{1,0:T(8,128)(2,1)}, f32[1024,384]{1,0:T(8,128)}) custom-call(bf16[256,1536]{1,0:T(8,128)(2,1)} %fusion.26.own_ref, bf16[384,1536]{1,0:T(8,128)(2,1)} %bitcast.44), custom_call_target="tpu_custom_call" | custom-call | tf_op jit(solution)/shard_map/gather_product/pallas_call | solution.py:429
  296.7 3.7 fusion.15
  300.4 55.6 %middle_backward.1 = (bf16[1024,1280]{1,0:T(8,128)(2,1)}, f32[8,128]{1,0:T(8,128)}, f32[256,1536]{1,0:T(8,128)}, bf16[192,1536]{1,0:T(8,128)(2,1)}) custom-call(bf16[1024,1280]{1,0:T(8,128)(2,1)} %fusion.6.q_ref.k_ref.v_ref.f_ref.joined_ref, bf16[1024,384]{1,0:T(8,128)(2,1)} %get-tuple-element.96.d_out_ref, f32[8,1024]{1,0:T(8,128)} %get-tuple-element.63.offset_ref, ...), custom_call_target="tpu_custom_call" | custom-call | tf_op jit(solution)/shard_map/middle_backward/pallas_call | solution.py:1298
  356.0 63.1 %last_backward.1 = (f32[256,1536]{1,0:T(8,128)}, bf16[192,1664]{1,0:T(8,128)(2,1)}, bf16[192,1536]{1,0:T(8,128)(2,1)}) custom-call(bf16[1024,1280]{1,0:T(8,128)(2,1)} %get-tuple-element.68.grads_ref, bf16[1024,384]{1,0:T(8,128)(2,1)} %get-tuple-element.95.gate_ref, bf16[1024,1536]{1,0:T(8,128)(2,1)} %get-tuple-element.50.normed_ref, ...), custom_call_target="tpu_custom_call" | custom-call | tf_op jit(solution)/shard_map/last_backward/pallas_call | solution.py:1358
  419.0 0.0 copy-start.14
  419.0 0.0 copy-start.3
  419.0 2.3 convert_element_type.85
  421.3 0.1 slice_reduce_fusion
  421.5 0.2 dynamic_update_slice.3
  421.7 2.0 fusion.12
  423.7 0.6 fusion.23.refs_3_
  424.3 4.3 fusion.18
  428.7 72.3 %last_gather.1 = (bf16[768,1664]{1,0:T(8,128)(2,1)}, bf16[768,2048]{1,0:T(8,128)(2,1)}, bf16[512,1536]{1,0:T(8,128)(2,1)}, f32[32,128]{1,0:T(8,128)}) custom-call(bf16[192,1664]{1,0:T(8,128)(2,1)} %get-tuple-element.71.refs_0_, bf16[192,2048]{1,0:T(8,128)(2,1)} %reduce-scatter.3.cloned.1.call-done.refs_1_, ...), custom_call_target="tpu_custom_call" | custom-call | tf_op jit(solution)/shard_map/last_gather/pallas_call | solution.py:778
  501.0 4.4 join_columns.1
  505.4 1.0 convert_bitcast_fusion
  506.3 0.2 copy.35
  506.5 0.6 reshape.101
  507.1 0.6 slice_bitcast_fusion
  507.7 0.5 slice.45
  508.3 6.5 %join_units.1 = (f32[192,4096]{1,0:T(8,128)}, f32[192,4096]{1,0:T(8,128)}, f32[512,1536]{1,0:T(8,128)}) custom-call(bf16[4,192,2048]{2,1,0:T(8,128)(2,1)} %bitcast.45, bf16[512,1536]{1,0:T(8,128)(2,1)} %get-tuple-element.82.down_ref), custom_call_target="tpu_custom_call" | custom-call | tf_op jit(solution)/shard_map/join_units/pallas_call | solution.py:818
  (33 shorter events, 0.1 us)
Async XLA Ops:
  7.2 12.4 %copy-start = (bf16[512,1536]{1,0:T(8,128)(2,1)S(1)}, bf16[512,1536]{1,0:T(8,128)(2,1)}, u32[]{:S(2)}) copy-start(bf16[512,1536]{1,0:T(8,128)(2,1)} %param.28) | copy-start | bytes 4718596
  7.2 10.2 %copy-start.6 = (bf16[1,256,1536]{2,1,0:T(8,128)(2,1)S(1)}, bf16[1,256,1536]{2,1,0:T(8,128)(2,1)}, u32[]{:S(2)}) copy-start(bf16[1,256,1536]{2,1,0:T(8,128)(2,1)} %param.29) | copy-start | bytes 2359300
  7.2 151.6 %all-gather.5.cloned.1.call-start = ((), (), s32[]{:S(2)}) async-start(), calls=%async_computation.3 | async-start | bytes 7077888 | tf_op jit(solution)/shard_map/all_gather | solution.py:1382
  10.3 8.1 %copy-start.2 = (bf16[1,256,1536]{2,1,0:T(8,128)(2,1)S(1)}, bf16[1,256,1536]{2,1,0:T(8,128)(2,1)}, u32[]{:S(2)}) copy-start(bf16[1,256,1536]{2,1,0:T(8,128)(2,1)} %param.15) | copy-start | bytes 2359300
  10.3 8.1 %copy-start.12 = (f32[1536]{0:T(1024)S(1)}, f32[1536]{0:T(1024)}, u32[]{:S(2)}) copy-start(f32[1536]{0:T(1024)} %param.17) | copy-start | bytes 18436
  20.3 62.4 %copy-start.16 = (f32[24]{0:T(128)S(1)}, f32[24]{0:T(128)}, u32[]{:S(2)}) copy-start(f32[24]{0:T(128)} %param.23) | copy-start | bytes 292
  81.9 114.2 %all-gather.3.cloned.1.call-start = ((), (), s32[]{:S(2)}) async-start(), calls=%async_computation.2 | async-start | bytes 3538944 | tf_op jit(solution)/shard_map/all_gather | solution.py:1382
  82.7 346.0 %reduce-scatter.5.cloned.1.call-start = ((), (), s32[]{:S(2)}) async-start(), calls=%async_computation.5 | async-start | bytes 3538944 | tf_op jit(solution)/shard_map/reduce_scatter | solution.py:1386
  92.1 15.0 %copy-start.9 = (bf16[1024,1536]{1,0:T(8,128)(2,1)S(1)}, bf16[1024,1536]{1,0:T(8,128)(2,1)}, u32[]{:S(2)}) copy-start(bf16[1024,1536]{1,0:T(8,128)(2,1)} %get-tuple-element.50.normed_ref) | copy-start | bytes 9437188
  155.8 1.9 copy-start.11
  196.2 13.6 %copy-start.15 = (bf16[1024,1536]{1,0:T(8,128)(2,1)S(1)}, bf16[1024,1536]{1,0:T(8,128)(2,1)}, u32[]{:S(2)}) copy-start(bf16[1024,1536]{1,0:T(8,128)(2,1)} %get-tuple-element.54) | copy-start | bytes 9437188
  208.4 1.3 copy-start.10
  215.3 213.4 %reduce-scatter.3.cloned.1.call-start = ((), (), s32[]{:S(2)}) async-start(), calls=%async_computation.4 | async-start | bytes 7077888 | tf_op jit(solution)/shard_map/reduce_scatter | solution.py:1386
  260.2 1.4 copy-start.4
  261.6 1.1 copy-start.7
  419.0 2.3 copy-start.14
  419.0 2.7 copy-start.3
  421.3 3.0 copy-start.8
  421.7 2.6 copy-start.5
  501.0 6.2 %copy-start.13 = (f32[32,128]{1,0:T(8,128)S(1)}, f32[32,128]{1,0:T(8,128)}, u32[]{:S(2)}) copy-start(f32[32,128]{1,0:T(8,128)} %get-tuple-element.74) | copy-start | bytes 49156
  508.3 6.5 %copy-start.1 = (bf16[512,1536]{1,0:T(8,128)(2,1)S(1)}, bf16[512,1536]{1,0:T(8,128)(2,1)}, u32[]{:S(2)}) copy-start(bf16[512,1536]{1,0:T(8,128)(2,1)} %param.28) | copy-start | bytes 4718596
Sparse Core Ops, SparseCore 0:
  82.0 73.8 all-gather.4
  158.1 36.9 all-gather.2
  215.4 38.5 reduce-scatter.4
  260.3 79.0 reduce-scatter.2

commit v5 on v4

--- a/solution.py
+++ b/solution.py
@@ -47,93 +47,106 @@
     return jnp.dot(left, right, precision=lax.Precision.HIGHEST, preferred_element_type=jnp.float32)
 
 
-def attention_fwd(joined, bias, length, head_size, scale):
-    slots = joined.shape[0]
-    pairs = (joined.shape[1] // PAIR - 1) // 3
-    tile = min(256, slots)
+class Forward:
     some = 8
 
-    def body(length_ref, q_ref, k_ref, v_ref, f_ref, bias_ref, o_ref, offset_ref, col_ref, logit_ref, row):
-        pair = pl.program_id(0)
-
-        @pl.when(pair == 0)
-        def _():
-            logits = f_ref[...].astype(jnp.float32) + bias_ref[...]
-            logit_rows = logits.T[:some]
-            logit_ref[...] = logit_rows
-            logs = jnp.minimum(logit_rows, 0.0) - jnp.log1p(jnp.exp(-jnp.abs(logit_rows)))
-            ones = low_triangle(tile).astype(jnp.float32)
-            carry = jnp.zeros((some, 1), jnp.float32)
-            for first in range(0, slots, tile):
-                sums = exact(logs[:, first : first + tile], ones) + carry
-                row[:, first : first + tile] = sums
-                carry = sums[:, tile - 1 : tile]
-            wide = jnp.concatenate([row[...], jnp.zeros((PAIR - some, slots), jnp.float32)], axis=0).T
-            usable = lax.broadcasted_iota(jnp.int32, (slots, PAIR), 0) < length_ref[0]
-            col_ref[...] = jnp.where(usable, wide, -NEG_FILL)
-
-        key_all = k_ref[...]
-        value_t = v_ref[...].T
-        query_t = (q_ref[...].astype(jnp.float32) * scale).astype(jnp.bfloat16).T
+    def __init__(self, joined, bias, length, attended, offset, col, logit, row, head_size, scale):
+        self.joined, self.bias, self.length = joined, bias, length
+        self.attended, self.offset, self.col, self.logit, self.row = attended, offset, col, logit, row
+        self.head_size, self.scale = head_size, scale
+        self.slots = joined.shape[0]
+        self.pairs = (joined.shape[1] // PAIR - 1) // 3
+        self.tile = min(256, self.slots)
+
+    @staticmethod
+    def results(slots, pairs):
+        rows = jax.ShapeDtypeStruct((Forward.some, slots), jnp.float32)
+        return [
+            jax.ShapeDtypeStruct((slots, pairs * PAIR), jnp.bfloat16),
+            rows,
+            jax.ShapeDtypeStruct((slots, PAIR), jnp.float32),
+            rows,
+        ]
+
+    def lanes(self, pair, part=0):
+        return pl.ds(pl.multiple_of((part * self.pairs + pair) * PAIR, PAIR), PAIR)
+
+    def start(self):
+        slots, tile, some = self.slots, self.tile, self.some
+        logits = self.joined[:, 3 * self.pairs * PAIR :].astype(jnp.float32) + self.bias[...]
+        logit_rows = logits.T[:some]
+        self.logit[...] = logit_rows
+        logs = jnp.minimum(logit_rows, 0.0) - jnp.log1p(jnp.exp(-jnp.abs(logit_rows)))
+        ones = low_triangle(tile).astype(jnp.float32)
+        carry = jnp.zeros((some, 1), jnp.float32)
+        for first in range(0, slots, tile):
+            sums = exact(logs[:, first : first + tile], ones) + carry
+            self.row[:, first : first + tile] = sums
+            carry = sums[:, tile - 1 : tile]
+        wide = jnp.concatenate([self.row[...], jnp.zeros((PAIR - some, slots), jnp.float32)], axis=0).T
+        usable = lax.broadcasted_iota(jnp.int32, (slots, PAIR), 0) < self.length[...]
+        self.col[...] = jnp.where(usable, wide, -NEG_FILL)
+
+    def pair(self, pair):
+        slots, tile, half = self.slots, self.tile, self.head_size
+        key_all = self.joined[:, self.lanes(pair, 1)]
+        value_t = self.joined[:, self.lanes(pair, 2)].T
+        query_t = (self.joined[:, self.lanes(pair)].astype(jnp.float32) * self.scale).astype(jnp.bfloat16).T
         sub = lax.broadcasted_iota(jnp.int32, (PAIR, tile), 0)
-        lanes = lax.broadcasted_iota(jnp.int32, (slots, PAIR), 1)
+        wide = lax.broadcasted_iota(jnp.int32, (slots, PAIR), 1)
         diag = low_triangle(tile)
         columns = [
-            jnp.sum(jnp.where(lanes == 2 * pair + a, col_ref[...], 0.0), axis=1, keepdims=True) for a in range(2)
+            jnp.sum(jnp.where(wide == 2 * pair + a, self.col[...], 0.0), axis=1, keepdims=True) for a in range(2)
         ]
         for number in range(slots // tile):
             first, last = number * tile, (number + 1) * tile
             outs = []
             for a in range(2):
-                mine = (sub >= a * head_size) & (sub < (a + 1) * head_size)
+                mine = (sub >= a * half) & (sub < (a + 1) * half)
+                at = pl.ds(2 * pair + a, 1)
                 query = jnp.where(mine, query_t[:, first:last], jnp.zeros((), query_t.dtype))
                 scores = product(key_all[:last], query)
-                own_row = row[pl.ds(2 * pair + a, 1), first:last]
+                own_row = self.row[at, first:last]
                 scores = scores + (own_row - columns[a][:last])
                 tail = jnp.where(diag, scores[first:], NEG_FILL)
                 scores = tail if number == 0 else jnp.concatenate([scores[:first], tail], axis=0)
                 top = jnp.max(scores, axis=0, keepdims=True)
                 weights = jnp.exp(scores - top)
                 total = jnp.sum(weights, axis=0, keepdims=True)
-                mixed = product(
-                    value_t[a * head_size : (a + 1) * head_size, :last], weights.astype(jnp.bfloat16)
-                )
+                mixed = product(value_t[a * half : (a + 1) * half, :last], weights.astype(jnp.bfloat16))
                 outs.append(mixed / total)
-                offset_ref[pl.ds(2 * pair + a, 1), first:last] = own_row - (top + jnp.log(total))
-            o_ref[first:last, :] = jnp.concatenate(outs, axis=0).T.astype(o_ref.dtype)
-
-    def lane(start):
-        return pl.BlockSpec((slots, PAIR), lambda p, start=start: (0, start + p))
-
-    def fixed(shape):
-        return pl.BlockSpec(shape, lambda p: (0, 0))
-
-    rows = jax.ShapeDtypeStruct((some, slots), jnp.float32)
+                self.offset[at, first:last] = own_row - (top + jnp.log(total))
+            self.attended[first:last, self.lanes(pair)] = jnp.concatenate(outs, axis=0).T.astype(jnp.bfloat16)
+
+
+def attention_fwd(joined, bias, length, head_size, scale):
+    slots = joined.shape[0]
+    pairs = (joined.shape[1] // PAIR - 1) // 3
+
+    def body(joined_ref, bias_ref, length_ref, attended, offset, col, logit, row):
+        work = Forward(joined_ref, bias_ref, length_ref, attended, offset, col, logit, row, head_size, scale)
+        work.start()
+        offset[...] = jnp.zeros_like(offset)
+
+        def step(pair, carry):
+            work.pair(pair)
+            return carry
+
+        lax.fori_loop(0, pairs, step, 0)
+
+    vmem = pl.BlockSpec(memory_space=pltpu.VMEM)
     return pl.pallas_call(
         body,
-        grid=(pairs,),
-        in_specs=[
-            pl.BlockSpec(memory_space=pltpu.SMEM),
-            lane(0),
-            lane(pairs),
-            lane(2 * pairs),
-            pl.BlockSpec((slots, PAIR), lambda p: (0, 3 * pairs)),
-            fixed((1, PAIR)),
-        ],
-        out_specs=[lane(0), fixed((some, slots)), fixed((slots, PAIR)), fixed((some, slots))],
-        out_shape=[
-            jax.ShapeDtypeStruct((slots, pairs * PAIR), jnp.bfloat16),
-            rows,
-            jax.ShapeDtypeStruct((slots, PAIR), jnp.float32),
-            rows,
-        ],
-        scratch_shapes=[pltpu.VMEM((some, slots), jnp.float32)],
+        in_specs=[vmem] * 3,
+        out_specs=[vmem] * 4,
+        out_shape=Forward.results(slots, pairs),
+        scratch_shapes=[pltpu.VMEM((Forward.some, slots), jnp.float32)],
         compiler_params=pltpu.CompilerParams(vmem_limit_bytes=56 << 20),
         cost_estimate=pl.CostEstimate(
             flops=4 * slots * slots * pairs * PAIR, bytes_accessed=8 * slots * pairs * PAIR, transcendentals=0
         ),
         name="attention_fwd",
-    )(length, joined, joined, joined, joined, bias)
+    )(joined, bias, length)
 
 
 def backward_scratch(slots):
@@ -303,80 +316,46 @@
     def place(self, rank, part):
         return self.full.at[pl.ds(pl.multiple_of(rank * self.rows + part * self.half, self.half), self.half)]
 
-    def start(self):
+    def copy(self, index):
         me, side, down, across = sides()
         mine = [self.own.at[pl.ds(part * self.half, self.half)] for part in (0, 1)]
-        to_side, to_down = {"seq": side}, {"seq": down}
-        self.first = push(mine[0], self.place(me, 0), self.send.at[0], self.recv.at[0], to_side)
-        self.second = push(mine[1], self.place(me, 1), self.send.at[1], self.recv.at[1], to_down)
-        self.third = push(mine[1], self.place(me, 1), self.send.at[2], self.recv.at[2], to_side)
-        self.fourth = push(mine[0], self.place(me, 0), self.send.at[3], self.recv.at[3], to_down)
+        source, target, peer = (
+            (mine[0], self.place(me, 0), side),
+            (mine[1], self.place(me, 1), down),
+            (mine[1], self.place(me, 1), side),
+            (mine[0], self.place(me, 0), down),
+            (self.place(side, 0), self.place(side, 0), down),
+            (self.place(down, 1), self.place(down, 1), side),
+        )[index]
+        return pltpu.make_async_remote_copy(
+            src_ref=source,
+            dst_ref=target,
+            send_sem=self.send.at[index],
+            recv_sem=self.recv.at[index],
+            device_id={"seq": peer},
+            device_id_type=MESH,
+        )
+
+    def start(self):
+        for index in range(4):
+            self.copy(index).start()
 
     def relay(self):
-        me, side, down, across = sides()
-        self.first.wait_recv()
-        self.fifth = push(
-            self.place(side, 0), self.place(side, 0), self.send.at[4], self.recv.at[4], {"seq": down}
-        )
-        self.second.wait_recv()
-        self.sixth = push(
-            self.place(down, 1), self.place(down, 1), self.send.at[5], self.recv.at[5], {"seq": side}
-        )
+        for index in (0, 1):
+            self.copy(index).wait_recv()
+            self.copy(4 + index).start()
 
     def near(self):
-        self.third.wait_recv()
-        self.fourth.wait_recv()
+        self.copy(2).wait_recv()
+        self.copy(3).wait_recv()
 
     def far(self):
-        self.fifth.wait_recv()
-        self.sixth.wait_recv()
+        self.copy(4).wait_recv()
+        self.copy(5).wait_recv()
 
     def finish(self):
-        for copy in (self.first, self.second, self.third, self.fourth, self.fifth, self.sixth):
-            copy.wait_send()
-
-
-def gather_square(values, collective_id):
-    count = len(values)
-
-    def body(*refs):
-        own, full = refs[:count], refs[count : 2 * count]
-        send, recv, local = refs[2 * count :]
-        me, side, down, across = sides()
-        meet({"seq": side}, {"seq": down})
-        jobs = [SquareGather(own[i], full[i], send.at[i], recv.at[i]) for i in range(count)]
-        keeps = []
-        for i, job in enumerate(jobs):
-            job.start()
-            rows = own[i].shape[0]
-            keep = pltpu.make_async_copy(
-                own[i], full[i].at[pl.ds(pl.multiple_of(me * rows, rows), rows)], local.at[i]
-            )
-            keep.start()
-            keeps.append(keep)
-        for job in jobs:
-            job.relay()
-        for job, keep in zip(jobs, keeps):
-            job.near()
-            job.far()
-            job.finish()
-            keep.wait()
-
-    return pl.pallas_call(
-        body,
-        in_specs=[pl.BlockSpec(memory_space=pltpu.VMEM)] * count,
-        out_specs=[pl.BlockSpec(memory_space=pl.ANY)] * count,
-        out_shape=[jax.ShapeDtypeStruct((4 * v.shape[0],) + v.shape[1:], v.dtype) for v in values],
-        scratch_shapes=[
-            pltpu.SemaphoreType.DMA((count, 6)),
-            pltpu.SemaphoreType.DMA((count, 6)),
-            pltpu.SemaphoreType.DMA((count,)),
-        ],
-        compiler_params=pltpu.CompilerParams(
-            collective_id=collective_id, has_side_effects=True, vmem_limit_bytes=VMEM_LIMIT
-        ),
-        name="gather_square",
-    )(*values)
+        for index in range(6):
+            self.copy(index).wait_send()
 
 
 def block_product(left, right, transposed, tile, store):
@@ -385,9 +364,9 @@
     def step(number, carry):
         columns = pl.ds(pl.multiple_of(number * tile, tile), tile)
         if transposed:
-            store(columns, product_nt(left, right[columns, :]))
+            store(columns, product_nt(left[...], right[columns, :]))
         else:
-            store(columns, product(left, right[:, columns]))
+            store(columns, product(left[...], right[:, columns]))
         return carry
 
     lax.fori_loop(0, total // tile, step, 0)
@@ -467,9 +446,14 @@
 
 
 class LineGather:
-    def __init__(self, own, full, forth_send, back_send, twin_send, recv, local):
-        self.own, self.full, self.local = own, full, local
-        self.sends = (forth_send, back_send, twin_send)
+    @staticmethod
+    def scratch(chips):
+        dma = pltpu.SemaphoreType.DMA
+        return [dma((3, chips)), dma((2 * chips,)), dma((1,))]
+
+    def __init__(self, own, full, send, recv, local):
+        self.own, self.full, self.local = own, full, local.at[0]
+        self.sends = (send.at[0], send.at[1], send.at[2])
         self.recv = recv
         self.rows = own.shape[0]
         self.chips, self.chip, self.core, *self.devices = line()
@@ -554,6 +538,11 @@
 class LineSpread:
     pieces = 4
 
+    @staticmethod
+    def scratch():
+        dma = pltpu.SemaphoreType.DMA
+        return [dma((3, LineSpread.pieces)), dma((2, LineSpread.pieces))]
+
     def __init__(self, own, whole, send, recv):
         self.own, self.whole, self.send, self.recv = own, whole, send, recv
         self.rows = own.shape[0] // self.pieces
@@ -575,25 +564,23 @@
             device_id_type=MESH,
         )
 
-    def start(self):
-        @pl.when(self.chip == self.source)
+    def level(self, number, pieces):
+        @pl.when((self.chip == self.source + number) | (self.chip == self.source - number))
         def _():
-            self.whole[self.core] = self.own[...]
-
-    def step(self, piece):
-        @pl.when(self.chip != self.source)
-        def _():
-            self.copy(0, piece).wait_recv()
-
-        for way in (0, 1):
-
-            @pl.when(self.goes[way])
-            def _():
-                self.copy(way, piece).start()
-
-        self.copy(2, piece).start()
-
-    def finish(self):
+            if number == 0:
+                self.whole[self.core] = self.own[...]
+            for piece in pieces:
+                if number:
+                    self.copy(0, piece).wait_recv()
+                for way in (0, 1):
+
+                    @pl.when(self.goes[way])
+                    def _():
+                        self.copy(way, piece).start()
+
+                self.copy(2, piece).start()
+
+    def end(self):
         for piece in range(self.pieces):
             other = self.whole.at[1 - self.core, pl.ds(piece * self.rows, self.rows)]
             pltpu.make_async_remote_copy(
@@ -610,96 +597,6 @@
                 @pl.when(self.goes[way])
                 def _():
                     self.copy(way, piece).wait_send()
-
-
-def first_gather(first, second, weights, block, w_gate, w_up, part, collective_id):
-    rows, width = block.shape
-    shards = 2 * lax.axis_size("seq")
-    chips = shards // 2
-    units = w_gate.shape[1] // 4
-    blocks = units // part
-
-    def body(first_ref, second_ref, weights_ref, block_ref, gate_ref, up_ref,
-             first_full, second_full, weights_full, whole, picked,
-             send, recv, local, line_send, line_recv, spread_send, spread_recv, pick):
-        me, side, down, across = sides()
-        line_chips, chip, core, forth, back, twin = line()
-        meet({"seq": side}, {"seq": down}, forth, back, twin)
-        one = SquareGather(first_ref, first_full, send.at[0], recv.at[0])
-        two = SquareGather(second_ref, second_full, send.at[1], recv.at[1])
-        run = LineGather(
-            weights_ref, weights_full, line_send.at[0], line_send.at[1], line_send.at[2], line_recv, local.at[2]
-        )
-        spread = LineSpread(block_ref, whole, spread_send, spread_recv)
-        spread.start()
-        one.start()
-        run.start()
-        keeps = []
-        for index, (own, full) in enumerate(((first_ref, first_full), (second_ref, second_full))):
-            size = own.shape[0]
-            keep = pltpu.make_async_copy(
-                own, full.at[pl.ds(pl.multiple_of(me * size, size), size)], local.at[index]
-            )
-            keep.start()
-            keeps.append(keep)
-        two.start()
-        spread.step(0)
-        for index, source in enumerate((gate_ref, up_ref)):
-            for number in range(blocks):
-                column = pl.multiple_of((number * 4 + me) * part, part)
-                taken = pltpu.make_async_copy(
-                    source.at[:, pl.ds(column, part)],
-                    picked.at[:, pl.ds(index * units + number * part, part)],
-                    pick.at[index, number],
-                )
-                taken.start()
-                keeps.append(taken)
-        run.step(1)
-        one.relay()
-        spread.step(1)
-        run.step(2)
-        two.relay()
-        spread.step(2)
-        run.step(3)
-        spread.step(3)
-        for job in (one, two):
-            job.near()
-            job.far()
-            job.finish()
-        for keep in keeps:
-            keep.wait()
-        run.finish()
-        spread.finish()
-
-    vmem = pl.BlockSpec(memory_space=pltpu.VMEM)
-    anywhere = pl.BlockSpec(memory_space=pl.ANY)
-    dma = pltpu.SemaphoreType.DMA
-    return pl.pallas_call(
-        body,
-        in_specs=[vmem] * 4 + [anywhere] * 2,
-        out_specs=[anywhere] * 3 + [vmem] * 2,
-        out_shape=[
-            jax.ShapeDtypeStruct((4 * first.shape[0],) + first.shape[1:], first.dtype),
-            jax.ShapeDtypeStruct((4 * second.shape[0],) + second.shape[1:], second.dtype),
-            jax.ShapeDtypeStruct((shards * weights.shape[0],) + weights.shape[1:], weights.dtype),
-            jax.ShapeDtypeStruct((2, rows, width), block.dtype),
-            jax.ShapeDtypeStruct((w_gate.shape[0], 2 * units), w_gate.dtype),
-        ],
-        scratch_shapes=[
-            dma((2, 6)),
-            dma((2, 6)),
-            dma((3,)),
-            dma((3, chips)),
-            dma((shards,)),
-            dma((3, LineSpread.pieces)),
-            dma((2, LineSpread.pieces)),
-            dma((2, blocks)),
-        ],
-        compiler_params=pltpu.CompilerParams(
-            collective_id=collective_id, has_side_effects=True, vmem_limit_bytes=VMEM_LIMIT
-        ),
-        name="first_gather",
-    )(first, second, weights, block, w_gate, w_up)
 
 
 class Everywhere:
@@ -1316,22 +1213,23 @@
     )(joined, d_out, offset, col, logit, hidden, w_down, gated, grad_branch)
 
 
-def last_backward(grads, grad_gate_pre, normed, weights, collected, collective_id):
+def last_backward(grads, grad_gate_pre, normed, weights, gate_weights, collected, collective_id):
     slots, depth = normed.shape
     front = grads.shape[1]
-    lanes = weights.shape[1]
+    lanes = front + gate_weights.shape[1]
     tokens = slots // 4
     shards = 2 * lax.axis_size("seq")
     rows = depth // shards
 
-    def body(grads_ref, gate_ref, normed_ref, weights_ref, collected_ref, summed, share, spread_out, terms,
+    def body(grads_ref, gate_ref, normed_ref, weights_ref, gate_weights_ref, collected_ref,
+             summed, share, spread_out, terms,
              spread_send, spread_recv, *scratch):
         me, side, down, across = sides()
         chips, chip, core, forth, back, twin = line()
         meet({"seq": side}, {"seq": down}, forth, back, twin)
         job = SquareScatter(
             [grads_ref, gate_ref],
-            [weights_ref.at[:, pl.ds(0, front)], weights_ref.at[:, pl.ds(front, lanes - front)]],
+            [weights_ref, gate_weights_ref],
             True,
             summed,
             *scratch[:7],
@@ -1357,7 +1255,7 @@
     low = jnp.bfloat16
     return pl.pallas_call(
         body,
-        in_specs=[vmem] * 5,
+        in_specs=[vmem] * 6,
         out_specs=[vmem] * 3,
         out_shape=[
             jax.ShapeDtypeStruct((tokens, depth), jnp.float32),
@@ -1375,7 +1273,271 @@
             collective_id=collective_id, has_side_effects=True, vmem_limit_bytes=VMEM_LIMIT
         ),
         name="last_backward",
-    )(grads, grad_gate_pre, normed, weights, collected)
+    )(grads, grad_gate_pre, normed, weights, gate_weights, collected)
+
+
+def norm_rows(values, gain):
+    scale = lax.rsqrt(jnp.mean(values * values, axis=-1, keepdims=True) + EPS)
+    return scale, values * scale * gain
+
+
+def whole_forward(inputs, gain, cotangent, weights, forget, bias, length, block, w_gate, w_up,
+                  head_size, scale, collective_id):
+    rows, depth = inputs.shape
+    groups = 4
+    slots = groups * rows
+    chips = groups
+    shards = 2 * chips
+    mine = weights[0].shape[0]
+    columns = depth // groups
+    front = 3 * columns + PAIR
+    pairs = columns // PAIR
+    part = w_gate.shape[1] // (groups * shards)
+    units = shards * part
+    low = jnp.bfloat16
+
+    def body(inputs_ref, gain_ref, cot_ref, q_ref, k_ref, v_ref, og_ref, forget_ref, bias_ref, length_ref, block_ref,
+             gate_ref, up_ref,
+             normed, cot_full, full_front, full_gate, full_out, full_ffn, joined, attended, offset, col, logit,
+             gate_pre, gated, middle,
+             own_normed, own_front, own_gate, own_ffn, row, picks, cot_send, cot_recv, keep,
+             x_send, x_recv, *scratch):
+        me, side, down, across = sides()
+        line_chips, chip, core, forth, back, twin = line()
+        front_line = LineGather(own_front, full_front, *scratch[0:3])
+        gate_line = LineGather(own_gate, full_gate, *scratch[3:6])
+        ffn_line = LineGather(own_ffn, full_ffn, *scratch[6:9])
+        spread = LineSpread(block_ref, full_out, *scratch[9:11])
+        job = SquareScatter([gated], [full_out_rows(full_out)], False, middle, *scratch[11:18])
+        taken = []
+        my_columns = pl.ds(pl.multiple_of(me * columns, columns), columns)
+        for index, source in enumerate((q_ref, k_ref, v_ref)):
+            taken.append((source.at[:, my_columns], own_front.at[:, pl.ds(index * columns, columns)]))
+        taken.append((og_ref.at[:, my_columns], own_gate))
+        for index, source in enumerate((gate_ref, up_ref)):
+            for number in range(shards):
+                column = pl.ds(pl.multiple_of((number * groups + me) * part, part), part)
+                taken.append((source.at[:, column], own_ffn.at[:, pl.ds(index * units + number * part, part)]))
+        taken = [pltpu.make_async_copy(a, b, picks.at[i]) for i, (a, b) in enumerate(taken)]
+        for copy in taken:
+            copy.start()
+        values = inputs_ref[...].astype(jnp.float32)
+        own_normed[...] = norm_rows(values, gain_ref[...])[1].astype(low)
+        own_front[:, 3 * columns :] = forget_ref[...]
+        meet({"seq": side}, {"seq": down}, forth, back, twin)
+        one = SquareGather(own_normed, normed, x_send, x_recv)
+        two = SquareGather(cot_ref, cot_full, cot_send, cot_recv)
+        one.start()
+        for copy in taken:
+            copy.wait()
+        front_line.start()
+        at_me = pl.ds(pl.multiple_of(me * rows, rows), rows)
+        kept = pltpu.make_async_copy(cot_ref, cot_full.at[at_me], keep.at[0])
+        kept.start()
+        normed[at_me, :] = own_normed[...]
+        one.relay()
+        front_line.step(1)
+        front_line.step(2)
+        one.near()
+        one.far()
+        front_line.step(3)
+        front_line.finish()
+        one.finish()
+        spread.level(0, range(4))
+        gate_line.start()
+        two.start()
+
+        def store_joined(at_columns, value):
+            joined[:, at_columns] = value.astype(low)
+
+        block_product(normed, full_front, False, 256, store_joined)
+        spread.level(1, (0,))
+        work = Forward(joined, bias_ref, length_ref, attended, offset, col, logit, row, head_size, scale)
+        offset[...] = jnp.zeros_like(offset)
+        work.start()
+
+        def step(pair, carry):
+            work.pair(pair)
+
+            @pl.when(pair == 0)
+            def _():
+                spread.level(1, (1, 2))
+                spread.level(2, (0, 1))
+                gate_line.step(1)
+                two.relay()
+
+            @pl.when(pair == 1)
+            def _():
+                spread.level(1, (3,))
+                spread.level(2, (2, 3))
+                gate_line.step(2)
+
+            return carry
+
+        lax.fori_loop(0, pairs, step, 0)
+        ffn_line.start()
+        gate_line.step(3)
+        spread.level(3, range(4))
+        gate_line.finish()
+
+        def store_gate(at_columns, value):
+            gate_pre[:, at_columns] = value
+
+        block_product(normed, full_gate, False, PAIR, store_gate)
+        gated[...] = (attended[...].astype(jnp.float32) * jax.nn.sigmoid(gate_pre[...])).astype(low)
+        spread.end()
+        job.begin()
+        ffn_line.step(1)
+        job.relay()
+        job.own()
+        ffn_line.step(2)
+        two.near()
+        two.far()
+        two.finish()
+        kept.wait()
+        job.end()
+        middle[...] += inputs_ref[...].astype(jnp.float32)
+        ffn_line.step(3)
+        ffn_line.finish()
+
+    def shape(size, kind=low):
+        return jax.ShapeDtypeStruct(size, kind)
+
+    vmem = pl.BlockSpec(memory_space=pltpu.VMEM)
+    anywhere = pl.BlockSpec(memory_space=pl.ANY)
+    dma = pltpu.SemaphoreType.DMA
+    return pl.pallas_call(
+        body,
+        in_specs=[vmem] * 3 + [anywhere] * 4 + [vmem] * 4 + [anywhere] * 2,
+        out_specs=[vmem, anywhere, vmem, vmem, vmem, anywhere] + [vmem] * 8,
+        out_shape=[
+            shape((slots, depth)),
+            shape((slots, depth)),
+            shape((depth, front)),
+            shape((depth, columns)),
+            shape((2, block.shape[0], depth)),
+            shape((depth, 2 * units)),
+            shape((slots, front)),
+            *Forward.results(slots, pairs),
+            shape((slots, columns), jnp.float32),
+            shape((slots, columns)),
+            shape((rows, depth), jnp.float32),
+        ],
+        scratch_shapes=[
+            pltpu.VMEM((rows, depth), low),
+            pltpu.VMEM((mine, front), low),
+            pltpu.VMEM((mine, columns), low),
+            pltpu.VMEM((mine, 2 * units), low),
+            pltpu.VMEM((Forward.some, slots), jnp.float32),
+            dma((4 + 2 * shards,)),
+            dma((6,)),
+            dma((6,)),
+            dma((1,)),
+            dma((6,)),
+            dma((6,)),
+        ]
+        + 3 * LineGather.scratch(chips)
+        + LineSpread.scratch()
+        + SquareScatter.scratch(rows, depth),
+        compiler_params=pltpu.CompilerParams(
+            collective_id=collective_id, has_side_effects=True, vmem_limit_bytes=VMEM_LIMIT
+        ),
+        name="whole_forward",
+    )(inputs, gain, cotangent, *weights, forget, bias, length, block, w_gate, w_up)
+
+
+class full_out_rows:
+    def __init__(self, ref):
+        self.ref = ref
+        self.shape = (2 * ref.shape[1], ref.shape[2])
+
+    def __getitem__(self, index):
+        rows, columns = index
+        return jnp.concatenate([self.ref[0, :, columns], self.ref[1, :, columns]], axis=0)
+
+
+def feed_forward(middle, gain, weights, own_down, cotangent, collective_id):
+    rows, depth = middle.shape
+    slots = 4 * rows
+    units = weights.shape[1] // 2
+    chips = 4
+    low = jnp.bfloat16
+
+    def body(middle_ref, gain_ref, weights_ref, down_ref, cot_ref, normed, hidden, full_down, grads, terms,
+             own_normed, both, send, recv, *scratch):
+        me, side, down, across = sides()
+        line_chips, chip, core, forth, back, twin = line()
+        down_line = LineGather(down_ref, full_down, *scratch)
+        own_normed[...] = norm_rows(middle_ref[...], gain_ref[...])[1].astype(low)
+        meet({"seq": side}, {"seq": down}, forth, back, twin)
+        job = SquareGather(own_normed, normed, send, recv)
+        job.start()
+        down_line.start()
+
+        def ahead(rank):
+            at = pl.ds(pl.multiple_of(rank * rows, rows), rows)
+
+            def store(columns, value):
+                both[at, columns] = value
+
+            block_product(normed.at[at], weights_ref, False, 512, store)
+            gate, upward = both[at, :units], both[at, units:]
+            hidden[at, :] = (gate * jax.nn.sigmoid(gate) * upward).astype(low)
+
+        normed[pl.ds(pl.multiple_of(me * rows, rows), rows), :] = own_normed[...]
+        ahead(me)
+        job.relay()
+        down_line.step(1)
+        down_line.step(2)
+        job.near()
+        ahead(side)
+        ahead(down)
+        down_line.step(3)
+        job.far()
+        ahead(across)
+        down_line.finish()
+        job.finish()
+
+        def behind(number, carry):
+            at = pl.ds(pl.multiple_of(number * rows, rows), rows)
+            grad_hidden = product_nt(cot_ref[at, :], full_down[...])
+            gate, upward = both[at, :units], both[at, units:]
+            sigma = jax.nn.sigmoid(gate)
+            grads[at, :units] = (grad_hidden * upward * sigma * (1.0 + gate * (1.0 - sigma))).astype(low)
+            grads[at, units:] = (grad_hidden * gate * sigma).astype(low)
+            return carry
+
+        lax.fori_loop(0, 4, behind, 0)
+        transposed_product(hidden, cot_ref, terms)
+
+    def shape(size, kind=low):
+        return jax.ShapeDtypeStruct(size, kind)
+
+    vmem = pl.BlockSpec(memory_space=pltpu.VMEM)
+    dma = pltpu.SemaphoreType.DMA
+    return pl.pallas_call(
+        body,
+        in_specs=[vmem] * 5,
+        out_specs=[vmem] * 5,
+        out_shape=[
+            shape((slots, depth)),
+            shape((slots, units)),
+            shape((units, depth)),
+            shape((slots, 2 * units)),
+            shape((units, depth)),
+        ],
+        scratch_shapes=[
+            pltpu.VMEM((rows, depth), low),
+            pltpu.VMEM((slots, 2 * units), jnp.float32),
+            dma((6,)),
+            dma((6,)),
+        ]
+        + LineGather.scratch(chips),
+        compiler_params=pltpu.CompilerParams(
+            collective_id=collective_id, has_side_effects=True, vmem_limit_bytes=VMEM_LIMIT
+        ),
+        name="feed_forward",
+    )(middle, gain, weights, own_down, cotangent)
 
 
 def gather(value, axis_name):
@@ -1457,46 +1619,49 @@
     own_forget = jnp.pad(own_forget, ((0, 0), (0, PAIR - local_heads)))
     own_bias = lax.dynamic_slice_in_dim(forget_bias, seq_rank * local_heads, local_heads)
     own_bias = jnp.pad(own_bias, (0, PAIR - local_heads))[None]
-    mine_attn = jnp.concatenate(
-        [*(own_columns(w, lanes) for w in (w_query, w_key, w_value)), own_forget, own_columns(w_ogate, columns)],
-        axis=1,
-    )
+    length_row = jnp.broadcast_to(lengths[:, None], (1, PAIR))
     mine_down = lax.dynamic_slice_in_dim(w_down, seq_rank * part, part, 0)
-    normed_attn_own = rms_norm(inputs, norm_attn).astype(low)
     if fast:
-        normed_attn, cotangent_all, full_attn, full_out, mine_ffn = first_gather(
-            normed_attn_own, cotangent_low, mine_attn, w_out, w_gate, w_up, part, 0
+        (
+            normed_attn, cotangent_all, full_front, full_ogate, full_out, full_ffn,
+            joined, attended_low, offset, col, logit, gate_pre, gated, middle,
+        ) = whole_forward(
+            layer_input[0], norm_attn[None], cotangent_low, (w_query, w_key, w_value, w_ogate), own_forget,
+            own_bias, length_row, w_out, w_gate, w_up, head_size, scale, 0,
         )
         full_out = full_out.reshape(columns, width)
-        mine_ffn, mine_down = lax.optimization_barrier((mine_ffn, mine_down))
     else:
-        full_attn = gather(mine_attn, "wshard")
-        normed_attn = gather(normed_attn_own, "seq")
+        mine_front = jnp.concatenate(
+            [*(own_columns(w, lanes) for w in (w_query, w_key, w_value)), own_forget], axis=1
+        )
+        full_front = gather(mine_front, "wshard")
+        full_ogate = gather(own_columns(w_ogate, columns), "wshard")
+        normed_attn = gather(rms_norm(inputs, norm_attn).astype(low), "seq")
         cotangent_all = gather(cotangent_low, "seq")
         full_out = lax.dynamic_slice_in_dim(gather(w_out, "wshard"), seq_rank * columns, columns, 0)
         mine_ffn = jnp.concatenate([own_units(w_gate), own_units(w_up)], axis=1)
-    full_ffn = gather(mine_ffn, "wshard")
-    full_down = gather(mine_down, "wshard")
-
-    joined = product(normed_attn, full_attn[:, :front]).astype(low)
-    gate_pre = product(normed_attn, full_attn[:, front:])
-    attended_low, offset, col, logit = attention_fwd(joined, own_bias, lengths, head_size, scale)
-    attended = attended_low[:, :columns].astype(jnp.float32)
-    gated_full, pull_gate = jax.vjp(gate_product, attended, gate_pre)
-    gated = gated_full.astype(low)
-    (branch,) = multiply_scatter([gated], [full_out], False, 1)
-    middle = inputs + branch
+        full_ffn = gather(mine_ffn, "wshard")
+        joined = product(normed_attn, full_front).astype(low)
+        gate_pre = product(normed_attn, full_ogate)
+        attended_low, offset, col, logit = attention_fwd(joined, own_bias, length_row, head_size, scale)
+        gated = gate_product(attended_low[:, :columns].astype(jnp.float32), gate_pre).astype(low)
+        middle = inputs + multiply_scatter([gated], [full_out], False, 1)[0]
+    unused_gated, pull_gate = jax.vjp(gate_product, attended_low[:, :columns].astype(jnp.float32), gate_pre)
     normed_ffn_own, pull_ffn_norm = jax.vjp(rms_norm, middle, norm_ffn)
-    normed_ffn, gate_up = gather_multiply(normed_ffn_own.astype(low), full_ffn, False, 2)
-    hidden_full, pull_swiglu = jax.vjp(swiglu, gate_up[:, :units], gate_up[:, units:])
-    hidden = hidden_full.astype(low)
-
-    grad_w_down = product_tn(hidden, cotangent_all).astype(low)
+    if fast:
+        normed_ffn, hidden, full_down, grad_gate_up, grad_w_down = feed_forward(
+            middle, norm_ffn[None], full_ffn, mine_down, cotangent_all, 2
+        )
+    else:
+        full_down = gather(mine_down, "wshard")
+        normed_ffn, gate_up = gather_multiply(normed_ffn_own.astype(low), full_ffn, False, 2)
+        hidden_full, pull_swiglu = jax.vjp(swiglu, gate_up[:, :units], gate_up[:, units:])
+        hidden = hidden_full.astype(low)
+        grad_w_down = product_tn(hidden, cotangent_all).astype(low)
+        grad_hidden = product_nt(cotangent_all, full_down)
+        grad_gate_full, grad_up_full = pull_swiglu(grad_hidden)
+        grad_gate_up = jnp.concatenate([grad_gate_full.astype(low), grad_up_full.astype(low)], axis=1)
     share_down = scatter(grad_w_down, "wshard")
-    grad_hidden = product_nt(cotangent_all, full_down)
-    grad_gate_full, grad_up_full = pull_swiglu(grad_hidden)
-    grad_gate_up = jnp.concatenate([grad_gate_full.astype(low), grad_up_full.astype(low)], axis=1)
-    grad_gate_up, grad_w_down = lax.optimization_barrier((grad_gate_up, grad_w_down))
     grad_normed_ffn, grad_w_ffn = multiply_scatter(
         [grad_gate_up], [full_ffn], True, 3, [(normed_ffn, grad_gate_up)]
     )
@@ -1514,13 +1679,14 @@
             joined, grad_attended, offset, col, logit, hidden, full_down, gated, grad_branch, head_size, scale, 5
         )
         grad_normed_attn, share_attn, grad_out = last_backward(
-            grads, grad_gate_pre, normed_attn, full_attn, collected, 6
+            grads, grad_gate_pre, normed_attn, full_front, full_ogate, collected, 6
         )
         grad_out = grad_out.astype(jnp.float32)
     else:
         grads, bias_rows = attention_bwd(joined, grad_attended, offset, col, logit, head_size, scale)
         grad_projected = jnp.concatenate([grads, grad_gate_pre], axis=1)
         share_attn = scatter(product_tn(normed_attn, grad_projected).astype(low), "wshard")
+        full_attn = jnp.concatenate([full_front, full_ogate], axis=1)
         grad_normed_attn = scatter(product_nt(grad_projected, full_attn).astype(low), "seq").astype(jnp.float32)
         lowered = scatter(product(hidden, full_down).astype(low), "seq").astype(jnp.float32)
         share_out = scatter(product_tn(gated, grad_branch).astype(low), "wshard")

time: 526 us -> 517 us (0.983)
  Pallas kernels: 432 us -> 465 us
  matrix products: 31.4 us -> 0 us
  other arithmetic: 26.9 us -> 18.7 us
    pallas_call x3, Pallas kernels: 140 us -> 254 us  [the longest x1 137 us: whole_forward(): pl.pallas_call(body, in_specs=[vmem] * 3 + [anywhere] * 4 + [vmem] * 4 +...]
    pallas_call x2 -> x1, Pallas kernels: 84 us -> 41.2 us  [product_scatter(): pl.pallas_call(body, in_specs=[vmem] * (2 * count + 2 * more), out_specs=...]
    pallas_call x2 -> x1, Pallas kernels: 69.9 us -> 31.2 us  [gather_product(): pl.pallas_call(body, in_specs=[vmem, vmem], out_specs=[vmem, vmem], out_s...]
    dot_general x4 -> x0, matrix products: 31.4 us -> none  [the longest x2 13.6 us: product(): return jnp.dot(left, right, preferred_element_type=jnp.float32)]
    unnamed x39 -> x25, local copies, waits for them, and re-layouts: 9.09 us -> 3.33 us
  transfers between devices with their start and end apart: 4 -> 2, of which waited for: 0 -> 0; matrix products, arithmetic and copies ran while one was open for 7% -> 3% of each run, Pallas kernels for 55% -> 37%
where the time goes in v5:
time: 517 us; the launch traced here: 511 us
  Pallas kernels  465 us (90%)
  other arithmetic  18.7 us (4%)
  between operations  15.2 us (3%)
  local copies, waits for them, and re-layouts  12.2 us (2%)
    pallas_call x1, Pallas kernels, whole_forward(): pl.pallas_call(body, in_specs=[vmem] * 3 + [anywhere] * 4 + [vmem] * 4 +...  137 us
    pallas_call x1, Pallas kernels, last_gather(): pl.pallas_call(body, in_specs=[vmem] * (count + 1), out_specs=[pl.BlockSp...  74.6 us
    pallas_call x1, Pallas kernels, last_backward(): pl.pallas_call(body, in_specs=[vmem] * 6, out_specs=[vmem] * 3, out_shape...  63 us
    pallas_call x1, Pallas kernels, middle_backward(): pl.pallas_call(body, in_specs=[vmem] * 9, out_specs=[vmem] * 4, out_shape...  53.6 us
    pallas_call x1, Pallas kernels, feed_forward(): pl.pallas_call(body, in_specs=[vmem] * 5, out_specs=[vmem] * 5, out_shape...  53.6 us
    pallas_call x1, Pallas kernels, product_scatter(): pl.pallas_call(body, in_specs=[vmem] * (2 * count + 2 * more), out_specs=...  41.2 us
    pallas_call x1, Pallas kernels, gather_product(): pl.pallas_call(body, in_specs=[vmem, vmem], out_specs=[vmem, vmem], out_s...  31.2 us
  transfers between devices with their start and end apart: 2, of which 0 were waited for; matrix products, arithmetic and copies ran while one was open for 3% of the time, Pallas kernels for 37%

profile of v5, /device:TPU:0, one launch (start us, length us, event | category | flops | bytes accessed | tf_op | source)
XLA Modules:
  0.0 511.4 jit_solution(9283062602192836993)
XLA Ops:
  7.2 0.0 copy-start
  7.2 0.0 reduce-scatter.5.cloned.1.call-start
  7.2 0.8 constant_dynamic-slice_fusion.1
  8.1 0.1 copy.32
  8.2 0.7 dynamic_slice.10
  9.0 0.5 pad_bitcast_fusion.bias_ref
  10.1 1.3 broadcast_in_dim.44.gain_ref
  11.4 1.3 broadcast_in_dim.49.gain_ref
  12.7 0.6 pad.12.forget_ref
  13.3 2.1 bitcast_select_fusion.cot_ref
  15.5 0.0 copy-done
  15.5 0.8 constant_dynamic-slice_fusion.down_ref
  16.3 0.5 broadcast_in_dim.48.length_ref
  16.8 137.0 %whole_forward.1 = (bf16[1024,1536]{1,0:T(8,128)(2,1)}, bf16[1024,1536]{1,0:T(8,128)(2,1)}, bf16[1536,1280]{1,0:T(8,128)(2,1)}, bf16[1536,384]{1,0:T(8,128)(2,1)...) custom-call(bf16[256,1536]{1,0:T(8,128)(2,1)} %bitcast.34, ...), custom_call_target="tpu_custom_call" | custom-call | tf_op jit(solution)/shard_map/whole_forward/pallas_call | solution.py:1409
  153.8 53.6 %feed_forward.1 = (bf16[1024,1536]{1,0:T(8,128)(2,1)}, bf16[1024,1024]{1,0:T(8,128)(2,1)}, bf16[1024,1536]{1,0:T(8,128)(2,1)}, bf16[1024,2048]{1,0:T(8,128)(2,1)}, bf16[1024,1536]{1,0:T(8,128)(2,1)}) custom-call(f32[256,1536]{1,0:T(8,128)} %get-tuple-element.55.middle_ref, f32[1,1536]{1,0:T(1,128)} %broadcast_in_dim.49.gain_ref, ...), custom_call_target="tpu_custom_call" | custom-call | tf_op jit(solution)/shard_map/feed_forward/pallas_call | solution.py:1518
  207.4 0.0 reduce-scatter.5.cloned.1.call-update
  207.4 0.2 reduce-scatter.3.cloned.1.call-start
  207.6 41.2 %product_scatter.1 = (f32[256,1536]{1,0:T(8,128)}, bf16[1536,2048]{1,0:T(8,128)(2,1)}) custom-call(bf16[1024,2048]{1,0:T(8,128)(2,1)} %get-tuple-element.59.refs_0_.refs_3_, bf16[1536,2048]{1,0:T(8,128)(2,1)} %get-tuple-element.57.weights_ref.refs_1_, bf16[1024,1536]{1,0:T(8,128)(2,1)} %get-tuple-element.60.refs_2_, ...), custom_call_target="tpu_custom_call" | custom-call | tf_op jit(solution)/shard_map/product_scatter/pallas_call | solution.py:1136
  248.8 0.0 copy-start.2
  248.8 0.0 copy-start.8
  248.8 0.0 reduce-scatter.3.cloned.1.call-update
  248.8 1.4 copy-done.2
  250.2 0.0 copy-start.3
  250.2 0.2 multiply_reduce_fusion.2
  250.4 0.0 copy-done.8
  250.4 1.2 copy-done.3
  251.6 0.0 copy-start.6
  251.6 0.5 multiply_reduce_fusion
  252.2 0.6 copy-done.6
  252.8 1.4 fusion.13.own_ref
  254.2 31.2 %gather_product.1 = (bf16[1024,1536]{1,0:T(8,128)(2,1)}, f32[1024,384]{1,0:T(8,128)}) custom-call(bf16[256,1536]{1,0:T(8,128)(2,1)} %fusion.13.own_ref, bf16[384,1536]{1,0:T(8,128)(2,1)} %bitcast.38), custom_call_target="tpu_custom_call" | custom-call | tf_op jit(solution)/shard_map/gather_product/pallas_call | solution.py:408
  285.4 3.9 fusion.2
  289.3 53.6 %middle_backward.1 = (bf16[1024,1280]{1,0:T(8,128)(2,1)}, f32[8,128]{1,0:T(8,128)}, f32[256,1536]{1,0:T(8,128)}, bf16[192,1536]{1,0:T(8,128)(2,1)}) custom-call(bf16[1024,1280]{1,0:T(8,128)(2,1)} %get-tuple-element.56.joined_ref, bf16[1024,384]{1,0:T(8,128)(2,1)} %get-tuple-element.101.d_out_ref, f32[8,1024]{1,0:T(8,128)} %get-tuple-element.65.offset_ref, ...), custom_call_target="tpu_custom_call" | custom-call | tf_op jit(solution)/shard_map/middle_backward/pallas_call | solution.py:1195
  343.0 63.0 %last_backward.1 = (f32[256,1536]{1,0:T(8,128)}, bf16[192,1664]{1,0:T(8,128)(2,1)}, bf16[192,1536]{1,0:T(8,128)(2,1)}) custom-call(bf16[1024,1280]{1,0:T(8,128)(2,1)} %get-tuple-element.73.grads_ref, bf16[1024,384]{1,0:T(8,128)(2,1)} %get-tuple-element.100.gate_ref, bf16[1024,1536]{1,0:T(8,128)(2,1)} %get-tuple-element.75.normed_ref, ...), custom_call_target="tpu_custom_call" | custom-call | tf_op jit(solution)/shard_map/last_backward/pallas_call | solution.py:1256
  406.0 0.0 copy-start.11
  406.0 0.0 copy-start.5
  406.1 0.0 copy-start.9
  406.1 2.3 convert_element_type.49
  408.3 0.0 copy-done.11
  408.3 0.1 slice_reduce_fusion
  408.5 0.2 dynamic_update_slice.3
  408.7 0.0 copy-done.5
  408.7 0.0 copy-start.4
  408.7 0.0 copy-start.7
  408.7 0.2 fusion.5
  409.0 0.0 copy-done.9
  409.0 2.0 fusion.8
  411.0 0.6 fusion.10.refs_3_
  411.6 0.0 copy-done.4
  411.6 0.0 copy-done.7
  411.6 4.3 fusion.4
  416.0 0.0 reduce-scatter.5.cloned.1.call-done.refs_2_
  416.0 74.6 %last_gather.1 = (bf16[768,1664]{1,0:T(8,128)(2,1)}, bf16[768,2048]{1,0:T(8,128)(2,1)}, bf16[512,1536]{1,0:T(8,128)(2,1)}, f32[32,128]{1,0:T(8,128)}) custom-call(bf16[192,1664]{1,0:T(8,128)(2,1)} %get-tuple-element.80.refs_0_, bf16[192,2048]{1,0:T(8,128)(2,1)} %reduce-scatter.3.cloned.1.call-done.refs_1_, ...), custom_call_target="tpu_custom_call" | custom-call | tf_op jit(solution)/shard_map/last_gather/pallas_call | solution.py:675
  490.5 0.0 copy-start.10
  490.5 4.4 join_columns.1
  494.9 1.0 convert_bitcast_fusion
  495.9 0.2 copy.31
  496.1 0.6 reshape.101
  496.7 0.0 copy-done.10
  496.7 0.6 slice_bitcast_fusion
  497.3 0.5 slice.29
  497.8 0.0 copy-start.1
  497.8 6.5 %join_units.1 = (f32[192,4096]{1,0:T(8,128)}, f32[192,4096]{1,0:T(8,128)}, f32[512,1536]{1,0:T(8,128)}) custom-call(bf16[4,192,2048]{2,1,0:T(8,128)(2,1)} %bitcast.35, bf16[512,1536]{1,0:T(8,128)(2,1)} %get-tuple-element.92.down_ref), custom_call_target="tpu_custom_call" | custom-call | tf_op jit(solution)/shard_map/join_units/pallas_call | solution.py:715
  504.3 0.0 copy-done.1
  (7 shorter events, 0.0 us)
Async XLA Ops:
  7.2 8.3 %copy-start = (bf16[512,1536]{1,0:T(8,128)(2,1)S(1)}, bf16[512,1536]{1,0:T(8,128)(2,1)}, u32[]{:S(2)}) copy-start(bf16[512,1536]{1,0:T(8,128)(2,1)} %param.28) | copy-start | bytes 4718596
  7.2 408.8 %reduce-scatter.5.cloned.1.call-start = ((), (), s32[]{:S(2)}) async-start(), calls=%async_computation.3 | async-start | bytes 3538944 | tf_op jit(solution)/shard_map/reduce_scatter | solution.py:1548
  207.4 208.6 %reduce-scatter.3.cloned.1.call-start = ((), (), s32[]{:S(2)}) async-start(), calls=%async_computation.2 | async-start | bytes 7077888 | tf_op jit(solution)/shard_map/reduce_scatter | solution.py:1548
  248.8 1.4 copy-start.2
  248.8 1.6 copy-start.8
  250.2 1.4 copy-start.3
  251.6 1.1 copy-start.6
  406.0 2.3 copy-start.11
  406.0 2.7 copy-start.5
  406.1 2.9 copy-start.9
  408.7 2.9 copy-start.4
  408.7 2.9 copy-start.7
  490.5 6.2 %copy-start.10 = (f32[32,128]{1,0:T(8,128)S(1)}, f32[32,128]{1,0:T(8,128)}, u32[]{:S(2)}) copy-start(f32[32,128]{1,0:T(8,128)} %get-tuple-element.84) | copy-start | bytes 49156
  497.8 6.5 %copy-start.1 = (bf16[512,1536]{1,0:T(8,128)(2,1)S(1)}, bf16[512,1536]{1,0:T(8,128)(2,1)}, u32[]{:S(2)}) copy-start(bf16[512,1536]{1,0:T(8,128)(2,1)} %param.28) | copy-start | bytes 4718596
Sparse Core Ops, SparseCore 0:
  207.5 39.5 reduce-scatter.4
  249.4 81.4 reduce-scatter.2
